TPU v7x, 8 devices: a whole 2x2x1 slice. The times are simulated.
8 devices in a mesh: dp: 1 (over z), tp: 2 (over y), ep: 4 (over x, core).
Axes of the slice: x: 2, y: 2, z: 1, core: 2. Of those that a mesh axis runs over, the one named last changes fastest.
Arguments:
- hidden: bfloat16 [2048, 1024], P(('dp', 'ep'))
- seq_lens: int32 [2048], P(('dp', 'ep'))
- rope_cos: float32 [2048, 32], P(('dp', 'ep'))
- rope_sin: float32 [2048, 32], P(('dp', 'ep'))
- ln1_scale: bfloat16 [1024], replicated
- ln1_bias: bfloat16 [1024], replicated
- w_qkv: bfloat16 [1024, 2048], P(None, 'tp')
- b_qkv: bfloat16 [2048], P('tp')
- w_out: bfloat16 [1024, 1024], P('tp')
- b_out: bfloat16 [1024], replicated
- k_cache: bfloat16 [2048, 128, 8, 64], P(('dp', 'ep'), None, 'tp')
- v_cache: bfloat16 [2048, 128, 8, 64], P(('dp', 'ep'), None, 'tp')
- ln2_scale: bfloat16 [1024], replicated
- ln2_bias: bfloat16 [1024], replicated
- w_router: bfloat16 [1024, 32], replicated
- expert_ids: int32 [2048, 8], P(('dp', 'ep'))
- w_gate: bfloat16 [32, 1024, 512], P('ep', None, 'tp')
- w_up: bfloat16 [32, 1024, 512], P('ep', None, 'tp')
- w_down: bfloat16 [32, 512, 1024], P('ep', 'tp')
Outputs:
- output 1: bfloat16 [2048, 1024], P(('dp', 'ep'))
- output 2: bfloat16 [2048, 128, 8, 64], P(('dp', 'ep'), None, 'tp')
- output 3: bfloat16 [2048, 128, 8, 64], P(('dp', 'ep'), None, 'tp')
All inputs are finite; a program needn't handle non-finite values.
Results may differ from a plain program's by a relative error of at most 0.0106167.
Values are sent between devices in bfloat16 or wider.
A program may use at most 1 GiB of HBM per device.

v0:
```python
import jax
import jax.numpy as jnp
from jax import lax
from jax.sharding import PartitionSpec as P

EPS = 1e-5


def layer_norm(values, ln_scale, ln_bias):
    vals_f32 = values.astype(jnp.float32)
    row_mean = jnp.mean(vals_f32, axis=-1, keepdims=True)
    centered = vals_f32 - row_mean
    row_var = jnp.mean(centered * centered, axis=-1, keepdims=True)
    normed = centered * lax.rsqrt(row_var + EPS)
    return (normed * ln_scale.astype(jnp.float32) + ln_bias.astype(jnp.float32)).astype(jnp.bfloat16)


def apply_rope(values, cos_part, sin_part):
    half_dim = values.shape[-1] // 2
    vals_f32 = values.astype(jnp.float32)
    first_half = vals_f32[..., :half_dim]
    second_half = vals_f32[..., half_dim:]
    rotated = jnp.concatenate([first_half * cos_part - second_half * sin_part, second_half * cos_part + first_half * sin_part], axis=-1)
    return rotated.astype(jnp.bfloat16)


def attention_part(normed, seq_lens, rope_cos, rope_sin, w_qkv, b_qkv, w_out, k_cache, v_cache):
    n_batch, s_max, n_groups, head_dim = k_cache.shape
    q_per = w_qkv.shape[1] // (n_groups * head_dim) - 2
    qkv_rows = (jnp.dot(normed, w_qkv, preferred_element_type=jnp.float32) + b_qkv.astype(jnp.float32)).astype(jnp.bfloat16)
    qkv_rows = qkv_rows.reshape(n_batch, n_groups, q_per + 2, head_dim)
    queries = apply_rope(qkv_rows[:, :, :q_per], rope_cos[:, None, None, :], rope_sin[:, None, None, :])
    key_new = apply_rope(qkv_rows[:, :, q_per], rope_cos[:, None, :], rope_sin[:, None, :])
    value_new = qkv_rows[:, :, q_per + 1]
    positions = jnp.arange(s_max)
    write_mask = (positions[None, :] == seq_lens[:, None])[:, :, None, None]
    k_cache_out = jnp.where(write_mask, key_new[:, None], k_cache)
    v_cache_out = jnp.where(write_mask, value_new[:, None], v_cache)
    scores = jnp.einsum('bgqh,bsgh->bgqs', queries, k_cache_out, preferred_element_type=jnp.float32) * head_dim ** -0.5
    in_range = positions[None, None, None, :] <= seq_lens[:, None, None, None]
    attn_probs = jax.nn.softmax(jnp.where(in_range, scores, -jnp.inf), axis=-1).astype(jnp.bfloat16)
    context = jnp.einsum('bgqs,bsgh->bgqh', attn_probs, v_cache_out, preferred_element_type=jnp.float32).astype(jnp.bfloat16)
    attn_part = jnp.dot(context.reshape(n_batch, n_groups * q_per * head_dim), w_out, preferred_element_type=jnp.float32)
    return attn_part, k_cache_out, v_cache_out


def route_tables(expert_ids, gate_probs, first_expert, n_exp, capacity):
    id_match = expert_ids[..., None] == (first_expert + jnp.arange(n_exp))
    chosen_mask = jnp.sum(id_match.astype(jnp.int32), axis=-2)
    slot_rank = jnp.cumsum(chosen_mask, axis=-2) - chosen_mask
    slot_of = jnp.swapaxes(jnp.where(chosen_mask > 0, slot_rank, -1), -1, -2)
    dispatch = (slot_of[..., None, :] == jnp.arange(capacity)[:, None]).astype(jnp.bfloat16)
    gate_dense = jnp.sum(jnp.where(id_match, gate_probs[..., None].astype(jnp.float32), 0.0), axis=-2)
    combine = dispatch * jnp.swapaxes(gate_dense, -1, -2)[..., None, :].astype(jnp.bfloat16)
    return dispatch, combine


def expert_ffn(routed_rows, w_gate, w_up, w_down):
    gate_pre = jnp.einsum('secd,edf->escf', routed_rows, w_gate, preferred_element_type=jnp.float32)
    up_pre = jnp.einsum('secd,edf->escf', routed_rows, w_up, preferred_element_type=jnp.float32)
    hidden_act = (jax.nn.silu(gate_pre) * up_pre).astype(jnp.bfloat16)
    return jnp.einsum('escf,efd->escd', hidden_act, w_down, preferred_element_type=jnp.float32)


def solution(mesh):
    n_ep = mesh.shape['ep']
    token_rows = P(('dp', 'ep'), None)
    token_vec = P(('dp', 'ep'))
    cache_spec = P(('dp', 'ep'), None, 'tp', None)
    expert_in = P('ep', None, 'tp')
    expert_down = P('ep', 'tp', None)

    def device_step(hidden, seq_lens, rope_cos, rope_sin, ln1_scale, ln1_bias, w_qkv, b_qkv, w_out, b_out, k_cache, v_cache, ln2_scale, ln2_bias, w_router, expert_ids, w_gate, w_up, w_down):
        n_batch, d_model = hidden.shape
        e_local = w_gate.shape[0]
        n_exp = e_local * n_ep
        top_k = expert_ids.shape[1]
        capacity = (2 * top_k * n_batch + n_exp - 1) // n_exp
        normed = layer_norm(hidden, ln1_scale, ln1_bias)
        attn_part, k_cache_out, v_cache_out = attention_part(normed, seq_lens, rope_cos, rope_sin, w_qkv, b_qkv, w_out, k_cache, v_cache)
        attn_sum = lax.psum(attn_part.astype(jnp.bfloat16), 'tp')
        hidden_mid = (hidden.astype(jnp.float32) + attn_sum.astype(jnp.float32) + b_out.astype(jnp.float32)).astype(jnp.bfloat16)
        normed2 = layer_norm(hidden_mid, ln2_scale, ln2_bias)
        logits = jnp.dot(normed2, w_router, preferred_element_type=jnp.float32)
        gate_probs = jax.nn.softmax(jnp.take_along_axis(logits, expert_ids, axis=1), axis=-1).astype(jnp.bfloat16)
        dispatch, combine = route_tables(expert_ids, gate_probs, 0, n_exp, capacity)
        outgoing = jnp.einsum('ecb,bd->ecd', dispatch, normed2, preferred_element_type=jnp.float32).astype(jnp.bfloat16)
        received = lax.all_to_all(outgoing, 'ep', 0, 0, tiled=True).reshape(n_ep, e_local, capacity, d_model)
        down_part = expert_ffn(received, w_gate, w_up, w_down).astype(jnp.bfloat16)
        expert_out = lax.psum(down_part, 'tp')
        returned = lax.all_to_all(expert_out, 'ep', 1, 0, tiled=True).reshape(n_exp, capacity, d_model)
        moe_sum = jnp.einsum('ecb,ecd->bd', combine, returned, preferred_element_type=jnp.float32)
        hidden_out = (hidden_mid.astype(jnp.float32) + moe_sum).astype(jnp.bfloat16)
        return hidden_out, k_cache_out, v_cache_out

    in_specs = (token_rows, token_vec, token_rows, token_rows, P(), P(), P(None, 'tp'), P('tp'), P('tp', None), P(), cache_spec, cache_spec, P(), P(), P(), token_rows, expert_in, expert_in, expert_down)
    return jax.shard_map(device_step, mesh=mesh, in_specs=in_specs, out_specs=(token_rows, cache_spec, cache_spec), check_vma=False)
```

profile of v0, /device:TPU:0, one launch (start us, length us, event | category | flops | bytes accessed | tf_op | source)
XLA Modules:
  0.0 988.0 jit_solution(15640450713016348195)
XLA Ops:
  10.9 1.6 fusion.34
  12.6 2.3 add_convert_fusion.1
  16.7 1.7 copy.89
  18.3 1.7 copy.88
  23.1 2.0 copy.105
  25.1 2.0 convert_element_type.105
  27.2 3.9 subtract_convert_fusion
  31.1 44.4 %broadcast_select_fusion.1 = (bf16[512,128,4,64]{1,3,2,0:T(8,128)(2,1)}, bf16[512,128,4,64]{1,3,2,0:T(8,128)(2,1)}) fusion(bf16[512,128,4,64]{1,3,2,0:T(8,128)(2,1)} %param.29, pred[512,128]{1,0:T(8,128)(4,1)S(1)} %get-tuple-element.14, bf16[512,4,64]{2,1,0:T(4,128)(2,1)S(1)} %copy-done.7, bf16[512,128,4,64]{1,3,2,0:T(8,128)(2,1)} %param.30, ...), kind=kLoop, calls=%fused_computation.3 | loop fusion | flops 33554432 | bytes 134807552 | tf_op jit(solution)/shard_map/jit(_where)/select_n | solution.py:37
  75.6 17.0 %fusion.65 = (f32[512,4,2]{2,1,0:T(4,128)}, f32[512,4,2,128]{3,2,1,0:T(2,128)}) fusion(pred[512,128]{1,0:T(8,128)(4,1)S(1)} %get-tuple-element.13, bf16[512,128,4,64]{1,3,2,0:T(8,128)(2,1)} %get-tuple-element.11, bf16[512,4,2,32]{3,2,1,0:T(2,128)(2,1)S(1)} %copy-done.6, bf16[512,4,2,32]{3,2,1,0:T(2,128)(2,1)S(1)} %copy-done.5), kind=kOutput, calls=%fused_computation.95 | convolution fusion | flops 70254720 | bytes 36257792 | tf_op jit(solution)/shard_map/sub | solution.py:41
  92.6 22.4 %convolution_convert_fusion.1 = bf16[512,4,2,64]{3,2,1,0:T(2,128)(2,1)S(1)} fusion(bf16[512,128,4,64]{1,3,2,0:T(8,128)(2,1)} %get-tuple-element.12, f32[512,4,2,128]{3,2,1,0:T(2,128)} %get-tuple-element.16, f32[512,4,2]{2,1,0:T(4,128)} %get-tuple-element.15), kind=kOutput, calls=%fused_computation.50 | convolution fusion | flops 68419584 | bytes 36192256 | tf_op jit(solution)/shard_map/bgqs,bsgh->bgqh/dot_general | solution.py:42
  115.0 1.6 copy.92
  116.6 2.9 convolution_convert_fusion.2
  121.3 35.5 %all-reduce.3.cloned.1.call-done = bf16[512,1024]{1,0:T(8,128)(2,1)} async-done(((bf16[512,1024]{1,0:T(8,128)(2,1)}), bf16[512,1024]{1,0:T(8,128)(2,1)}) %all-reduce.3.cloned.1.call-update) | async-done | bytes 1048592 | tf_op jit(solution)/shard_map/psum | solution.py:81
  156.8 1.7 convert_reduce_fusion
  159.0 11.3 %fusion.7 = bf16[32,256,1024]{2,1,0:T(8,128)(2,1)S(1)} fusion(s32[32,512]{1,0:T(8,128)S(1)} %fusion.54, bf16[512,1024]{1,0:T(8,128)(2,1)S(1)} %get-tuple-element.4, f32[1024]{0:T(1024)S(1)} %convert_element_type.117, f32[1024]{0:T(1024)S(1)} %convert_element_type.116, f32[512]{0:T(512)S(1)} %add_rsqrt_fusion, f32[512]{0:T(512)S(1)} %broadcast_multiply_fusion), kind=kOutput, calls=%fused_computation.12 | convolution fusion | flops 8605663232 | bytes 17903616 | tf_op jit(solution)/shard_map/ecb,bd->ecd/dot_general | solution.py:87
  170.3 187.5 %all_to_all.20 = bf16[32,256,1024]{2,1,0:T(8,128)(2,1)} all-to-all(bf16[32,256,1024]{2,1,0:T(8,128)(2,1)S(1)} %fusion.7), channel_id=1, replica_groups=mesh['dp'=1,'tp'=2,'ep'=4] {'ep'}, dimensions={0} | all-to-all | bytes 33554432 | tf_op jit(solution)/shard_map/all_to_all | solution.py:88
  357.8 10.1 %fusion.3 = f32[8,4,256,256]{3,2,1,0:T(8,128)} fusion(bf16[4,8,256,1024]{3,2,1,0:T(8,128)(2,1)} %bitcast.70, bf16[8,1024,256]{2,1,0:T(8,128)(2,1)S(1)} %copy-done.16), kind=kOutput, calls=%fused_computation.7 | convolution fusion | flops 4294967296 | bytes 29360128 | tf_op jit(solution)/shard_map/secd,edf->escf/dot_general | solution.py:60
  367.9 22.6 %convolution_convert_fusion = bf16[8,4,256,1024]{3,2,1,0:T(8,128)(2,1)} fusion(f32[8,4,256,256]{3,2,1,0:T(8,128)} %fusion.3, bf16[8,256,1024]{2,1,0:T(8,128)(2,1)} %param.37, bf16[4,8,256,1024]{3,2,1,0:T(8,128)(2,1)} %bitcast.71, bf16[8,1024,256]{2,1,0:T(8,128)(2,1)} %param.35), kind=kOutput, calls=%fused_computation.11 | convolution fusion | flops 8610906112 | bytes 50331648 | tf_op jit(solution)/shard_map/escf,efd->escd/dot_general | solution.py:62
  390.5 371.2 %all-reduce.5.cloned.1.call-done = bf16[8,4,256,1024]{3,2,1,0:T(8,128)(2,1)} async-done(((bf16[8,4,256,1024]{3,2,1,0:T(8,128)(2,1)}), bf16[8,4,256,1024]{3,2,1,0:T(8,128)(2,1)}) %all-reduce.5.cloned.1.call-update) | async-done | bytes 16777232 | tf_op jit(solution)/shard_map/psum | solution.py:90
  761.7 13.9 %copy.100 = bf16[8,4,256,1024]{3,2,0,1:T(8,128)(2,1)} copy(bf16[8,4,256,1024]{3,2,1,0:T(8,128)(2,1)} %all-reduce.5.cloned.1.call-done) | data formatting | bytes 33554432 | tf_op jit(solution)/shard_map/psum | solution.py:90
  775.5 7.3 all-to-all-start.1
  783.8 33.0 %gather_fusion = f32[4096]{0:T(1024)S(1)} fusion(f32[512,32]{0,1:T(8,128)S(1)} %fusion.62, s32[4096]{0:T(1024)S(1)} %reshape.169), kind=kCustom, calls=%fused_computation | custom fusion | bytes 65536 | tf_op jit(solution)/shard_map/jit(take_along_axis)/gather | solution.py:85
  817.2 148.1 %all-to-all-done.1 = bf16[8,4,256,1024]{3,2,0,1:T(8,128)(2,1)} async-done(((bf16[8,4,256,1024]{3,2,0,1:T(8,128)(2,1)}), bf16[8,4,256,1024]{3,2,0,1:T(8,128)(2,1)}, u32[]{:S(2)}, u32[]{:S(2)}) %all-to-all-start.1) | async-done | bytes 16777248 | tf_op jit(solution)/shard_map/all_to_all | solution.py:91
  965.4 15.8 %fusion.40 = bf16[512,1024]{1,0:T(8,128)(2,1)} fusion(bf16[512,1024]{1,0:T(8,128)(2,1)S(1)} %copy-done.4, bf16[32,256,1024]{2,1,0:T(8,128)(2,1)} %bitcast.18, s32[32,512]{1,0:T(8,128)S(1)} %fusion.54, bf16[32,512]{1,0:T(8,128)(2,1)S(1)} %bitcast.75), kind=kOutput, calls=%fused_computation.43 | convolution fusion | flops 8599896064 | bytes 18972672 | tf_op jit(solution)/shard_map/ecb,ecd->bd/dot_general | solution.py:92
  (77 shorter events, 12.0 us)
Async XLA Ops:
  7.2 5.4 copy-start
  7.2 5.4 copy-start.2
  7.2 149.6 %all-reduce.3.cloned.1.call-start = ((), (), s32[]{:S(2)}) async-start(), calls=%async_computation.2 | async-start | bytes 2097152 | tf_op jit(solution)/shard_map/psum | solution.py:81
  14.9 1.6 copy-start.12
  23.1 4.0 copy-start.9
  25.1 2.0 copy-start.10
  27.2 4.0 copy-start.7
  27.2 4.0 copy-start.8
  31.1 44.4 %copy-start.5 = (bf16[512,4,2,32]{3,2,1,0:T(2,128)(2,1)S(1)}, bf16[512,4,2,32]{3,2,1,0:T(2,128)(2,1)}, u32[]{:S(2)}) copy-start(bf16[512,4,2,32]{3,2,1,0:T(2,128)(2,1)} %get-tuple-element.5) | copy-start | bytes 786436
  31.1 44.4 %copy-start.6 = (bf16[512,4,2,32]{3,2,1,0:T(2,128)(2,1)S(1)}, bf16[512,4,2,32]{3,2,1,0:T(2,128)(2,1)}, u32[]{:S(2)}) copy-start(bf16[512,4,2,32]{3,2,1,0:T(2,128)(2,1)} %get-tuple-element.6) | copy-start | bytes 786436
  116.6 3.1 copy-start.13
  116.6 3.1 copy-start.11
  116.6 4.6 copy-start.14
  116.6 4.6 copy-start.15
  119.6 642.1 %all-reduce.5.cloned.1.call-start = ((), (), s32[]{:S(2)}) async-start(), calls=%async_computation.3 | async-start | bytes 33554432 | tf_op jit(solution)/shard_map/psum | solution.py:90
  158.5 624.7 %copy-start.3 = (bf16[512,1024]{1,0:T(8,128)(2,1)}, bf16[512,1024]{1,0:T(8,128)(2,1)S(1)}, u32[]{:S(2)}) copy-start(bf16[512,1024]{1,0:T(8,128)(2,1)S(1)} %get-tuple-element.4) | copy-start | bytes 3145732
  170.3 187.5 %copy-start.16 = (bf16[8,1024,256]{2,1,0:T(8,128)(2,1)S(1)}, bf16[8,1024,256]{2,1,0:T(8,128)(2,1)}, u32[]{:S(2)}) copy-start(bf16[8,1024,256]{2,1,0:T(8,128)(2,1)} %param.36) | copy-start | bytes 12582916
  775.5 7.6 copy-start.17
  775.5 189.8 %all-to-all-start.1 = ((bf16[8,4,256,1024]{3,2,0,1:T(8,128)(2,1)}), bf16[8,4,256,1024]{3,2,0,1:T(8,128)(2,1)}, u32[]{:S(2)}, u32[]{:S(2)}) async-start(bf16[8,4,256,1024]{3,2,0,1:T(8,128)(2,1)} %copy.100), calls=%async_computation.1 | async-start | bytes 33554432 | tf_op jit(solution)/shard_map/all_to_all | solution.py:91
  783.8 181.6 %copy-start.4 = (bf16[512,1024]{1,0:T(8,128)(2,1)S(1)}, bf16[512,1024]{1,0:T(8,128)(2,1)}, u32[]{:S(2)}) copy-start(bf16[512,1024]{1,0:T(8,128)(2,1)} %copy-done.3) | copy-start | bytes 3145732
  965.4 15.8 %copy-start.1 = (bf16[1024,1024]{1,0:T(8,128)(2,1)S(1)}, bf16[1024,1024]{1,0:T(8,128)(2,1)}, u32[]{:S(2)}) copy-start(bf16[1024,1024]{1,0:T(8,128)(2,1)} %param.25) | copy-start | bytes 6291460
Sparse Core Ops, SparseCore 0:
  119.7 37.0 all-reduce.2
  390.6 371.0 all-reduce.4
where the time goes:
time: 989 us; the launch traced here: 988 us
  waiting for transfers between devices  555 us (56%)
  blocking collectives  187 us (19%)
  matrix products  105 us (11%)
  other arithmetic  60.4 us (6%)
  local copies, waits for them, and re-layouts  58.4 us (6%)
  between operations  14.4 us (1%)
    psum x1, waiting for transfers between devices, device_step(): expert_out = lax.psum(down_part, 'tp')  371 us
    all_to_all x1, blocking collectives, device_step(): lax.all_to_all(outgoing, 'ep', 0, 0, tiled=True)  187 us
    all_to_all x1, waiting for transfers between devices, device_step(): lax.all_to_all(expert_out, 'ep', 1, 0, tiled=True)  148 us
    select_n x1, other arithmetic, attention_part(): k_cache_out = jnp.where(write_mask, key_new[:, None], k_cache)  44.4 us
    psum x1, waiting for transfers between devices, device_step(): attn_sum = lax.psum(attn_part.astype(jnp.bfloat16), 'tp')  35.5 us
    gather x5, local copies, waits for them, and re-layouts, device_step(): jnp.take_along_axis(logits, expert_ids, axis=1)  33.6 us
    dot_general x1, matrix products, expert_ffn(): jnp.einsum('escf,efd->escd', hidden_act, w_down, preferred_element_type=j...  22.6 us
    dot_general x1, matrix products, attention_part(): jnp.einsum('bgqs,bsgh->bgqh', attn_probs, v_cache_out, preferred_element_...  22.4 us
  transfers between devices with their start and end apart: 3, of which 3 were waited for; matrix products, arithmetic and copies ran while one was open for 4% of the time, Pallas kernels for 0%

commit v1 on v0

v1 whole, which is shorter than its diff:
```python
import functools

import jax
import jax.numpy as jnp
from jax import lax
from jax.experimental import pallas as pl
from jax.experimental.pallas import tpu as pltpu
from jax.sharding import PartitionSpec as P

EPS = 1e-5
BF = jnp.bfloat16
F32 = jnp.float32
CHUNKS = 1
SUB = 128
BB = 32
VMEM_LIMIT = 60 * 1024 * 1024


def norm_rows(x, scale, bias):
    mean = jnp.mean(x, axis=-1, keepdims=True)
    cen = x - mean
    var = jnp.mean(cen * cen, axis=-1, keepdims=True)
    return (cen * lax.rsqrt(var + EPS) * scale + bias).astype(BF)


def attention_kernel(len_ref, hid_ref, cos_ref, sin_ref, s1_ref, b1_ref, wqkv_ref, bqkv_ref, wout_ref, k_ref, v_ref, *rest):
    part_ref, ko_ref, vo_ref, qs_ref, kt_ref, vt_ref, sc_ref, pr_ref, cx_ref, ctx_ref = rest[-10:]
    i, j = pl.program_id(0), pl.program_id(1)
    n_j = pl.num_programs(1)
    lane = lax.broadcasted_iota(jnp.int32, (SUB, 128), 1)
    low = lane < 64

    @pl.when(j == 0)
    def _():
        normed = norm_rows(hid_ref[...].astype(F32), s1_ref[...].astype(F32), b1_ref[...].astype(F32))
        qkv = jnp.dot(normed, wqkv_ref[...], preferred_element_type=F32) + bqkv_ref[...].astype(F32)
        qkv = qkv.astype(BF).astype(F32)
        col = [qkv[:, m * 128:(m + 1) * 128] for m in range(8)]
        rol = [pltpu.roll(c, 64, 1) for c in col]

        def first(a, b):
            return jnp.where(low, col[a], rol[b])

        def second(a, b):
            return jnp.where(low, rol[a], col[b])

        cos_t, sin_t = cos_ref[...], sin_ref[...]
        cos = jnp.transpose(jnp.concatenate([cos_t] * 4, axis=0))
        sin = jnp.transpose(jnp.concatenate([-sin_t, sin_t] * 2, axis=0))

        def rope(x):
            other = jnp.where(lane % 64 < 32, pltpu.roll(x, 96, 1), pltpu.roll(x, 32, 1))
            return (x * cos + other * sin).astype(BF).astype(F32)

        for h in range(2):
            q0 = rope(first(4 * h, 4 * h + 2))
            q1 = rope(second(4 * h, 4 * h + 2))
            kk = rope(first(4 * h + 1, 4 * h + 3))
            vv = second(4 * h + 1, 4 * h + 3)
            kt_ref[h * 128:(h + 1) * 128, :] = jnp.transpose(kk)
            vt_ref[h * 128:(h + 1) * 128, :] = jnp.transpose(vv)
            for r in range(8):
                src = q0 if r % 2 == 0 else q1
                if r // 4 == h:
                    src = jnp.where(low if (r // 2) % 2 == 0 else ~low, src, 0.0)
                else:
                    src = jnp.zeros_like(src)
                qs_ref[pl.ds(h * SUB * 8 + r, SUB, stride=8), :] = src

    shift = lax.rem(SUB - j * BB, SUB)
    kt = pltpu.roll(kt_ref[...], shift, 1)
    vt = pltpu.roll(vt_ref[...], shift, 1)
    lane8 = lax.broadcasted_iota(jnp.int32, (8, 128), 1)
    lane256 = lax.broadcasted_iota(jnp.int32, (256, 128), 1)
    row0 = pl.multiple_of(j * BB * 8, BB * 8)
    base = i * SUB + j * BB
    for b in range(BB):
        pos = len_ref[base + b]
        hit = lane256 == pos
        k_old = k_ref[b].reshape(256, 128).astype(F32)
        k_new = jnp.where(hit, kt[:, b:b + 1], k_old).astype(BF)
        ko_ref[b] = k_new.reshape(4, 64, 128)
        q_one = jnp.concatenate([qs_ref[pl.ds(row0 + h * SUB * 8 + b * 8, 8), :] for h in range(2)], axis=1).astype(BF)
        s_one = jnp.dot(q_one, k_new, preferred_element_type=F32) * 0.125
        sc_ref[b * 8:(b + 1) * 8, :] = jnp.where(lane8 <= pos, s_one, -jnp.inf)
    s_all = sc_ref[...]
    e_all = jnp.exp(s_all - jnp.max(s_all, axis=-1, keepdims=True))
    pr_ref[...] = e_all / jnp.sum(e_all, axis=-1, keepdims=True)
    for b in range(BB):
        pos = len_ref[base + b]
        hit = lane256 == pos
        v_old = v_ref[b].reshape(256, 128).astype(F32)
        v_new = jnp.where(hit, vt[:, b:b + 1], v_old).astype(BF)
        vo_ref[b] = v_new.reshape(4, 64, 128)
        p_one = pr_ref[b * 8:(b + 1) * 8, :].astype(BF)
        c_one = lax.dot_general(p_one, v_new, (((1,), (1,)), ((), ())), preferred_element_type=F32)
        cx_ref[b * 8:(b + 1) * 8, :] = c_one[:, :128]
        cx_ref[BB * 8 + b * 8:BB * 8 + (b + 1) * 8, :] = c_one[:, 128:]
    low_b = lax.broadcasted_iota(jnp.int32, (BB, 128), 1) < 64
    for h in range(2):
        for g in range(2):
            r = 4 * h + 2 * g
            one = cx_ref[pl.ds(h * BB * 8 + r, BB, stride=8), :]
            two = cx_ref[pl.ds(h * BB * 8 + r + 1, BB, stride=8), :]
            if g == 0:
                both = jnp.where(low_b, one, pltpu.roll(two, 64, 1))
            else:
                both = jnp.where(low_b, pltpu.roll(one, 64, 1), two)
            ctx_ref[pl.ds(pl.multiple_of(j * BB, BB), BB), (2 * h + g) * 128:(2 * h + g + 1) * 128] = both.astype(BF)

    @pl.when(j == n_j - 1)
    def _():
        part_ref[...] = jnp.dot(ctx_ref[...], wout_ref[...], preferred_element_type=F32).astype(BF)


def attention(chunk, rows, lens, hidden, cos_t, sin_t, s1, b1, wqkv, bqkv, wout, kt, vt, prev):
    n_batch = hidden.shape[0]
    n_i, n_j = rows // SUB, SUB // BB
    first = chunk * n_i
    full = lambda shape: pl.BlockSpec(shape, lambda i, j, s: (0,) * len(shape), pipeline_mode=pl.Buffered(1))
    cache = pl.BlockSpec((BB, 4, 64, 128), lambda i, j, s: ((first + i) * n_j + j, 0, 0, 0))
    in_specs = [
        pl.BlockSpec((SUB, 1024), lambda i, j, s: (first + i, 0)),
        pl.BlockSpec((32, SUB), lambda i, j, s: (0, first + i)),
        pl.BlockSpec((32, SUB), lambda i, j, s: (0, first + i)),
        full((1, 1024)), full((1, 1024)), full((1024, 1024)), full((1, 1024)), full((512, 1024)),
        cache, cache,
    ]
    args = [lens[chunk * rows:(chunk + 1) * rows], hidden, cos_t, sin_t, s1, b1, wqkv, bqkv, wout, kt, vt]
    aliases = {}
    if prev is not None:
        in_specs += [pl.BlockSpec(memory_space=pl.ANY)] * 2
        aliases = {len(args): 1, len(args) + 1: 2}
        args += list(prev)
    return pl.pallas_call(
        attention_kernel,
        grid_spec=pltpu.PrefetchScalarGridSpec(
            num_scalar_prefetch=1, grid=(n_i, n_j), in_specs=in_specs,
            out_specs=[pl.BlockSpec((SUB, 1024), lambda i, j, s: (i, 0)), cache, cache],
            scratch_shapes=[
                pltpu.VMEM((2 * SUB * 8, 128), F32), pltpu.VMEM((256, SUB), F32), pltpu.VMEM((256, SUB), F32),
                pltpu.VMEM((BB * 8, 128), F32), pltpu.VMEM((BB * 8, 128), F32),
                pltpu.VMEM((2 * BB * 8, 128), F32), pltpu.VMEM((SUB, 512), BF)]),
        out_shape=[jax.ShapeDtypeStruct((rows, 1024), BF), jax.ShapeDtypeStruct(kt.shape, BF), jax.ShapeDtypeStruct(vt.shape, BF)],
        input_output_aliases=aliases,
        compiler_params=pltpu.CompilerParams(dimension_semantics=("arbitrary", "arbitrary"), vmem_limit_bytes=VMEM_LIMIT),
        cost_estimate=pl.CostEstimate(flops=rows * 20_000_000, bytes_accessed=rows * 262144, transcendentals=0),
        name="attention",
    )(*args)


def mid_kernel(hid_ref, one_ref, two_ref, bo_ref, s2_ref, b2_ref, x1_ref, h2_ref):
    attn = one_ref[...].astype(F32) + two_ref[...].astype(F32)
    x1 = (hid_ref[...].astype(F32) + attn + bo_ref[...].astype(F32)).astype(BF)
    x1_ref[...] = x1
    h2_ref[...] = norm_rows(x1.astype(F32), s2_ref[...].astype(F32), b2_ref[...].astype(F32))


def middle(chunk, rows, hidden, one, two, b_out, s2, b2):
    tile = 128
    off = chunk * rows // tile
    vec = pl.BlockSpec((1, 1024), lambda i: (0, 0))
    blk = pl.BlockSpec((tile, 1024), lambda i: (i, 0))
    return pl.pallas_call(
        mid_kernel, grid=(rows // tile,),
        in_specs=[pl.BlockSpec((tile, 1024), lambda i: (off + i, 0)), blk, blk, vec, vec, vec],
        out_specs=[blk, blk],
        out_shape=[jax.ShapeDtypeStruct((rows, 1024), BF)] * 2,
        cost_estimate=pl.CostEstimate(flops=rows * 400_000, bytes_accessed=rows * 10240, transcendentals=0),
        name="middle",
    )(hidden, one, two, b_out, s2, b2)


def expert_kernel(rows, first_ref, x0, x1, x2, x3, i0, i1, i2, i3, wr_ref, wg_ref, wu_ref, wd_ref, o0, o1, o2, o3, acc_ref, gate_ref):
    e = pl.program_id(0)
    n_e = pl.num_programs(0)
    xs, ids, outs = (x0, x1, x2, x3), (i0, i1, i2, i3), (o0, o1, o2, o3)
    tile = min(rows, 256)

    @pl.when(e == 0)
    def _():
        for n in range(4):
            logit = lax.dot_general(wr_ref[...], xs[n][...], (((1,), (1,)), ((), ())), preferred_element_type=F32)
            eid = lax.broadcasted_iota(jnp.int32, (32, rows), 0)
            picked = eid == ids[n][0:1, :]
            for m in range(1, 8):
                picked = picked | (eid == ids[n][m:m + 1, :])
            logit = jnp.where(picked, logit, -jnp.inf)
            ex = jnp.exp(logit - jnp.max(logit, axis=0, keepdims=True))
            prob = (ex / jnp.sum(ex, axis=0, keepdims=True)).astype(BF).astype(F32)
            gate_ref[n * rows:(n + 1) * rows, :] = jnp.transpose(prob)

    mine = first_ref[0] + e
    for n in range(4):
        for t in range(rows // tile):
            sl = slice(t * tile, (t + 1) * tile)
            row = n * rows + t * tile
            x = xs[n][sl, :]
            gate = jnp.dot(x, wg_ref[0], preferred_element_type=F32)
            up = jnp.dot(x, wu_ref[0], preferred_element_type=F32)
            act = (gate * jax.nn.sigmoid(gate) * up).astype(BF)
            y = jnp.dot(act, wd_ref[0], preferred_element_type=F32).astype(BF).astype(F32)
            g_all = gate_ref[row:row + tile, :]
            lane = lax.broadcasted_iota(jnp.int32, (tile, 32), 1)
            g_one = jnp.sum(jnp.where(lane == mine, g_all, 0.0), axis=-1, keepdims=True)
            term = g_one * y

            @pl.when(e == 0)
            def _():
                acc_ref[row:row + tile, :] = term

            @pl.when((e > 0) & (e < n_e - 1))
            def _():
                acc_ref[row:row + tile, :] += term

            @pl.when(e == n_e - 1)
            def _():
                outs[n][sl, :] = (acc_ref[row:row + tile, :] + term).astype(BF)


def experts(rows, first, xs, ids, wr_t, wg, wu, wd):
    n_e = wg.shape[0]
    full = lambda shape: pl.BlockSpec(shape, lambda e, s: (0,) * len(shape), pipeline_mode=pl.Buffered(1))
    wspec = lambda a: pl.BlockSpec((1,) + a.shape[1:], lambda e, s: (e, 0, 0))
    return pl.pallas_call(
        functools.partial(expert_kernel, rows),
        grid_spec=pltpu.PrefetchScalarGridSpec(
            num_scalar_prefetch=1, grid=(n_e,),
            in_specs=[full((rows, 1024))] * 4 + [full((8, rows))] * 4 + [full((32, 1024)), wspec(wg), wspec(wu), wspec(wd)],
            out_specs=[full((rows, 1024))] * 4,
            scratch_shapes=[pltpu.VMEM((4 * rows, 1024), F32), pltpu.VMEM((4 * rows, 32), F32)]),
        out_shape=[jax.ShapeDtypeStruct((rows, 1024), BF)] * 4,
        compiler_params=pltpu.CompilerParams(dimension_semantics=("arbitrary",), vmem_limit_bytes=VMEM_LIMIT),
        cost_estimate=pl.CostEstimate(flops=rows * 4 * n_e * 1_600_000, bytes_accessed=14_000_000, transcendentals=0),
        name="experts",
    )(first, *xs, *ids, wr_t, wg, wu, wd)


def solution(mesh):
    n_ep = mesh.shape['ep']
    token_rows = P(('dp', 'ep'), None)
    token_vec = P(('dp', 'ep'))
    cache_spec = P(('dp', 'ep'), None, 'tp', None)
    expert_in = P('ep', None, 'tp')
    expert_down = P('ep', 'tp', None)

    def swap_ep(x, bit):
        return lax.ppermute(x, 'ep', [(d, d ^ bit) for d in range(n_ep)])

    def swap_tp(x):
        return lax.ppermute(x, 'tp', [(0, 1), (1, 0)])

    def spread(x):
        far = swap_ep(x, 2)
        return [x, swap_ep(x, 1), far, swap_ep(far, 1)]

    def device_step(hidden, seq_lens, rope_cos, rope_sin, ln1_scale, ln1_bias, w_qkv, b_qkv, w_out, b_out, k_cache, v_cache, ln2_scale, ln2_bias, w_router, expert_ids, w_gate, w_up, w_down):
        n_batch = hidden.shape[0]
        rows = n_batch // CHUNKS
        kt, vt = (jnp.transpose(c, (0, 2, 3, 1)) for c in (k_cache, v_cache))
        row = lambda a: a.reshape(1, -1)
        ids = spread(expert_ids.T)
        first = (lax.axis_index('ep') * w_gate.shape[0]).astype(jnp.int32).reshape(1)
        prev = None
        outs = []
        for c in range(CHUNKS):
            part, *prev = attention(c, rows, seq_lens, hidden, rope_cos.T, rope_sin.T, row(ln1_scale), row(ln1_bias), w_qkv, row(b_qkv), w_out, kt, vt, prev)
            x1, h2 = middle(c, rows, hidden, part, swap_tp(part), row(b_out), row(ln2_scale), row(ln2_bias))
            cut = [a[:, c * rows:(c + 1) * rows] for a in ids]
            o = experts(rows, first, spread(h2), cut, w_router.T, w_gate, w_up, w_down)
            near = (o[0].astype(F32) + swap_ep(o[1], 1).astype(F32)).astype(BF)
            far = (o[2].astype(F32) + swap_ep(o[3], 1).astype(F32)).astype(BF)
            total = (near.astype(F32) + swap_ep(far, 2).astype(F32)).astype(BF)
            moe = total.astype(F32) + swap_tp(total).astype(F32)
            outs.append((x1.astype(F32) + moe).astype(BF))
        hidden_out = outs[0] if CHUNKS == 1 else jnp.concatenate(outs, axis=0)
        return hidden_out, *(jnp.transpose(c, (0, 3, 1, 2)) for c in prev)

    in_specs = (token_rows, token_vec, token_rows, token_rows, P(), P(), P(None, 'tp'), P('tp'), P('tp', None), P(), cache_spec, cache_spec, P(), P(), P(), token_rows, expert_in, expert_in, expert_down)
    return jax.shard_map(device_step, mesh=mesh, in_specs=in_specs, out_specs=(token_rows, cache_spec, cache_spec), check_vma=False)
```

time: 989 us -> 243 us (0.25)
  waiting for transfers between devices: 555 us -> 96.1 us
  blocking collectives: 187 us -> 0 us
  Pallas kernels: 0 us -> 124 us
  matrix products: 105 us -> 0 us
  other arithmetic: 60.4 us -> 3.9 us
  local copies, waits for them, and re-layouts: 58.4 us -> 7.88 us
  between operations: 14.4 us -> 0.73 us
    psum x2 -> x0, waiting for transfers between devices: 407 us -> none  [the longest x1 371 us: device_step(): expert_out = lax.psum(down_part, 'tp')]
    all_to_all x1 -> x0, blocking collectives: 187 us -> none  [device_step(): lax.all_to_all(outgoing, 'ep', 0, 0, tiled=True)]
    all_to_all x1 -> x0, waiting for transfers between devices: 148 us -> none  [device_step(): lax.all_to_all(expert_out, 'ep', 1, 0, tiled=True)]
    pallas_call x0 -> x3, Pallas kernels: none -> 124 us  [the longest x1 64.6 us: attention(): pl.pallas_call(attention_kernel, grid_spec=pltpu.PrefetchScalarGridSpec(n...]
    ppermute x0 -> x11, waiting for transfers between devices: none -> 96.1 us  [the longest x9 51.8 us: swap_ep(): return lax.ppermute(x, 'ep', [(d, d ^ bit) for d in range(n_ep)])]
    dot_general x8 -> x0, matrix products: 87.9 us -> none  [the longest x1 22.6 us: expert_ffn(): jnp.einsum('escf,efd->escd', hidden_act, w_down, preferred_element_type=j...]
    select_n x2 -> x0, other arithmetic: 44.5 us -> none  [the longest x1 44.4 us: attention_part(): k_cache_out = jnp.where(write_mask, key_new[:, None], k_cache)]
    gather x5 -> x0, local copies, waits for them, and re-layouts: 33.6 us -> none  [device_step(): jnp.take_along_axis(logits, expert_ids, axis=1)]
  transfers between devices with their start and end apart: 3 -> 11, of which waited for: 3 -> 7; matrix products, arithmetic and copies ran while one was open for 4% -> 1% of each run, Pallas kernels for 0% -> 0%
where the time goes in v1:
time: 243 us
  Pallas kernels  124 us (51%)
  waiting for transfers between devices  96.1 us (40%)
  starting transfers between devices  10.2 us (4%)
  local copies, waits for them, and re-layouts  7.88 us (3%)
  other arithmetic  3.9 us (2%)
    pallas_call x1, Pallas kernels, attention(): pl.pallas_call(attention_kernel, grid_spec=pltpu.PrefetchScalarGridSpec(n...  64.6 us
    pallas_call x1, Pallas kernels, experts(): pl.pallas_call(functools.partial(expert_kernel, rows), grid_spec=pltpu.Pr...  55.1 us
    ppermute x9, waiting for transfers between devices, swap_ep(): return lax.ppermute(x, 'ep', [(d, d ^ bit) for d in range(n_ep)])  51.8 us
    ppermute x2, waiting for transfers between devices, swap_tp(): return lax.ppermute(x, 'tp', [(0, 1), (1, 0)])  44.3 us
    reshape x6, local copies, waits for them, and re-layouts, device_step(): row = lambda a: a.reshape(1, -1)  5.61 us
    ppermute x9, starting transfers between devices, swap_ep(): return lax.ppermute(x, 'ep', [(d, d ^ bit) for d in range(n_ep)])  5.35 us
    ppermute x2, starting transfers between devices, swap_tp(): return lax.ppermute(x, 'tp', [(0, 1), (1, 0)])  4.87 us
  transfers between devices with their start and end apart: 11, of which 7 were waited for; matrix products, arithmetic and copies ran while one was open for 1% of the time, Pallas kernels for 0%

profile of v1, /device:TPU:0, one launch (start us, length us, event | category | flops | bytes accessed | tf_op | source)
XLA Modules:
  0.0 242.9 jit_solution(4479982008391979038)
XLA Ops:
  0.6 1.3 reshape.27.s1_ref
  1.9 1.3 reshape.28.b1_ref
  3.2 1.3 reshape.29.bqkv_ref
  4.5 64.6 %attention.1 = (bf16[512,1024]{1,0:T(8,128)(2,1)}, bf16[512,4,64,128]{3,2,1,0:T(8,128)(2,1)}, bf16[512,4,64,128]{3,2,1,0:T(8,128)(2,1)}) custom-call(s32[512]{0:T(512)} %len_ref.1, bf16[512,1024]{1,0:T(8,128)(2,1)} %hid_ref.3, f32[32,512]{1,0:T(8,128)} %bitcast.11, f32[32,512]{1,0:T(8,128)} %bitcast.12, bf16[1,1024]{1,0:T(2,128)(2,1)} %reshape.27.s1_ref, ...), custom_call_target="tpu_custom_call" | custom-call | flops 10240000000 | bytes 134217728 | tf_op jit(solution)/shard_map/attention/pallas_call | solution.py:135
  69.1 3.4 %collective-permute-start = (bf16[512,1024]{1,0:T(8,128)(2,1)}, bf16[512,1024]{1,0:T(8,128)(2,1)S(1)}, u32[]{:S(2)}, u32[]{:S(2)}) collective-permute-start(bf16[512,1024]{1,0:T(8,128)(2,1)} %get-tuple-element.12.one_ref), channel_id=1, source_target_pairs={{0,4},{4,0},{1,5},{5,1},{2,6},{6,2},{3,7},{7,3}} | collective-permute-start | bytes 3145736 | tf_op jit(solution)/shard_map/ppermute | solution.py:251
  72.5 0.6 reshape.30.bo_ref
  73.7 0.6 reshape.32.b2_ref
  74.2 21.4 %collective-permute-done.two_ref = bf16[512,1024]{1,0:T(8,128)(2,1)S(1)} collective-permute-done((bf16[512,1024]{1,0:T(8,128)(2,1)}, bf16[512,1024]{1,0:T(8,128)(2,1)S(1)}, u32[]{:S(2)}, u32[]{:S(2)}) %collective-permute-start) | collective-permute-done | bytes 1048608 | tf_op jit(solution)/shard_map/ppermute | solution.py:251
  95.6 1.0 copy-done
  96.6 4.4 %middle.1 = (bf16[512,1024]{1,0:T(8,128)(2,1)}, bf16[512,1024]{1,0:T(8,128)(2,1)}) custom-call(bf16[512,1024]{1,0:T(8,128)(2,1)} %hid_ref.3, bf16[512,1024]{1,0:T(8,128)(2,1)} %get-tuple-element.12.one_ref, bf16[512,1024]{1,0:T(8,128)(2,1)} %copy-done, bf16[1,1024]{1,0:T(2,128)(2,1)} %reshape.30.bo_ref, bf16[1,1024]{1,0:T(2,128)(2,1)} %reshape.31.s2_ref, ...), custom_call_target="tpu_custom_call" | custom-call | flops 204800000 | bytes 5242880 | tf_op jit(solution)/shard_map/middle/pallas_call | solution.py:164
  101.0 1.7 collective-permute-start.2
  102.7 22.6 %collective-permute-done.2.x2 = bf16[512,1024]{1,0:T(8,128)(2,1)S(1)} collective-permute-done((bf16[512,1024]{1,0:T(8,128)(2,1)}, bf16[512,1024]{1,0:T(8,128)(2,1)S(1)}, u32[]{:S(2)}, u32[]{:S(2)}) %collective-permute-start.2) | collective-permute-done | bytes 1048608 | tf_op jit(solution)/shard_map/ppermute | solution.py:248
  125.3 1.5 collective-permute-start.5
  126.9 2.1 collective-permute-done.5.i2
  129.1 1.2 collective-permute-done.6.i3
  131.5 55.1 %experts.1 = (bf16[512,1024]{1,0:T(8,128)(2,1)}, bf16[512,1024]{1,0:T(8,128)(2,1)}, bf16[512,1024]{1,0:T(8,128)(2,1)}, bf16[512,1024]{1,0:T(8,128)(2,1)}) custom-call(s32[1]{0:T(128)} %bitcast.4.first_ref, bf16[512,1024]{1,0:T(8,128)(2,1)} %get-tuple-element.14.x0, bf16[512,1024]{1,0:T(8,128)(2,1)} %copy-done.7, bf16[512,1024]{1,0:T(8,128)(2,1)} %copy-done.6, ...), custom_call_target="tpu_custom_call" | custom-call | flops 26214400000 | bytes 14000000 | tf_op jit(solution)/shard_map/experts/pallas_call | solution.py:225
  187.2 2.1 collective-permute-done.8
  189.3 1.6 add_convert_fusion.2
  190.9 1.5 collective-permute-start.9
  192.4 23.8 %collective-permute-done.9 = bf16[512,1024]{1,0:T(8,128)(2,1)S(1)} collective-permute-done((bf16[512,1024]{1,0:T(8,128)(2,1)S(1)}, bf16[512,1024]{1,0:T(8,128)(2,1)S(1)}, u32[]{:S(2)}, u32[]{:S(2)}) %collective-permute-start.9) | collective-permute-done | bytes 1048608 | tf_op jit(solution)/shard_map/ppermute | solution.py:248
  216.2 0.7 add_convert_fusion.1
  216.8 1.5 collective-permute-start.10
  218.3 22.9 %collective-permute-done.10 = bf16[512,1024]{1,0:T(8,128)(2,1)S(1)} collective-permute-done((bf16[512,1024]{1,0:T(8,128)(2,1)S(1)}, bf16[512,1024]{1,0:T(8,128)(2,1)S(1)}, u32[]{:S(2)}, u32[]{:S(2)}) %collective-permute-start.10) | collective-permute-done | bytes 1048608 | tf_op jit(solution)/shard_map/ppermute | solution.py:251
  241.2 1.6 add_convert_fusion
  (36 shorter events, 2.6 us)
Async XLA Ops:
  4.5 68.0 %copy-start.3 = (bf16[1024]{0:T(1024)(128)(2,1)S(1)}, bf16[1024]{0:T(1024)(128)(2,1)}, u32[]{:S(2)}) copy-start(bf16[1024]{0:T(1024)(128)(2,1)} %param.28) | copy-start | bytes 6148
  4.5 68.6 %copy-start.4 = (bf16[1024]{0:T(1024)(128)(2,1)S(1)}, bf16[1024]{0:T(1024)(128)(2,1)}, u32[]{:S(2)}) copy-start(bf16[1024]{0:T(1024)(128)(2,1)} %param.31) | copy-start | bytes 6148
  4.5 69.2 %copy-start.5 = (bf16[1024]{0:T(1024)(128)(2,1)S(1)}, bf16[1024]{0:T(1024)(128)(2,1)}, u32[]{:S(2)}) copy-start(bf16[1024]{0:T(1024)(128)(2,1)} %param.32) | copy-start | bytes 6148
  69.0 56.2 %copy-start.9 = (s32[512,8]{0,1:T(8,128)S(1)}, s32[512,8]{0,1:T(8,128)}, u32[]{:S(2)}) copy-start(s32[512,8]{0,1:T(8,128)} %param.34) | copy-start | bytes 49156
  69.1 26.5 %collective-permute-start = (bf16[512,1024]{1,0:T(8,128)(2,1)}, bf16[512,1024]{1,0:T(8,128)(2,1)S(1)}, u32[]{:S(2)}, u32[]{:S(2)}) collective-permute-start(bf16[512,1024]{1,0:T(8,128)(2,1)} %get-tuple-element.12.one_ref), channel_id=1, source_target_pairs={{0,4},{4,0},{1,5},{5,1},{2,6},{6,2},{3,7},{7,3}} | collective-permute-start | bytes 3145736 | tf_op jit(solution)/shard_map/ppermute | solution.py:251
  95.6 1.0 copy-start
  101.0 24.3 %collective-permute-start.2 = (bf16[512,1024]{1,0:T(8,128)(2,1)}, bf16[512,1024]{1,0:T(8,128)(2,1)S(1)}, u32[]{:S(2)}, u32[]{:S(2)}) collective-permute-start(bf16[512,1024]{1,0:T(8,128)(2,1)} %get-tuple-element.14.x0), channel_id=1, source_target_pairs={{0,2},{1,3},{2,0},{3,1},{4,6},{5,7},{6,4},{7,5}} | collective-permute-start | bytes 3145736 | tf_op jit(solution)/shard_map/ppermute | solution.py:248
  102.7 27.6 %collective-permute-start.1 = (bf16[512,1024]{1,0:T(8,128)(2,1)}, bf16[512,1024]{1,0:T(8,128)(2,1)S(1)}, u32[]{:S(2)}, u32[]{:S(2)}) collective-permute-start(bf16[512,1024]{1,0:T(8,128)(2,1)} %get-tuple-element.14.x0), channel_id=1, source_target_pairs={{0,1},{1,0},{2,3},{3,2},{4,5},{5,4},{6,7},{7,6}} | collective-permute-start | bytes 3145736 | tf_op jit(solution)/shard_map/ppermute | solution.py:248
  125.3 5.0 %copy-start.6 = (bf16[512,1024]{1,0:T(8,128)(2,1)}, bf16[512,1024]{1,0:T(8,128)(2,1)S(1)}, u32[]{:S(2)}) copy-start(bf16[512,1024]{1,0:T(8,128)(2,1)S(1)} %collective-permute-done.2.x2) | copy-start | bytes 3145732
  125.3 5.0 %collective-permute-start.3 = (bf16[512,1024]{1,0:T(8,128)(2,1)S(1)}, bf16[512,1024]{1,0:T(8,128)(2,1)S(1)}, u32[]{:S(2)}, u32[]{:S(2)}) collective-permute-start(bf16[512,1024]{1,0:T(8,128)(2,1)S(1)} %collective-permute-done.2.x2), channel_id=1, source_target_pairs={{0,1},{1,0},{2,3},{3,2},{4,5},{5,4},{6,7},{7,6}} | collective-permute-start | bytes 3145736 | tf_op jit(solution)/shard_map/ppermute | solution.py:248
  125.3 3.8 %collective-permute-start.5 = (s32[8,512]{1,0:T(8,128)S(1)}, s32[8,512]{1,0:T(8,128)S(1)}, u32[]{:S(2)}, u32[]{:S(2)}) collective-permute-start(s32[8,512]{1,0:T(8,128)S(1)} %bitcast.17), channel_id=1, source_target_pairs={{0,2},{1,3},{2,0},{3,1},{4,6},{5,7},{6,4},{7,5}} | collective-permute-start | bytes 49160 | tf_op jit(solution)/shard_map/ppermute | solution.py:248
  126.7 2.3 collective-permute-start.4
  129.0 1.2 copy-start.10
  129.1 1.2 collective-permute-start.6
  129.1 1.2 copy-start.11
  130.2 0.6 copy-start.12
  130.2 1.0 copy-start.7
  130.2 1.3 copy-start.8
  186.6 29.6 %copy-start.2 = (bf16[512,1024]{1,0:T(8,128)(2,1)S(1)}, bf16[512,1024]{1,0:T(8,128)(2,1)}, u32[]{:S(2)}) copy-start(bf16[512,1024]{1,0:T(8,128)(2,1)} %get-tuple-element.15) | copy-start | bytes 3145732
  186.6 2.7 %collective-permute-start.8 = (bf16[512,1024]{1,0:T(8,128)(2,1)}, bf16[512,1024]{1,0:T(8,128)(2,1)S(1)}, u32[]{:S(2)}, u32[]{:S(2)}) collective-permute-start(bf16[512,1024]{1,0:T(8,128)(2,1)} %get-tuple-element.18), channel_id=1, source_target_pairs={{0,1},{1,0},{2,3},{3,2},{4,5},{5,4},{6,7},{7,6}} | collective-permute-start | bytes 3145736 | tf_op jit(solution)/shard_map/ppermute | solution.py:248
  186.8 5.6 %collective-permute-start.7 = (bf16[512,1024]{1,0:T(8,128)(2,1)}, bf16[512,1024]{1,0:T(8,128)(2,1)S(1)}, u32[]{:S(2)}, u32[]{:S(2)}) collective-permute-start(bf16[512,1024]{1,0:T(8,128)(2,1)} %get-tuple-element.16), channel_id=1, source_target_pairs={{0,1},{1,0},{2,3},{3,2},{4,5},{5,4},{6,7},{7,6}} | collective-permute-start | bytes 3145736 | tf_op jit(solution)/shard_map/ppermute | solution.py:248
  190.9 25.2 %collective-permute-start.9 = (bf16[512,1024]{1,0:T(8,128)(2,1)S(1)}, bf16[512,1024]{1,0:T(8,128)(2,1)S(1)}, u32[]{:S(2)}, u32[]{:S(2)}) collective-permute-start(bf16[512,1024]{1,0:T(8,128)(2,1)S(1)} %add_convert_fusion.2), channel_id=1, source_target_pairs={{0,2},{1,3},{2,0},{3,1},{4,6},{5,7},{6,4},{7,5}} | collective-permute-start | bytes 3145736 | tf_op jit(solution)/shard_map/ppermute | solution.py:248
  216.2 25.1 %copy-start.1 = (bf16[512,1024]{1,0:T(8,128)(2,1)S(1)}, bf16[512,1024]{1,0:T(8,128)(2,1)}, u32[]{:S(2)}) copy-start(bf16[512,1024]{1,0:T(8,128)(2,1)} %get-tuple-element.13) | copy-start | bytes 3145732
  216.8 24.4 %collective-permute-start.10 = (bf16[512,1024]{1,0:T(8,128)(2,1)S(1)}, bf16[512,1024]{1,0:T(8,128)(2,1)S(1)}, u32[]{:S(2)}, u32[]{:S(2)}) collective-permute-start(bf16[512,1024]{1,0:T(8,128)(2,1)S(1)} %add_convert_fusion.1), channel_id=1, source_target_pairs={{0,4},{4,0},{1,5},{5,1},{2,6},{6,2},{3,7},{7,3}} | collective-permute-start | bytes 3145736 | tf_op jit(solution)/shard_map/ppermute | solution.py:251

commit v2 on v1

v2 whole, which is shorter than its diff:
```python
import functools

import jax
import jax.numpy as jnp
from jax import lax
from jax.experimental import pallas as pl
from jax.experimental.pallas import tpu as pltpu
from jax.sharding import PartitionSpec as P

EPS = 1e-5
BF = jnp.bfloat16
F32 = jnp.float32
CHUNKS = 4
SUB = 128
BB = 16
SLOTS = 8
AHEAD = 5
VMEM_LIMIT = 60 * 1024 * 1024


def norm_rows(x, scale, bias):
    mean = jnp.mean(x, axis=-1, keepdims=True)
    cen = x - mean
    var = jnp.mean(cen * cen, axis=-1, keepdims=True)
    return (cen * lax.rsqrt(var + EPS) * scale + bias).astype(BF)


def wide(ref):
    return ref[...].astype(F32).reshape(1, -1)


def attention_kernel(base_row, has_prev, len_ref, hid_ref, cos_ref, sin_ref, s1_ref, b1_ref, bqkv_ref, wqkv_hbm, wout_hbm, k_hbm, v_hbm, *rest):
    part_ref, ko_hbm, vo_hbm = rest[2 * has_prev:2 * has_prev + 3]
    wqkv_ref, wout_ref, kb_ref, vb_ref, qs_ref, kt_ref, vt_ref, sc_ref, pr_ref, cx_ref, ctx_ref, in_sem, out_sem, w_sem = rest[2 * has_prev + 3:]
    step = pl.program_id(0)
    n_step = pl.num_programs(0)
    per_sub = SUB // BB
    j = lax.rem(step, per_sub)
    lane = lax.broadcasted_iota(jnp.int32, (SUB, 128), 1)
    low = lane < 64

    def moves(s, out):
        slot = lax.rem(s, SLOTS)
        src = pl.ds(base_row + s * BB, BB)
        pairs = ((k_hbm, kb_ref, ko_hbm, 0), (v_hbm, vb_ref, vo_hbm, 1))
        if out:
            return [(pltpu.make_async_copy(buf.at[slot], dst.at[src], out_sem.at[t, slot]), t) for _, buf, dst, t in pairs]
        return [(pltpu.make_async_copy(hbm.at[src], buf.at[slot], in_sem.at[t, slot]), t) for hbm, buf, _, t in pairs]

    def begin(s, out):
        for copy, t in moves(s, out):
            copy.start(priority=t)

    def finish(s, out):
        for copy, _ in moves(s, out):
            copy.wait()

    load_qkv = pltpu.make_async_copy(wqkv_hbm, wqkv_ref, w_sem.at[0])
    load_out = pltpu.make_async_copy(wout_hbm, wout_ref, w_sem.at[1])

    @pl.when(step == 0)
    def _():
        load_qkv.start()
        for s in range(AHEAD):
            begin(s, False)
        load_out.start()
        load_qkv.wait()

    @pl.when(j == 0)
    def _():
        normed = norm_rows(hid_ref[...].astype(F32), wide(s1_ref), wide(b1_ref))
        qkv = jnp.dot(normed, wqkv_ref[...], preferred_element_type=F32) + wide(bqkv_ref)
        qkv = qkv.astype(BF).astype(F32)
        col = [qkv[:, m * 128:(m + 1) * 128] for m in range(8)]
        rol = [pltpu.roll(c, 64, 1) for c in col]

        def first(a, b):
            return jnp.where(low, col[a], rol[b])

        def second(a, b):
            return jnp.where(low, rol[a], col[b])

        cos_t, sin_t = cos_ref[...], sin_ref[...]
        cos = jnp.transpose(jnp.concatenate([cos_t] * 4, axis=0))
        sin = jnp.transpose(jnp.concatenate([-sin_t, sin_t] * 2, axis=0))

        def rope(x):
            other = jnp.where(lane % 64 < 32, pltpu.roll(x, 96, 1), pltpu.roll(x, 32, 1))
            return (x * cos + other * sin).astype(BF).astype(F32)

        for h in range(2):
            q0 = rope(first(4 * h, 4 * h + 2))
            q1 = rope(second(4 * h, 4 * h + 2))
            kk = rope(first(4 * h + 1, 4 * h + 3))
            vv = second(4 * h + 1, 4 * h + 3)
            kt_ref[h * 128:(h + 1) * 128, :] = jnp.transpose(kk)
            vt_ref[h * 128:(h + 1) * 128, :] = jnp.transpose(vv)
            for r in range(8):
                src = q0 if r % 2 == 0 else q1
                if r // 4 == h:
                    src = jnp.where(low if (r // 2) % 2 == 0 else ~low, src, 0.0)
                else:
                    src = jnp.zeros_like(src)
                qs_ref[pl.ds(h * SUB * 8 + r, SUB, stride=8), :] = src

    slot = lax.rem(step, SLOTS)
    finish(step, False)
    shift = lax.rem(SUB - j * BB, SUB)
    kt = pltpu.roll(kt_ref[...], shift, 1)
    vt = pltpu.roll(vt_ref[...], shift, 1)
    lane8 = lax.broadcasted_iota(jnp.int32, (8, 128), 1)
    lane256 = lax.broadcasted_iota(jnp.int32, (256, 128), 1)
    row0 = pl.multiple_of(j * BB * 8, BB * 8)
    base = base_row + step * BB
    for b in range(BB):
        pos = len_ref[base + b]
        k_old = kb_ref[slot, b].reshape(256, 128).astype(F32)
        k_new = jnp.where(lane256 == pos, kt[:, b:b + 1], k_old).astype(BF)
        kb_ref[slot, b] = k_new.reshape(4, 64, 128)
        q_one = jnp.concatenate([qs_ref[pl.ds(row0 + h * SUB * 8 + b * 8, 8), :] for h in range(2)], axis=1).astype(BF)
        s_one = jnp.dot(q_one, k_new, preferred_element_type=F32) * 0.125
        sc_ref[b * 8:(b + 1) * 8, :] = jnp.where(lane8 <= pos, s_one, -jnp.inf)
    s_all = sc_ref[...]
    e_all = jnp.exp(s_all - jnp.max(s_all, axis=-1, keepdims=True))
    pr_ref[...] = e_all / jnp.sum(e_all, axis=-1, keepdims=True)
    for b in range(BB):
        pos = len_ref[base + b]
        v_old = vb_ref[slot, b].reshape(256, 128).astype(F32)
        v_new = jnp.where(lane256 == pos, vt[:, b:b + 1], v_old).astype(BF)
        vb_ref[slot, b] = v_new.reshape(4, 64, 128)
        p_one = pr_ref[b * 8:(b + 1) * 8, :].astype(BF)
        c_one = lax.dot_general(p_one, v_new, (((1,), (1,)), ((), ())), preferred_element_type=F32)
        cx_ref[b * 8:(b + 1) * 8, :] = c_one[:, :128]
        cx_ref[BB * 8 + b * 8:BB * 8 + (b + 1) * 8, :] = c_one[:, 128:]
    low_b = lax.broadcasted_iota(jnp.int32, (BB, 128), 1) < 64
    for h in range(2):
        for g in range(2):
            r = 4 * h + 2 * g
            one = cx_ref[pl.ds(h * BB * 8 + r, BB, stride=8), :]
            two = cx_ref[pl.ds(h * BB * 8 + r + 1, BB, stride=8), :]
            if g == 0:
                both = jnp.where(low_b, one, pltpu.roll(two, 64, 1))
            else:
                both = jnp.where(low_b, pltpu.roll(one, 64, 1), two)
            ctx_ref[pl.ds(pl.multiple_of(j * BB, BB), BB), (2 * h + g) * 128:(2 * h + g + 1) * 128] = both.astype(BF)

    begin(step, True)

    @pl.when(step + AHEAD < n_step)
    def _():
        @pl.when(step + AHEAD >= SLOTS)
        def _():
            finish(step + AHEAD - SLOTS, True)

        begin(step + AHEAD, False)

    @pl.when(step == per_sub - 1)
    def _():
        load_out.wait()

    @pl.when(j == per_sub - 1)
    def _():
        part_ref[...] = jnp.dot(ctx_ref[...], wout_ref[...], preferred_element_type=F32).astype(BF)

    @pl.when(step == n_step - 1)
    def _():
        for back in range(SLOTS - 1, -1, -1):
            @pl.when(step >= back)
            def _():
                finish(step - back, True)


def attention(chunk, rows, lens, hidden, cos_t, sin_t, s1, b1, wqkv, bqkv, wout, kt, vt, prev):
    per_sub = SUB // BB
    n_step = rows // BB
    first = chunk * rows // SUB
    vec = pl.BlockSpec((1024,), lambda i, s: (0,))
    hbm = pl.BlockSpec(memory_space=pl.ANY)
    in_specs = [
        pl.BlockSpec((SUB, 1024), lambda i, s: (first + i // per_sub, 0)),
        pl.BlockSpec((32, SUB), lambda i, s: (0, first + i // per_sub)),
        pl.BlockSpec((32, SUB), lambda i, s: (0, first + i // per_sub)),
        vec, vec, vec, hbm, hbm, hbm, hbm,
    ]
    args = [lens, hidden, cos_t, sin_t, s1, b1, bqkv, wqkv, wout, kt, vt]
    aliases = {}
    if prev is not None:
        in_specs += [hbm, hbm]
        aliases = {len(args): 1, len(args) + 1: 2}
        args += list(prev)
    return pl.pallas_call(
        functools.partial(attention_kernel, chunk * rows, int(prev is not None)),
        grid_spec=pltpu.PrefetchScalarGridSpec(
            num_scalar_prefetch=1, grid=(n_step,), in_specs=in_specs,
            out_specs=[pl.BlockSpec((SUB, 1024), lambda i, s: (i // per_sub, 0)), hbm, hbm],
            scratch_shapes=[
                pltpu.VMEM(wqkv.shape, BF), pltpu.VMEM(wout.shape, BF),
                pltpu.VMEM((SLOTS, BB, 4, 64, 128), BF), pltpu.VMEM((SLOTS, BB, 4, 64, 128), BF),
                pltpu.VMEM((2 * SUB * 8, 128), F32), pltpu.VMEM((256, SUB), F32), pltpu.VMEM((256, SUB), F32),
                pltpu.VMEM((BB * 8, 128), F32), pltpu.VMEM((BB * 8, 128), F32),
                pltpu.VMEM((2 * BB * 8, 128), F32), pltpu.VMEM((SUB, 512), BF),
                pltpu.SemaphoreType.DMA((2, SLOTS)), pltpu.SemaphoreType.DMA((2, SLOTS)), pltpu.SemaphoreType.DMA((2,))]),
        out_shape=[jax.ShapeDtypeStruct((rows, 1024), BF), jax.ShapeDtypeStruct(kt.shape, BF), jax.ShapeDtypeStruct(vt.shape, BF)],
        input_output_aliases=aliases,
        compiler_params=pltpu.CompilerParams(dimension_semantics=("arbitrary",), vmem_limit_bytes=40 * 1024 * 1024),
        cost_estimate=pl.CostEstimate(flops=rows * 20_000_000, bytes_accessed=rows * 262144, transcendentals=0),
        name="attention",
    )(*args)


def mid_kernel(hid_ref, one_ref, two_ref, bo_ref, s2_ref, b2_ref, x1_ref, h2_ref):
    attn = one_ref[...].astype(F32) + two_ref[...].astype(F32)
    x1 = (hid_ref[...].astype(F32) + attn + wide(bo_ref)).astype(BF)
    x1_ref[...] = x1
    h2_ref[...] = norm_rows(x1.astype(F32), wide(s2_ref), wide(b2_ref))


def middle(chunk, rows, hidden, one, two, b_out, s2, b2):
    tile = 128
    off = chunk * rows // tile
    vec = pl.BlockSpec((1024,), lambda i: (0,))
    blk = pl.BlockSpec((tile, 1024), lambda i: (i, 0))
    return pl.pallas_call(
        mid_kernel, grid=(rows // tile,),
        in_specs=[pl.BlockSpec((tile, 1024), lambda i: (off + i, 0)), blk, blk, vec, vec, vec],
        out_specs=[blk, blk],
        out_shape=[jax.ShapeDtypeStruct((rows, 1024), BF)] * 2,
        cost_estimate=pl.CostEstimate(flops=rows * 400_000, bytes_accessed=rows * 10240, transcendentals=0),
        name="middle",
    )(hidden, one, two, b_out, s2, b2)


def expert_kernel(rows, first_ref, x0, x1, x2, x3, i0, i1, i2, i3, wr_ref, wg_ref, wu_ref, wd_ref, o0, o1, o2, o3, acc_ref, gate_ref):
    e = pl.program_id(0)
    n_e = pl.num_programs(0)
    xs, ids, outs = (x0, x1, x2, x3), (i0, i1, i2, i3), (o0, o1, o2, o3)
    tile = min(rows, 256)

    @pl.when(e == 0)
    def _():
        for n in range(4):
            logit = lax.dot_general(wr_ref[...], xs[n][...], (((1,), (1,)), ((), ())), preferred_element_type=F32)
            eid = lax.broadcasted_iota(jnp.int32, (32, rows), 0)
            picked = eid == ids[n][0:1, :]
            for m in range(1, 8):
                picked = picked | (eid == ids[n][m:m + 1, :])
            logit = jnp.where(picked, logit, -jnp.inf)
            ex = jnp.exp(logit - jnp.max(logit, axis=0, keepdims=True))
            prob = (ex / jnp.sum(ex, axis=0, keepdims=True)).astype(BF).astype(F32)
            gate_ref[n * rows:(n + 1) * rows, :] = jnp.transpose(prob)

        acc_ref[...] = jnp.zeros_like(acc_ref)

    mine = first_ref[0] + e
    lane = lax.broadcasted_iota(jnp.int32, (tile, 32), 1)
    for n in range(4):
        for t in range(rows // tile):
            row = n * rows + t * tile
            x = xs[n][t * tile:(t + 1) * tile, :]
            gate = jnp.dot(x, wg_ref[0], preferred_element_type=F32)
            up = jnp.dot(x, wu_ref[0], preferred_element_type=F32)
            act = (gate * jax.nn.sigmoid(gate) * up).astype(BF)
            y = jnp.dot(act, wd_ref[0], preferred_element_type=F32)
            g_one = jnp.sum(jnp.where(lane == mine, gate_ref[row:row + tile, :], 0.0), axis=-1, keepdims=True)
            acc_ref[row:row + tile, :] += g_one * y

    @pl.when(e == n_e - 1)
    def _():
        for n in range(4):
            outs[n][...] = acc_ref[n * rows:(n + 1) * rows, :].astype(BF)


def experts(rows, first, xs, ids, wr_t, wg, wu, wd):
    n_e = wg.shape[0]
    full = lambda shape: pl.BlockSpec(shape, lambda e, s: (0,) * len(shape), pipeline_mode=pl.Buffered(1))
    wspec = lambda a: pl.BlockSpec((1,) + a.shape[1:], lambda e, s: (e, 0, 0))
    return pl.pallas_call(
        functools.partial(expert_kernel, rows),
        grid_spec=pltpu.PrefetchScalarGridSpec(
            num_scalar_prefetch=1, grid=(n_e,),
            in_specs=[full((rows, 1024))] * 4 + [full((8, rows))] * 4 + [full((32, 1024)), wspec(wg), wspec(wu), wspec(wd)],
            out_specs=[full((rows, 1024))] * 4,
            scratch_shapes=[pltpu.VMEM((4 * rows, 1024), F32), pltpu.VMEM((4 * rows, 32), F32)]),
        out_shape=[jax.ShapeDtypeStruct((rows, 1024), BF)] * 4,
        compiler_params=pltpu.CompilerParams(dimension_semantics=("arbitrary",), vmem_limit_bytes=VMEM_LIMIT),
        cost_estimate=pl.CostEstimate(flops=rows * 4 * n_e * 1_600_000, bytes_accessed=14_000_000, transcendentals=0),
        name="experts",
    )(first, *xs, *ids, wr_t, wg, wu, wd)


def finish_kernel(x1_ref, one_ref, two_ref, *rest):
    moe = one_ref[...].astype(F32) + two_ref[...].astype(F32)
    rest[-1][...] = (x1_ref[...].astype(F32) + moe).astype(BF)


def finish_rows(chunk, n_batch, x1, one, two, prev):
    rows = x1.shape[0]
    blk = pl.BlockSpec((rows, 1024), lambda i: (0, 0))
    more = [] if prev is None else [prev]
    return pl.pallas_call(
        finish_kernel, grid=(1,),
        in_specs=[blk] * 3 + [pl.BlockSpec(memory_space=pl.ANY)] * len(more),
        out_specs=pl.BlockSpec((rows, 1024), lambda i: (chunk, 0)),
        out_shape=jax.ShapeDtypeStruct((n_batch, 1024), BF),
        input_output_aliases={3: 0} if more else {},
        cost_estimate=pl.CostEstimate(flops=rows * 100_000, bytes_accessed=rows * 8192, transcendentals=0),
        name="finish",
    )(x1, one, two, *more)


def add_rows(one, two):
    return (one.astype(F32) + two.astype(F32)).astype(BF)


def solution(mesh):
    n_ep = mesh.shape['ep']
    token_rows = P(('dp', 'ep'), None)
    token_vec = P(('dp', 'ep'))
    cache_spec = P(('dp', 'ep'), None, 'tp', None)
    expert_in = P('ep', None, 'tp')
    expert_down = P('ep', 'tp', None)

    def swap_ep(x, bit):
        return lax.ppermute(x, 'ep', [(d, d ^ bit) for d in range(n_ep)])

    def swap_tp(x):
        return lax.ppermute(x, 'tp', [(0, 1), (1, 0)])

    def device_step(hidden, seq_lens, rope_cos, rope_sin, ln1_scale, ln1_bias, w_qkv, b_qkv, w_out, b_out, k_cache, v_cache, ln2_scale, ln2_bias, w_router, expert_ids, w_gate, w_up, w_down):
        n_batch = hidden.shape[0]
        rows = n_batch // CHUNKS
        kt, vt = (jnp.transpose(c, (0, 2, 3, 1)) for c in (k_cache, v_cache))
        ids_far = swap_ep(expert_ids.T, 2)
        ids_near = swap_ep(expert_ids.T, 1)
        ids = [expert_ids.T, ids_near, ids_far, swap_ep(ids_far, 1)]
        first = (lax.axis_index('ep') * w_gate.shape[0]).astype(jnp.int32).reshape(1)
        prev, out, x1s, h2s = None, None, [], []
        for c in range(CHUNKS):
            part, *prev = attention(c, rows, seq_lens, hidden, rope_cos.T, rope_sin.T, ln1_scale, ln1_bias, w_qkv, b_qkv, w_out, kt, vt, prev)
            other = swap_tp(part)
            x1, h2 = middle(c, rows, hidden, part, other, b_out, ln2_scale, ln2_bias)
            far = swap_ep(h2, 2)
            near = swap_ep(h2, 1)
            both = swap_ep(far, 1)
            x1s.append(x1)
            h2s.append([h2, near, far, both])
        for c in range(CHUNKS):
            o = experts(rows, first, h2s[c], [a[:, c * rows:(c + 1) * rows] for a in ids], w_router.T, w_gate, w_up, w_down)
            from_near = swap_ep(o[1], 1)
            from_pass = swap_ep(o[3], 1)
            far = add_rows(o[2], from_pass)
            from_far = swap_ep(far, 2)
            near = add_rows(o[0], from_near)
            total = add_rows(near, from_far)
            other = swap_tp(total)
            out = finish_rows(c, n_batch, x1s[c], total, other, out)
        return out, *(jnp.transpose(c, (0, 3, 1, 2)) for c in prev)

    in_specs = (token_rows, token_vec, token_rows, token_rows, P(), P(), P(None, 'tp'), P('tp'), P('tp', None), P(), cache_spec, cache_spec, P(), P(), P(), token_rows, expert_in, expert_in, expert_down)
    return jax.shard_map(device_step, mesh=mesh, in_specs=in_specs, out_specs=(token_rows, cache_spec, cache_spec), check_vma=False)
```

time: 243 us -> 219 us (0.901)
  waiting for transfers between devices: 96.1 us -> 24.8 us
  Pallas kernels: 124 us -> 144 us
  starting transfers between devices: 10.2 us -> 27 us
  local copies, waits for them, and re-layouts: 7.88 us -> 17.4 us
    ppermute x9 -> x27, waiting for transfers between devices: 51.8 us -> 13 us  [swap_ep(): return lax.ppermute(x, 'ep', [(d, d ^ bit) for d in range(n_ep)])]
    ppermute x2 -> x8, waiting for transfers between devices: 44.3 us -> 11.8 us  [swap_tp(): return lax.ppermute(x, 'tp', [(0, 1), (1, 0)])]
    unnamed x26 -> x84, local copies, waits for them, and re-layouts: 2.28 us -> 15 us
    ppermute x9 -> x27, starting transfers between devices: 5.35 us -> 14.5 us  [swap_ep(): return lax.ppermute(x, 'ep', [(d, d ^ bit) for d in range(n_ep)])]
    pallas_call x1 -> x4, Pallas kernels: 55.1 us -> 63 us  [experts(): pl.pallas_call(functools.partial(expert_kernel, rows), grid_spec=pltpu.Pr...]
    ppermute x2 -> x8, starting transfers between devices: 4.87 us -> 12.5 us  [swap_tp(): return lax.ppermute(x, 'tp', [(0, 1), (1, 0)])]
    pallas_call x1 -> x8, Pallas kernels: 64.6 us -> 72.2 us  [the longest x4 64.5 us: attention(): pl.pallas_call(functools.partial(attention_kernel, chunk * rows, int(prev...]
    reshape x6 -> x0, local copies, waits for them, and re-layouts: 5.61 us -> none  [device_step(): row = lambda a: a.reshape(1, -1)]
  transfers between devices with their start and end apart: 11 -> 35, of which waited for: 7 -> 7; matrix products, arithmetic and copies ran while one was open for 1% -> 3% of each run, Pallas kernels for 0% -> 35%
where the time goes in v2:
time: 219 us
  Pallas kernels  144 us (66%)
  starting transfers between devices  27 us (12%)
  waiting for transfers between devices  24.8 us (11%)
  local copies, waits for them, and re-layouts  17.4 us (8%)
  other arithmetic  4.55 us (2%)
    pallas_call x4, Pallas kernels, attention(): pl.pallas_call(functools.partial(attention_kernel, chunk * rows, int(prev...  64.5 us
    pallas_call x4, Pallas kernels, experts(): pl.pallas_call(functools.partial(expert_kernel, rows), grid_spec=pltpu.Pr...  63 us
    unnamed x84, local copies, waits for them, and re-layouts  15 us
    ppermute x27, starting transfers between devices, swap_ep(): return lax.ppermute(x, 'ep', [(d, d ^ bit) for d in range(n_ep)])  14.5 us
    ppermute x27, waiting for transfers between devices, swap_ep(): return lax.ppermute(x, 'ep', [(d, d ^ bit) for d in range(n_ep)])  13 us
    ppermute x8, starting transfers between devices, swap_tp(): return lax.ppermute(x, 'tp', [(0, 1), (1, 0)])  12.5 us
    ppermute x8, waiting for transfers between devices, swap_tp(): return lax.ppermute(x, 'tp', [(0, 1), (1, 0)])  11.8 us
    pallas_call x4, Pallas kernels, middle(): pl.pallas_call(mid_kernel, grid=(rows // tile,), in_specs=[pl.BlockSpec((...  8.74 us
  transfers between devices with their start and end apart: 35, of which 7 were waited for; matrix products, arithmetic and copies ran while one was open for 3% of the time, Pallas kernels for 35%

profile of v2, /device:TPU:0, one launch (start us, length us, event | category | flops | bytes accessed | tf_op | source)
XLA Modules:
  0.0 218.7 jit_solution(3401514593537246852)
XLA Ops:
  9.1 16.1 %attention.4 = (bf16[128,1024]{1,0:T(8,128)(2,1)S(1)}, bf16[512,4,64,128]{3,2,1,0:T(8,128)(2,1)}, bf16[512,4,64,128]{3,2,1,0:T(8,128)(2,1)}) custom-call(s32[512]{0:T(512)S(1)} %copy-done.9, bf16[512,1024]{1,0:T(8,128)(2,1)S(1)} %copy-done, f32[32,512]{1,0:T(8,128)S(1)} %bitcast.9, f32[32,512]{1,0:T(8,128)S(1)} %bitcast.13, bf16[1024]{0:T(1024)(128)(2,1)S(1)} %copy-done.10, ...), custom_call_target="tpu_custom_call" | custom-call | flops 2560000000 | bytes 33554432 | tf_op jit(solution)/shard_map/attention/pallas_call | solution.py:191
  25.2 16.1 %attention.5 = (bf16[128,1024]{1,0:T(8,128)(2,1)S(1)}, bf16[512,4,64,128]{3,2,1,0:T(8,128)(2,1)}, bf16[512,4,64,128]{3,2,1,0:T(8,128)(2,1)}) custom-call(s32[512]{0:T(512)S(1)} %copy-done.9, bf16[512,1024]{1,0:T(8,128)(2,1)S(1)} %copy-done, f32[32,512]{1,0:T(8,128)S(1)} %bitcast.10, ...), custom_call_target="tpu_custom_call", output_to_operand_aliasing={{1}: (11, {}), {2}: (12, {})} | custom-call | flops 2560000000 | bytes 33554432 | tf_op jit(solution)/shard_map/attention/pallas_call | solution.py:191
  41.4 16.1 %attention.6 = (bf16[128,1024]{1,0:T(8,128)(2,1)S(1)}, bf16[512,4,64,128]{3,2,1,0:T(8,128)(2,1)}, bf16[512,4,64,128]{3,2,1,0:T(8,128)(2,1)}) custom-call(s32[512]{0:T(512)S(1)} %copy-done.9, bf16[512,1024]{1,0:T(8,128)(2,1)S(1)} %copy-done, f32[32,512]{1,0:T(8,128)S(1)} %bitcast.11, ...), custom_call_target="tpu_custom_call", output_to_operand_aliasing={{1}: (11, {}), {2}: (12, {})} | custom-call | flops 2560000000 | bytes 33554432 | tf_op jit(solution)/shard_map/attention/pallas_call | solution.py:191
  57.5 16.1 %attention.7 = (bf16[128,1024]{1,0:T(8,128)(2,1)S(1)}, bf16[512,4,64,128]{3,2,1,0:T(8,128)(2,1)}, bf16[512,4,64,128]{3,2,1,0:T(8,128)(2,1)}) custom-call(s32[512]{0:T(512)S(1)} %copy-done.9, bf16[512,1024]{1,0:T(8,128)(2,1)S(1)} %copy-done, f32[32,512]{1,0:T(8,128)S(1)} %bitcast.12, ...), custom_call_target="tpu_custom_call", output_to_operand_aliasing={{1}: (11, {}), {2}: (12, {})} | custom-call | flops 2560000000 | bytes 33554432 | tf_op jit(solution)/shard_map/attention/pallas_call | solution.py:191
  73.7 3.4 %collective-permute-start = (bf16[128,1024]{1,0:T(8,128)(2,1)S(1)}, bf16[128,1024]{1,0:T(8,128)(2,1)S(1)}, u32[]{:S(2)}, u32[]{:S(2)}) collective-permute-start(bf16[128,1024]{1,0:T(8,128)(2,1)S(1)} %get-tuple-element.45.one_ref), channel_id=1, source_target_pairs={{0,4},{4,0},{1,5},{5,1},{2,6},{6,2},{3,7},{7,3}} | collective-permute-start | bytes 786440 | tf_op jit(solution)/shard_map/ppermute | solution.py:327
  80.6 3.6 %collective-permute-done.two_ref = bf16[128,1024]{1,0:T(8,128)(2,1)S(1)} collective-permute-done((bf16[128,1024]{1,0:T(8,128)(2,1)S(1)}, bf16[128,1024]{1,0:T(8,128)(2,1)S(1)}, u32[]{:S(2)}, u32[]{:S(2)}) %collective-permute-start) | collective-permute-done | bytes 262176 | tf_op jit(solution)/shard_map/ppermute | solution.py:327
  84.9 2.2 %middle.4 = (bf16[128,1024]{1,0:T(8,128)(2,1)}, bf16[128,1024]{1,0:T(8,128)(2,1)}) custom-call(bf16[512,1024]{1,0:T(8,128)(2,1)} %hid_ref.15, bf16[128,1024]{1,0:T(8,128)(2,1)} %copy-done.8, bf16[128,1024]{1,0:T(8,128)(2,1)} %copy-done.25, bf16[1024]{0:T(1024)(128)(2,1)} %bo_ref.7, bf16[1024]{0:T(1024)(128)(2,1)} %s2_ref.7, bf16[1024]{0:T(1024)(128)(2,1)} %b2_ref.7), custom_call_target="tpu_custom_call" | custom-call | flops 51200000 | bytes 1310720 | tf_op jit(solution)/shard_map/middle/pallas_call | solution.py:223
  87.1 2.0 collective-permute-start.2
  91.9 2.2 middle.5
  97.7 2.2 middle.6
  100.9 2.2 %middle.7 = (bf16[128,1024]{1,0:T(8,128)(2,1)}, bf16[128,1024]{1,0:T(8,128)(2,1)}) custom-call(bf16[512,1024]{1,0:T(8,128)(2,1)} %hid_ref.15, bf16[128,1024]{1,0:T(8,128)(2,1)} %copy-done.5, bf16[128,1024]{1,0:T(8,128)(2,1)} %copy-done.23, bf16[1024]{0:T(1024)(128)(2,1)} %bo_ref.7, bf16[1024]{0:T(1024)(128)(2,1)} %s2_ref.7, bf16[1024]{0:T(1024)(128)(2,1)} %b2_ref.7), custom_call_target="tpu_custom_call" | custom-call | flops 51200000 | bytes 1310720 | tf_op jit(solution)/shard_map/middle/pallas_call | solution.py:223
  105.9 15.8 %experts.4 = (bf16[128,1024]{1,0:T(8,128)(2,1)}, bf16[128,1024]{1,0:T(8,128)(2,1)}, bf16[128,1024]{1,0:T(8,128)(2,1)}, bf16[128,1024]{1,0:T(8,128)(2,1)}) custom-call(s32[1]{0:T(128)} %bitcast.4.first_ref, bf16[128,1024]{1,0:T(8,128)(2,1)} %get-tuple-element.47.x0, bf16[128,1024]{1,0:T(8,128)(2,1)} %copy-done.37, bf16[128,1024]{1,0:T(8,128)(2,1)} %copy-done.30, ...), custom_call_target="tpu_custom_call" | custom-call | flops 6553600000 | bytes 14000000 | tf_op jit(solution)/shard_map/experts/pallas_call | solution.py:277
  123.0 15.8 %experts.5 = (bf16[128,1024]{1,0:T(8,128)(2,1)}, bf16[128,1024]{1,0:T(8,128)(2,1)}, bf16[128,1024]{1,0:T(8,128)(2,1)}, bf16[128,1024]{1,0:T(8,128)(2,1)}) custom-call(s32[1]{0:T(128)} %bitcast.4.first_ref, bf16[128,1024]{1,0:T(8,128)(2,1)} %get-tuple-element.54.x0, bf16[128,1024]{1,0:T(8,128)(2,1)} %copy-done.36, bf16[128,1024]{1,0:T(8,128)(2,1)} %copy-done.32, ...), custom_call_target="tpu_custom_call" | custom-call | flops 6553600000 | bytes 14000000 | tf_op jit(solution)/shard_map/experts/pallas_call | solution.py:277
  140.0 15.7 %experts.6 = (bf16[128,1024]{1,0:T(8,128)(2,1)}, bf16[128,1024]{1,0:T(8,128)(2,1)}, bf16[128,1024]{1,0:T(8,128)(2,1)}, bf16[128,1024]{1,0:T(8,128)(2,1)}) custom-call(s32[1]{0:T(128)} %bitcast.4.first_ref, bf16[128,1024]{1,0:T(8,128)(2,1)} %get-tuple-element.61.x0, bf16[128,1024]{1,0:T(8,128)(2,1)} %copy-done.33, bf16[128,1024]{1,0:T(8,128)(2,1)} %copy-done.34, ...), custom_call_target="tpu_custom_call" | custom-call | flops 6553600000 | bytes 14000000 | tf_op jit(solution)/shard_map/experts/pallas_call | solution.py:277
  156.5 15.7 %experts.7 = (bf16[128,1024]{1,0:T(8,128)(2,1)}, bf16[128,1024]{1,0:T(8,128)(2,1)}, bf16[128,1024]{1,0:T(8,128)(2,1)}, bf16[128,1024]{1,0:T(8,128)(2,1)}) custom-call(s32[1]{0:T(128)} %bitcast.4.first_ref, bf16[128,1024]{1,0:T(8,128)(2,1)} %get-tuple-element.68.x0, bf16[128,1024]{1,0:T(8,128)(2,1)} %copy-done.35, bf16[128,1024]{1,0:T(8,128)(2,1)} %copy-done.31, ...), custom_call_target="tpu_custom_call" | custom-call | flops 6553600000 | bytes 14000000 | tf_op jit(solution)/shard_map/experts/pallas_call | solution.py:277
  177.3 4.9 %collective-permute-done.17 = bf16[128,1024]{1,0:T(8,128)(2,1)S(1)} collective-permute-done((bf16[128,1024]{1,0:T(8,128)(2,1)S(1)}, bf16[128,1024]{1,0:T(8,128)(2,1)S(1)}, u32[]{:S(2)}, u32[]{:S(2)}) %collective-permute-start.17) | collective-permute-done | bytes 262176 | tf_op jit(solution)/shard_map/ppermute | solution.py:324
  184.4 3.4 %collective-permute-done.25 = bf16[128,1024]{1,0:T(8,128)(2,1)S(1)} collective-permute-done((bf16[128,1024]{1,0:T(8,128)(2,1)S(1)}, bf16[128,1024]{1,0:T(8,128)(2,1)S(1)}, u32[]{:S(2)}, u32[]{:S(2)}) %collective-permute-start.25) | collective-permute-done | bytes 262176 | tf_op jit(solution)/shard_map/ppermute | solution.py:324
  190.9 2.5 %collective-permute-done.33 = bf16[128,1024]{1,0:T(8,128)(2,1)S(1)} collective-permute-done((bf16[128,1024]{1,0:T(8,128)(2,1)S(1)}, bf16[128,1024]{1,0:T(8,128)(2,1)S(1)}, u32[]{:S(2)}, u32[]{:S(2)}) %collective-permute-start.33) | collective-permute-done | bytes 262176 | tf_op jit(solution)/shard_map/ppermute | solution.py:324
  196.3 2.2 %collective-permute-done.9 = bf16[128,1024]{1,0:T(8,128)(2,1)S(1)} collective-permute-done((bf16[128,1024]{1,0:T(8,128)(2,1)S(1)}, bf16[128,1024]{1,0:T(8,128)(2,1)S(1)}, u32[]{:S(2)}, u32[]{:S(2)}) %collective-permute-start.9) | collective-permute-done | bytes 262176 | tf_op jit(solution)/shard_map/ppermute | solution.py:324
  200.4 7.8 %collective-permute-done.34.two_ref = bf16[128,1024]{1,0:T(8,128)(2,1)S(1)} collective-permute-done((bf16[128,1024]{1,0:T(8,128)(2,1)S(1)}, bf16[128,1024]{1,0:T(8,128)(2,1)S(1)}, u32[]{:S(2)}, u32[]{:S(2)}) %collective-permute-start.34) | collective-permute-done | bytes 262176 | tf_op jit(solution)/shard_map/ppermute | solution.py:327
  208.9 1.9 finish.4.rest_0_
  211.5 1.9 finish.5.rest_0_
  214.2 1.9 finish.6.rest_0_
  216.8 1.9 finish.7
  (158 shorter events, 44.0 us)
Async XLA Ops:
  77.1 17.0 %collective-permute-start.4 = (s32[8,512]{1,0:T(8,128)S(1)}, s32[8,512]{1,0:T(8,128)S(1)}, u32[]{:S(2)}, u32[]{:S(2)}) collective-permute-start(s32[8,512]{1,0:T(8,128)S(1)} %bitcast.27), channel_id=1, source_target_pairs={{0,1},{1,0},{2,3},{3,2},{4,5},{5,4},{6,7},{7,6}} | collective-permute-start | bytes 49160 | tf_op jit(solution)/shard_map/ppermute | solution.py:324
  77.1 12.7 %collective-permute-start.5 = (s32[8,512]{1,0:T(8,128)S(1)}, s32[8,512]{1,0:T(8,128)S(1)}, u32[]{:S(2)}, u32[]{:S(2)}) collective-permute-start(s32[8,512]{1,0:T(8,128)S(1)} %bitcast.28), channel_id=1, source_target_pairs={{0,2},{1,3},{2,0},{3,1},{4,6},{5,7},{6,4},{7,5}} | collective-permute-start | bytes 49160 | tf_op jit(solution)/shard_map/ppermute | solution.py:324
  78.6 11.8 %collective-permute-start.11 = (bf16[128,1024]{1,0:T(8,128)(2,1)S(1)}, bf16[128,1024]{1,0:T(8,128)(2,1)S(1)}, u32[]{:S(2)}, u32[]{:S(2)}) collective-permute-start(bf16[128,1024]{1,0:T(8,128)(2,1)S(1)} %get-tuple-element.52.one_ref), channel_id=1, source_target_pairs={{0,4},{4,0},{1,5},{5,1},{2,6},{6,2},{3,7},{7,3}} | collective-permute-start | bytes 786440 | tf_op jit(solution)/shard_map/ppermute | solution.py:327
  79.1 17.9 %collective-permute-start.19 = (bf16[128,1024]{1,0:T(8,128)(2,1)S(1)}, bf16[128,1024]{1,0:T(8,128)(2,1)S(1)}, u32[]{:S(2)}, u32[]{:S(2)}) collective-permute-start(bf16[128,1024]{1,0:T(8,128)(2,1)S(1)} %get-tuple-element.59.one_ref), channel_id=1, source_target_pairs={{0,4},{4,0},{1,5},{5,1},{2,6},{6,2},{3,7},{7,3}} | collective-permute-start | bytes 786440 | tf_op jit(solution)/shard_map/ppermute | solution.py:327
  97.0 24.6 %collective-permute-start.12 = (bf16[128,1024]{1,0:T(8,128)(2,1)}, bf16[128,1024]{1,0:T(8,128)(2,1)S(1)}, u32[]{:S(2)}, u32[]{:S(2)}) collective-permute-start(bf16[128,1024]{1,0:T(8,128)(2,1)} %get-tuple-element.54.x0), channel_id=1, source_target_pairs={{0,1},{1,0},{2,3},{3,2},{4,5},{5,4},{6,7},{7,6}} | collective-permute-start | bytes 786440 | tf_op jit(solution)/shard_map/ppermute | solution.py:324
  100.2 38.6 %collective-permute-start.20 = (bf16[128,1024]{1,0:T(8,128)(2,1)}, bf16[128,1024]{1,0:T(8,128)(2,1)S(1)}, u32[]{:S(2)}, u32[]{:S(2)}) collective-permute-start(bf16[128,1024]{1,0:T(8,128)(2,1)} %get-tuple-element.61.x0), channel_id=1, source_target_pairs={{0,1},{1,0},{2,3},{3,2},{4,5},{5,4},{6,7},{7,6}} | collective-permute-start | bytes 786440 | tf_op jit(solution)/shard_map/ppermute | solution.py:324
  103.1 18.6 %collective-permute-start.21 = (bf16[128,1024]{1,0:T(8,128)(2,1)}, bf16[128,1024]{1,0:T(8,128)(2,1)S(1)}, u32[]{:S(2)}, u32[]{:S(2)}) collective-permute-start(bf16[128,1024]{1,0:T(8,128)(2,1)} %get-tuple-element.61.x0), channel_id=1, source_target_pairs={{0,2},{1,3},{2,0},{3,1},{4,6},{5,7},{6,4},{7,5}} | collective-permute-start | bytes 786440 | tf_op jit(solution)/shard_map/ppermute | solution.py:324
  104.9 17.3 %collective-permute-start.29 = (bf16[128,1024]{1,0:T(8,128)(2,1)}, bf16[128,1024]{1,0:T(8,128)(2,1)S(1)}, u32[]{:S(2)}, u32[]{:S(2)}) collective-permute-start(bf16[128,1024]{1,0:T(8,128)(2,1)} %get-tuple-element.68.x0), channel_id=1, source_target_pairs={{0,2},{1,3},{2,0},{3,1},{4,6},{5,7},{6,4},{7,5}} | collective-permute-start | bytes 786440 | tf_op jit(solution)/shard_map/ppermute | solution.py:324
  105.2 17.0 %collective-permute-start.14 = (bf16[128,1024]{1,0:T(8,128)(2,1)S(1)}, bf16[128,1024]{1,0:T(8,128)(2,1)S(1)}, u32[]{:S(2)}, u32[]{:S(2)}) collective-permute-start(bf16[128,1024]{1,0:T(8,128)(2,1)S(1)} %collective-permute-done.13.x2), channel_id=1, source_target_pairs={{0,1},{1,0},{2,3},{3,2},{4,5},{5,4},{6,7},{7,6}} | collective-permute-start | bytes 786440 | tf_op jit(solution)/shard_map/ppermute | solution.py:324
  121.6 34.0 %collective-permute-start.28 = (bf16[128,1024]{1,0:T(8,128)(2,1)}, bf16[128,1024]{1,0:T(8,128)(2,1)S(1)}, u32[]{:S(2)}, u32[]{:S(2)}) collective-permute-start(bf16[128,1024]{1,0:T(8,128)(2,1)} %get-tuple-element.68.x0), channel_id=1, source_target_pairs={{0,1},{1,0},{2,3},{3,2},{4,5},{5,4},{6,7},{7,6}} | collective-permute-start | bytes 786440 | tf_op jit(solution)/shard_map/ppermute | solution.py:324
  121.7 17.5 %collective-permute-start.22 = (bf16[128,1024]{1,0:T(8,128)(2,1)S(1)}, bf16[128,1024]{1,0:T(8,128)(2,1)S(1)}, u32[]{:S(2)}, u32[]{:S(2)}) collective-permute-start(bf16[128,1024]{1,0:T(8,128)(2,1)S(1)} %collective-permute-done.21.x2), channel_id=1, source_target_pairs={{0,1},{1,0},{2,3},{3,2},{4,5},{5,4},{6,7},{7,6}} | collective-permute-start | bytes 786440 | tf_op jit(solution)/shard_map/ppermute | solution.py:324
  122.2 33.6 %collective-permute-start.30 = (bf16[128,1024]{1,0:T(8,128)(2,1)S(1)}, bf16[128,1024]{1,0:T(8,128)(2,1)S(1)}, u32[]{:S(2)}, u32[]{:S(2)}) collective-permute-start(bf16[128,1024]{1,0:T(8,128)(2,1)S(1)} %collective-permute-done.29.x2), channel_id=1, source_target_pairs={{0,1},{1,0},{2,3},{3,2},{4,5},{5,4},{6,7},{7,6}} | collective-permute-start | bytes 786440 | tf_op jit(solution)/shard_map/ppermute | solution.py:324
  122.2 50.0 %collective-permute-start.8 = (bf16[128,1024]{1,0:T(8,128)(2,1)}, bf16[128,1024]{1,0:T(8,128)(2,1)S(1)}, u32[]{:S(2)}, u32[]{:S(2)}) collective-permute-start(bf16[128,1024]{1,0:T(8,128)(2,1)} %get-tuple-element.51), channel_id=1, source_target_pairs={{0,1},{1,0},{2,3},{3,2},{4,5},{5,4},{6,7},{7,6}} | collective-permute-start | bytes 786440 | tf_op jit(solution)/shard_map/ppermute | solution.py:324
  138.8 57.5 %collective-permute-start.7 = (bf16[128,1024]{1,0:T(8,128)(2,1)}, bf16[128,1024]{1,0:T(8,128)(2,1)S(1)}, u32[]{:S(2)}, u32[]{:S(2)}) collective-permute-start(bf16[128,1024]{1,0:T(8,128)(2,1)} %get-tuple-element.49), channel_id=1, source_target_pairs={{0,1},{1,0},{2,3},{3,2},{4,5},{5,4},{6,7},{7,6}} | collective-permute-start | bytes 786440 | tf_op jit(solution)/shard_map/ppermute | solution.py:324
  139.3 33.5 %collective-permute-start.16 = (bf16[128,1024]{1,0:T(8,128)(2,1)}, bf16[128,1024]{1,0:T(8,128)(2,1)S(1)}, u32[]{:S(2)}, u32[]{:S(2)}) collective-permute-start(bf16[128,1024]{1,0:T(8,128)(2,1)} %get-tuple-element.58), channel_id=1, source_target_pairs={{0,1},{1,0},{2,3},{3,2},{4,5},{5,4},{6,7},{7,6}} | collective-permute-start | bytes 786440 | tf_op jit(solution)/shard_map/ppermute | solution.py:324
  155.7 21.6 %collective-permute-start.15 = (bf16[128,1024]{1,0:T(8,128)(2,1)}, bf16[128,1024]{1,0:T(8,128)(2,1)S(1)}, u32[]{:S(2)}, u32[]{:S(2)}) collective-permute-start(bf16[128,1024]{1,0:T(8,128)(2,1)} %get-tuple-element.56), channel_id=1, source_target_pairs={{0,1},{1,0},{2,3},{3,2},{4,5},{5,4},{6,7},{7,6}} | collective-permute-start | bytes 786440 | tf_op jit(solution)/shard_map/ppermute | solution.py:324
  155.8 17.2 %collective-permute-start.24 = (bf16[128,1024]{1,0:T(8,128)(2,1)}, bf16[128,1024]{1,0:T(8,128)(2,1)S(1)}, u32[]{:S(2)}, u32[]{:S(2)}) collective-permute-start(bf16[128,1024]{1,0:T(8,128)(2,1)} %get-tuple-element.65), channel_id=1, source_target_pairs={{0,1},{1,0},{2,3},{3,2},{4,5},{5,4},{6,7},{7,6}} | collective-permute-start | bytes 786440 | tf_op jit(solution)/shard_map/ppermute | solution.py:324
  175.7 12.0 %collective-permute-start.25 = (bf16[128,1024]{1,0:T(8,128)(2,1)S(1)}, bf16[128,1024]{1,0:T(8,128)(2,1)S(1)}, u32[]{:S(2)}, u32[]{:S(2)}) collective-permute-start(bf16[128,1024]{1,0:T(8,128)(2,1)S(1)} %add_convert_fusion.4), channel_id=1, source_target_pairs={{0,2},{1,3},{2,0},{3,1},{4,6},{5,7},{6,4},{7,5}} | collective-permute-start | bytes 786440 | tf_op jit(solution)/shard_map/ppermute | solution.py:324
  177.3 13.3 %collective-permute-start.31 = (bf16[128,1024]{1,0:T(8,128)(2,1)}, bf16[128,1024]{1,0:T(8,128)(2,1)S(1)}, u32[]{:S(2)}, u32[]{:S(2)}) collective-permute-start(bf16[128,1024]{1,0:T(8,128)(2,1)} %get-tuple-element.70), channel_id=1, source_target_pairs={{0,1},{1,0},{2,3},{3,2},{4,5},{5,4},{6,7},{7,6}} | collective-permute-start | bytes 786440 | tf_op jit(solution)/shard_map/ppermute | solution.py:324
  184.0 14.4 %collective-permute-start.9 = (bf16[128,1024]{1,0:T(8,128)(2,1)S(1)}, bf16[128,1024]{1,0:T(8,128)(2,1)S(1)}, u32[]{:S(2)}, u32[]{:S(2)}) collective-permute-start(bf16[128,1024]{1,0:T(8,128)(2,1)S(1)} %add_convert_fusion.10), channel_id=1, source_target_pairs={{0,2},{1,3},{2,0},{3,1},{4,6},{5,7},{6,4},{7,5}} | collective-permute-start | bytes 786440 | tf_op jit(solution)/shard_map/ppermute | solution.py:324
  187.8 25.6 %collective-permute-start.18 = (bf16[128,1024]{1,0:T(8,128)(2,1)S(1)}, bf16[128,1024]{1,0:T(8,128)(2,1)S(1)}, u32[]{:S(2)}, u32[]{:S(2)}) collective-permute-start(bf16[128,1024]{1,0:T(8,128)(2,1)S(1)} %add_convert_fusion.6.one_ref), channel_id=1, source_target_pairs={{0,4},{4,0},{1,5},{5,1},{2,6},{6,2},{3,7},{7,3}} | collective-permute-start | bytes 786440 | tf_op jit(solution)/shard_map/ppermute | solution.py:327
  190.6 20.2 %collective-permute-start.26 = (bf16[128,1024]{1,0:T(8,128)(2,1)S(1)}, bf16[128,1024]{1,0:T(8,128)(2,1)S(1)}, u32[]{:S(2)}, u32[]{:S(2)}) collective-permute-start(bf16[128,1024]{1,0:T(8,128)(2,1)S(1)} %add_convert_fusion.3.one_ref), channel_id=1, source_target_pairs={{0,4},{4,0},{1,5},{5,1},{2,6},{6,2},{3,7},{7,3}} | collective-permute-start | bytes 786440 | tf_op jit(solution)/shard_map/ppermute | solution.py:327
  194.5 13.7 %collective-permute-start.34 = (bf16[128,1024]{1,0:T(8,128)(2,1)S(1)}, bf16[128,1024]{1,0:T(8,128)(2,1)S(1)}, u32[]{:S(2)}, u32[]{:S(2)}) collective-permute-start(bf16[128,1024]{1,0:T(8,128)(2,1)S(1)} %add_convert_fusion.one_ref), channel_id=1, source_target_pairs={{0,4},{4,0},{1,5},{5,1},{2,6},{6,2},{3,7},{7,3}} | collective-permute-start | bytes 786440 | tf_op jit(solution)/shard_map/ppermute | solution.py:327
  198.6 17.5 %collective-permute-start.10 = (bf16[128,1024]{1,0:T(8,128)(2,1)S(1)}, bf16[128,1024]{1,0:T(8,128)(2,1)S(1)}, u32[]{:S(2)}, u32[]{:S(2)}) collective-permute-start(bf16[128,1024]{1,0:T(8,128)(2,1)S(1)} %add_convert_fusion.9.one_ref), channel_id=1, source_target_pairs={{0,4},{4,0},{1,5},{5,1},{2,6},{6,2},{3,7},{7,3}} | collective-permute-start | bytes 786440 | tf_op jit(solution)/shard_map/ppermute | solution.py:327
  (53 other events, 638.5 us)

commit v3 on v2

--- a/solution.py
+++ b/solution.py
@@ -13,6 +13,8 @@
 CHUNKS = 4
 SUB = 128
 BB = 16
+TILE = 512
+WIDE = 1024 + 128
 SLOTS = 8
 AHEAD = 5
 VMEM_LIMIT = 60 * 1024 * 1024
@@ -29,7 +31,7 @@
     return ref[...].astype(F32).reshape(1, -1)
 
 
-def attention_kernel(base_row, has_prev, len_ref, hid_ref, cos_ref, sin_ref, s1_ref, b1_ref, bqkv_ref, wqkv_hbm, wout_hbm, k_hbm, v_hbm, *rest):
+def attention_kernel(form, base_row, has_prev, len_ref, hid_ref, cos_ref, sin_ref, s1_ref, b1_ref, bqkv_ref, wqkv_hbm, wout_hbm, k_hbm, v_hbm, *rest):
     part_ref, ko_hbm, vo_hbm = rest[2 * has_prev:2 * has_prev + 3]
     wqkv_ref, wout_ref, kb_ref, vb_ref, qs_ref, kt_ref, vt_ref, sc_ref, pr_ref, cx_ref, ctx_ref, in_sem, out_sem, w_sem = rest[2 * has_prev + 3:]
     step = pl.program_id(0)
@@ -93,8 +95,8 @@
             q1 = rope(second(4 * h, 4 * h + 2))
             kk = rope(first(4 * h + 1, 4 * h + 3))
             vv = second(4 * h + 1, 4 * h + 3)
-            kt_ref[h * 128:(h + 1) * 128, :] = jnp.transpose(kk)
-            vt_ref[h * 128:(h + 1) * 128, :] = jnp.transpose(vv)
+            kt_ref[h * 128:(h + 1) * 128, :] = jnp.transpose(kk).astype(BF)
+            vt_ref[h * 128:(h + 1) * 128, :] = jnp.transpose(vv).astype(BF)
             for r in range(8):
                 src = q0 if r % 2 == 0 else q1
                 if r // 4 == h:
@@ -106,16 +108,24 @@
     slot = lax.rem(step, SLOTS)
     finish(step, False)
     shift = lax.rem(SUB - j * BB, SUB)
-    kt = pltpu.roll(kt_ref[...], shift, 1)
-    vt = pltpu.roll(vt_ref[...], shift, 1)
+    kt, vt = None, None
+    if form == "A":
+        kt = pltpu.roll(kt_ref[...], shift, 1)
+        vt = pltpu.roll(vt_ref[...], shift, 1)
+
+    def pick(moved, ref, b, pos):
+        if form == "A":
+            return jnp.broadcast_to(moved[:, b:b + 1], (256, 128))
+        return pltpu.roll(ref[...], lax.rem(pos + shift + SUB - b, SUB), 1)
+
     lane8 = lax.broadcasted_iota(jnp.int32, (8, 128), 1)
-    lane256 = lax.broadcasted_iota(jnp.int32, (256, 128), 1)
+    lane256 = lax.broadcasted_iota(jnp.int16, (256, 128), 1)
     row0 = pl.multiple_of(j * BB * 8, BB * 8)
     base = base_row + step * BB
     for b in range(BB):
         pos = len_ref[base + b]
-        k_old = kb_ref[slot, b].reshape(256, 128).astype(F32)
-        k_new = jnp.where(lane256 == pos, kt[:, b:b + 1], k_old).astype(BF)
+        k_old = kb_ref[slot, b].reshape(256, 128)
+        k_new = jnp.where(lane256 == pos.astype(jnp.int16), pick(kt, kt_ref, b, pos), k_old)
         kb_ref[slot, b] = k_new.reshape(4, 64, 128)
         q_one = jnp.concatenate([qs_ref[pl.ds(row0 + h * SUB * 8 + b * 8, 8), :] for h in range(2)], axis=1).astype(BF)
         s_one = jnp.dot(q_one, k_new, preferred_element_type=F32) * 0.125
@@ -125,8 +135,8 @@
     pr_ref[...] = e_all / jnp.sum(e_all, axis=-1, keepdims=True)
     for b in range(BB):
         pos = len_ref[base + b]
-        v_old = vb_ref[slot, b].reshape(256, 128).astype(F32)
-        v_new = jnp.where(lane256 == pos, vt[:, b:b + 1], v_old).astype(BF)
+        v_old = vb_ref[slot, b].reshape(256, 128)
+        v_new = jnp.where(lane256 == pos.astype(jnp.int16), pick(vt, vt_ref, b, pos), v_old)
         vb_ref[slot, b] = v_new.reshape(4, 64, 128)
         p_one = pr_ref[b * 8:(b + 1) * 8, :].astype(BF)
         c_one = lax.dot_general(p_one, v_new, (((1,), (1,)), ((), ())), preferred_element_type=F32)
@@ -189,80 +199,81 @@
         aliases = {len(args): 1, len(args) + 1: 2}
         args += list(prev)
     return pl.pallas_call(
-        functools.partial(attention_kernel, chunk * rows, int(prev is not None)),
+        functools.partial(attention_kernel, 'AB'[chunk >= 2], chunk * rows, int(prev is not None)),
         grid_spec=pltpu.PrefetchScalarGridSpec(
             num_scalar_prefetch=1, grid=(n_step,), in_specs=in_specs,
             out_specs=[pl.BlockSpec((SUB, 1024), lambda i, s: (i // per_sub, 0)), hbm, hbm],
             scratch_shapes=[
                 pltpu.VMEM(wqkv.shape, BF), pltpu.VMEM(wout.shape, BF),
                 pltpu.VMEM((SLOTS, BB, 4, 64, 128), BF), pltpu.VMEM((SLOTS, BB, 4, 64, 128), BF),
-                pltpu.VMEM((2 * SUB * 8, 128), F32), pltpu.VMEM((256, SUB), F32), pltpu.VMEM((256, SUB), F32),
+                pltpu.VMEM((2 * SUB * 8, 128), F32), pltpu.VMEM((256, SUB), BF), pltpu.VMEM((256, SUB), BF),
                 pltpu.VMEM((BB * 8, 128), F32), pltpu.VMEM((BB * 8, 128), F32),
                 pltpu.VMEM((2 * BB * 8, 128), F32), pltpu.VMEM((SUB, 512), BF),
                 pltpu.SemaphoreType.DMA((2, SLOTS)), pltpu.SemaphoreType.DMA((2, SLOTS)), pltpu.SemaphoreType.DMA((2,))]),
         out_shape=[jax.ShapeDtypeStruct((rows, 1024), BF), jax.ShapeDtypeStruct(kt.shape, BF), jax.ShapeDtypeStruct(vt.shape, BF)],
         input_output_aliases=aliases,
-        compiler_params=pltpu.CompilerParams(dimension_semantics=("arbitrary",), vmem_limit_bytes=40 * 1024 * 1024),
+        compiler_params=pltpu.CompilerParams(dimension_semantics=("arbitrary",), vmem_limit_bytes=VMEM_LIMIT),
         cost_estimate=pl.CostEstimate(flops=rows * 20_000_000, bytes_accessed=rows * 262144, transcendentals=0),
         name="attention",
     )(*args)
 
 
-def mid_kernel(hid_ref, one_ref, two_ref, bo_ref, s2_ref, b2_ref, x1_ref, h2_ref):
+def mid_kernel(hid_ref, one_ref, two_ref, bo_ref, s2_ref, b2_ref, wr_ref, ids_ref, x1_ref, h2_ref):
     attn = one_ref[...].astype(F32) + two_ref[...].astype(F32)
     x1 = (hid_ref[...].astype(F32) + attn + wide(bo_ref)).astype(BF)
     x1_ref[...] = x1
-    h2_ref[...] = norm_rows(x1.astype(F32), wide(s2_ref), wide(b2_ref))
-
-
-def middle(chunk, rows, hidden, one, two, b_out, s2, b2):
-    tile = 128
-    off = chunk * rows // tile
+    h2 = norm_rows(x1.astype(F32), wide(s2_ref), wide(b2_ref))
+    h2_ref[:, :1024] = h2
+    rows = h2.shape[0]
+    logit = lax.dot_general(wr_ref[...], h2, (((1,), (1,)), ((), ())), preferred_element_type=F32)
+    eid = lax.broadcasted_iota(jnp.int32, (32, rows), 0)
+    picked = eid == ids_ref[0:1, :]
+    for m in range(1, 8):
+        picked = picked | (eid == ids_ref[m:m + 1, :])
+    logit = jnp.where(picked, logit, -jnp.inf)
+    ex = jnp.exp(logit - jnp.max(logit, axis=0, keepdims=True))
+    prob = ex / jnp.sum(ex, axis=0, keepdims=True)
+    full = jnp.concatenate([prob, jnp.zeros((96, rows), F32)], axis=0)
+    h2_ref[:, 1024:] = jnp.transpose(full).astype(BF)
+
+
+def middle(chunk, rows, hidden, one, two, b_out, s2, b2, wr_t, ids):
     vec = pl.BlockSpec((1024,), lambda i: (0,))
-    blk = pl.BlockSpec((tile, 1024), lambda i: (i, 0))
+    blk = pl.BlockSpec((rows, 1024), lambda i: (0, 0))
     return pl.pallas_call(
-        mid_kernel, grid=(rows // tile,),
-        in_specs=[pl.BlockSpec((tile, 1024), lambda i: (off + i, 0)), blk, blk, vec, vec, vec],
-        out_specs=[blk, blk],
-        out_shape=[jax.ShapeDtypeStruct((rows, 1024), BF)] * 2,
+        mid_kernel, grid=(1,),
+        in_specs=[pl.BlockSpec((rows, 1024), lambda i: (chunk, 0)), blk, blk, vec, vec, vec,
+                  pl.BlockSpec((32, 1024), lambda i: (0, 0)), pl.BlockSpec((8, rows), lambda i: (0, chunk))],
+        out_specs=[blk, pl.BlockSpec((rows, WIDE), lambda i: (0, 0))],
+        out_shape=[jax.ShapeDtypeStruct((rows, 1024), BF), jax.ShapeDtypeStruct((rows, WIDE), BF)],
+        compiler_params=pltpu.CompilerParams(vmem_limit_bytes=VMEM_LIMIT),
         cost_estimate=pl.CostEstimate(flops=rows * 400_000, bytes_accessed=rows * 10240, transcendentals=0),
         name="middle",
-    )(hidden, one, two, b_out, s2, b2)
-
-
-def expert_kernel(rows, first_ref, x0, x1, x2, x3, i0, i1, i2, i3, wr_ref, wg_ref, wu_ref, wd_ref, o0, o1, o2, o3, acc_ref, gate_ref):
+    )(hidden, one, two, b_out, s2, b2, wr_t, ids)
+
+
+def expert_kernel(rows, tile, first_ref, x0, x1, x2, x3, wg_ref, wu_ref, wd_ref, o0, o1, o2, o3, acc_ref, gate_ref, x_ref):
     e = pl.program_id(0)
     n_e = pl.num_programs(0)
-    xs, ids, outs = (x0, x1, x2, x3), (i0, i1, i2, i3), (o0, o1, o2, o3)
-    tile = min(rows, 256)
+    xs, outs = (x0, x1, x2, x3), (o0, o1, o2, o3)
 
     @pl.when(e == 0)
     def _():
         for n in range(4):
-            logit = lax.dot_general(wr_ref[...], xs[n][...], (((1,), (1,)), ((), ())), preferred_element_type=F32)
-            eid = lax.broadcasted_iota(jnp.int32, (32, rows), 0)
-            picked = eid == ids[n][0:1, :]
-            for m in range(1, 8):
-                picked = picked | (eid == ids[n][m:m + 1, :])
-            logit = jnp.where(picked, logit, -jnp.inf)
-            ex = jnp.exp(logit - jnp.max(logit, axis=0, keepdims=True))
-            prob = (ex / jnp.sum(ex, axis=0, keepdims=True)).astype(BF).astype(F32)
-            gate_ref[n * rows:(n + 1) * rows, :] = jnp.transpose(prob)
-
+            gate_ref[n * rows:(n + 1) * rows, :] = xs[n][:, 1024:].astype(F32)
+            x_ref[n * rows:(n + 1) * rows, :] = xs[n][:, :1024]
         acc_ref[...] = jnp.zeros_like(acc_ref)
 
     mine = first_ref[0] + e
-    lane = lax.broadcasted_iota(jnp.int32, (tile, 32), 1)
-    for n in range(4):
-        for t in range(rows // tile):
-            row = n * rows + t * tile
-            x = xs[n][t * tile:(t + 1) * tile, :]
-            gate = jnp.dot(x, wg_ref[0], preferred_element_type=F32)
-            up = jnp.dot(x, wu_ref[0], preferred_element_type=F32)
-            act = (gate * jax.nn.sigmoid(gate) * up).astype(BF)
-            y = jnp.dot(act, wd_ref[0], preferred_element_type=F32)
-            g_one = jnp.sum(jnp.where(lane == mine, gate_ref[row:row + tile, :], 0.0), axis=-1, keepdims=True)
-            acc_ref[row:row + tile, :] += g_one * y
+    lane = lax.broadcasted_iota(jnp.int32, (tile, 128), 1)
+    for row in range(0, 4 * rows, tile):
+        x = x_ref[row:row + tile, :]
+        gate = jnp.dot(x, wg_ref[0], preferred_element_type=F32)
+        up = jnp.dot(x, wu_ref[0], preferred_element_type=F32)
+        act = (gate * jax.nn.sigmoid(gate) * up).astype(BF)
+        y = jnp.dot(act, wd_ref[0], preferred_element_type=F32)
+        g_one = jnp.sum(jnp.where(lane == mine, gate_ref[row:row + tile, :], 0.0), axis=-1, keepdims=True)
+        acc_ref[row:row + tile, :] += g_one * y
 
     @pl.when(e == n_e - 1)
     def _():
@@ -270,46 +281,54 @@
             outs[n][...] = acc_ref[n * rows:(n + 1) * rows, :].astype(BF)
 
 
-def experts(rows, first, xs, ids, wr_t, wg, wu, wd):
+def experts(rows, tile, first, xs, wg, wu, wd):
     n_e = wg.shape[0]
     full = lambda shape: pl.BlockSpec(shape, lambda e, s: (0,) * len(shape), pipeline_mode=pl.Buffered(1))
     wspec = lambda a: pl.BlockSpec((1,) + a.shape[1:], lambda e, s: (e, 0, 0))
     return pl.pallas_call(
-        functools.partial(expert_kernel, rows),
+        functools.partial(expert_kernel, rows, tile),
         grid_spec=pltpu.PrefetchScalarGridSpec(
             num_scalar_prefetch=1, grid=(n_e,),
-            in_specs=[full((rows, 1024))] * 4 + [full((8, rows))] * 4 + [full((32, 1024)), wspec(wg), wspec(wu), wspec(wd)],
+            in_specs=[full((rows, WIDE))] * 4 + [wspec(wg), wspec(wu), wspec(wd)],
             out_specs=[full((rows, 1024))] * 4,
-            scratch_shapes=[pltpu.VMEM((4 * rows, 1024), F32), pltpu.VMEM((4 * rows, 32), F32)]),
+            scratch_shapes=[pltpu.VMEM((4 * rows, 1024), F32), pltpu.VMEM((4 * rows, 128), F32), pltpu.VMEM((4 * rows, 1024), BF)]),
         out_shape=[jax.ShapeDtypeStruct((rows, 1024), BF)] * 4,
         compiler_params=pltpu.CompilerParams(dimension_semantics=("arbitrary",), vmem_limit_bytes=VMEM_LIMIT),
         cost_estimate=pl.CostEstimate(flops=rows * 4 * n_e * 1_600_000, bytes_accessed=14_000_000, transcendentals=0),
         name="experts",
-    )(first, *xs, *ids, wr_t, wg, wu, wd)
-
-
-def finish_kernel(x1_ref, one_ref, two_ref, *rest):
-    moe = one_ref[...].astype(F32) + two_ref[...].astype(F32)
-    rest[-1][...] = (x1_ref[...].astype(F32) + moe).astype(BF)
-
-
-def finish_rows(chunk, n_batch, x1, one, two, prev):
-    rows = x1.shape[0]
+    )(first, *xs, wg, wu, wd)
+
+
+def finish_kernel(count, *refs):
+    rows = refs[0].shape[0]
+    for m in range(count):
+        x1, one, two = refs[3 * m:3 * m + 3]
+        moe = one[...].astype(F32) + two[...].astype(F32)
+        refs[-1][m * rows:(m + 1) * rows, :] = (x1[...].astype(F32) + moe).astype(BF)
+
+
+def finish_rows(first, n_batch, triples, prev):
+    count = len(triples)
+    rows = triples[0][0].shape[0]
     blk = pl.BlockSpec((rows, 1024), lambda i: (0, 0))
     more = [] if prev is None else [prev]
     return pl.pallas_call(
-        finish_kernel, grid=(1,),
-        in_specs=[blk] * 3 + [pl.BlockSpec(memory_space=pl.ANY)] * len(more),
-        out_specs=pl.BlockSpec((rows, 1024), lambda i: (chunk, 0)),
+        functools.partial(finish_kernel, count), grid=(1,),
+        in_specs=[blk] * (3 * count) + [pl.BlockSpec(memory_space=pl.ANY)] * len(more),
+        out_specs=pl.BlockSpec((count * rows, 1024), lambda i: (first // count, 0)),
         out_shape=jax.ShapeDtypeStruct((n_batch, 1024), BF),
-        input_output_aliases={3: 0} if more else {},
-        cost_estimate=pl.CostEstimate(flops=rows * 100_000, bytes_accessed=rows * 8192, transcendentals=0),
+        input_output_aliases={3 * count: 0} if more else {},
+        compiler_params=pltpu.CompilerParams(vmem_limit_bytes=VMEM_LIMIT),
+        cost_estimate=pl.CostEstimate(flops=rows * count * 100_000, bytes_accessed=rows * count * 8192, transcendentals=0),
         name="finish",
-    )(x1, one, two, *more)
-
-
-def add_rows(one, two):
-    return (one.astype(F32) + two.astype(F32)).astype(BF)
+    )(*[a for t in triples for a in t], *more)
+
+
+def add_rows(*parts):
+    total = parts[0].astype(F32)
+    for one in parts[1:]:
+        total = total + one.astype(F32)
+    return total.astype(BF)
 
 
 def solution(mesh):
@@ -330,30 +349,32 @@
         n_batch = hidden.shape[0]
         rows = n_batch // CHUNKS
         kt, vt = (jnp.transpose(c, (0, 2, 3, 1)) for c in (k_cache, v_cache))
-        ids_far = swap_ep(expert_ids.T, 2)
-        ids_near = swap_ep(expert_ids.T, 1)
-        ids = [expert_ids.T, ids_near, ids_far, swap_ep(ids_far, 1)]
         first = (lax.axis_index('ep') * w_gate.shape[0]).astype(jnp.int32).reshape(1)
-        prev, out, x1s, h2s = None, None, [], []
+        prev, out, x1s, h2s, sums = None, None, [], [], []
         for c in range(CHUNKS):
             part, *prev = attention(c, rows, seq_lens, hidden, rope_cos.T, rope_sin.T, ln1_scale, ln1_bias, w_qkv, b_qkv, w_out, kt, vt, prev)
             other = swap_tp(part)
-            x1, h2 = middle(c, rows, hidden, part, other, b_out, ln2_scale, ln2_bias)
+            x1, h2 = middle(c, rows, hidden, part, other, b_out, ln2_scale, ln2_bias, w_router.T, expert_ids.T)
             far = swap_ep(h2, 2)
             near = swap_ep(h2, 1)
             both = swap_ep(far, 1)
             x1s.append(x1)
             h2s.append([h2, near, far, both])
         for c in range(CHUNKS):
-            o = experts(rows, first, h2s[c], [a[:, c * rows:(c + 1) * rows] for a in ids], w_router.T, w_gate, w_up, w_down)
+            o = experts(rows, TILE, first, h2s[c], w_gate, w_up, w_down)
             from_near = swap_ep(o[1], 1)
-            from_pass = swap_ep(o[3], 1)
-            far = add_rows(o[2], from_pass)
-            from_far = swap_ep(far, 2)
-            near = add_rows(o[0], from_near)
-            total = add_rows(near, from_far)
-            other = swap_tp(total)
-            out = finish_rows(c, n_batch, x1s[c], total, other, out)
+            if c < CHUNKS - 1:
+                from_far = swap_ep(o[2], 2)
+                from_cross = swap_ep(o[3], 3)
+                total = add_rows(o[0], from_near, from_far, from_cross)
+            else:
+                from_cross = swap_ep(o[3], 1)
+                far = add_rows(o[2], from_cross)
+                from_far = swap_ep(far, 2)
+                total = add_rows(add_rows(o[0], from_near), from_far)
+            sums.append((x1s[c], total, swap_tp(total)))
+        out = finish_rows(0, n_batch, sums[:-1], None)
+        out = finish_rows(CHUNKS - 1, n_batch, sums[-1:], out)
         return out, *(jnp.transpose(c, (0, 3, 1, 2)) for c in prev)
 
     in_specs = (token_rows, token_vec, token_rows, token_rows, P(), P(), P(None, 'tp'), P('tp'), P('tp', None), P(), cache_spec, cache_spec, P(), P(), P(), token_rows, expert_in, expert_in, expert_down)

time: 219 us -> 221 us (level)
  waiting for transfers between devices: 24.8 us -> 45.5 us
  local copies, waits for them, and re-layouts: 17.4 us -> 5.24 us
  Pallas kernels: 144 us -> 141 us
  starting transfers between devices: 27 us -> 24.6 us
    ppermute x8, waiting for transfers between devices: 11.8 us -> 29.8 us  [swap_tp(): return lax.ppermute(x, 'tp', [(0, 1), (1, 0)])]
    unnamed x84 -> x60, local copies, waits for them, and re-layouts: 15 us -> 5.24 us
    pallas_call x16 -> x14, Pallas kernels: 144 us -> 141 us  [the longest x4 76.1 us: attention(): pl.pallas_call(functools.partial(attention_kernel, 'AB'[chunk >= 2], chun...]
    ppermute x27 -> x24, waiting for transfers between devices: 13 us -> 15.7 us  [swap_ep(): return lax.ppermute(x, 'ep', [(d, d ^ bit) for d in range(n_ep)])]
    slice x4 -> x0, local copies, waits for them, and re-layouts: 2.43 us -> none  [device_step(): a[:, c * rows:(c + 1) * rows]]
    ppermute x27 -> x24, starting transfers between devices: 14.5 us -> 12.5 us  [swap_ep(): return lax.ppermute(x, 'ep', [(d, d ^ bit) for d in range(n_ep)])]
    convert_element_type x8 -> x5, other arithmetic: 4.55 us -> 2.59 us  [add_rows(): return total.astype(BF)]
  transfers between devices with their start and end apart: 35 -> 32, of which waited for: 7 -> 11; matrix products, arithmetic and copies ran while one was open for 3% -> 1% of each run, Pallas kernels for 35% -> 27%
where the time goes in v3:
time: 221 us; the launch traced here: 220 us
  Pallas kernels  141 us (64%)
  waiting for transfers between devices  45.5 us (21%)
  starting transfers between devices  24.6 us (11%)
  local copies, waits for them, and re-layouts  5.24 us (2%)
  other arithmetic  2.59 us (1%)
    pallas_call x4, Pallas kernels, attention(): pl.pallas_call(functools.partial(attention_kernel, 'AB'[chunk >= 2], chun...  76.1 us
    pallas_call x4, Pallas kernels, experts(): pl.pallas_call(functools.partial(expert_kernel, rows, tile), grid_spec=pl...  50 us
    ppermute x8, waiting for transfers between devices, swap_tp(): return lax.ppermute(x, 'tp', [(0, 1), (1, 0)])  29.8 us
    ppermute x24, waiting for transfers between devices, swap_ep(): return lax.ppermute(x, 'ep', [(d, d ^ bit) for d in range(n_ep)])  15.7 us
    ppermute x24, starting transfers between devices, swap_ep(): return lax.ppermute(x, 'ep', [(d, d ^ bit) for d in range(n_ep)])  12.5 us
    ppermute x8, starting transfers between devices, swap_tp(): return lax.ppermute(x, 'tp', [(0, 1), (1, 0)])  12 us
    pallas_call x4, Pallas kernels, middle(): pl.pallas_call(mid_kernel, grid=(1,), in_specs=[pl.BlockSpec((rows, 1024)...  10 us
    unnamed x60, local copies, waits for them, and re-layouts  5.24 us
  transfers between devices with their start and end apart: 32, of which 11 were waited for; matrix products, arithmetic and copies ran while one was open for 1% of the time, Pallas kernels for 27%

profile of v3, /device:TPU:0, one launch (start us, length us, event | category | flops | bytes accessed | tf_op | source)
XLA Modules:
  0.0 219.7 jit_solution(9212776220127167056)
XLA Ops:
  0.6 19.8 %attention.4 = (bf16[128,1024]{1,0:T(8,128)(2,1)}, bf16[512,4,64,128]{3,2,1,0:T(8,128)(2,1)}, bf16[512,4,64,128]{3,2,1,0:T(8,128)(2,1)}) custom-call(s32[512]{0:T(512)} %len_ref.7, bf16[512,1024]{1,0:T(8,128)(2,1)} %hid_ref.15, f32[32,512]{1,0:T(8,128)} %bitcast.19, f32[32,512]{1,0:T(8,128)} %bitcast.23, bf16[1024]{0:T(1024)(128)(2,1)} %s1_ref.7, ...), custom_call_target="tpu_custom_call" | custom-call | flops 2560000000 | bytes 33554432 | tf_op jit(solution)/shard_map/attention/pallas_call | solution.py:201
  20.4 19.8 %attention.5 = (bf16[128,1024]{1,0:T(8,128)(2,1)}, bf16[512,4,64,128]{3,2,1,0:T(8,128)(2,1)}, bf16[512,4,64,128]{3,2,1,0:T(8,128)(2,1)}) custom-call(s32[512]{0:T(512)} %len_ref.7, bf16[512,1024]{1,0:T(8,128)(2,1)} %hid_ref.15, f32[32,512]{1,0:T(8,128)} %bitcast.20, f32[32,512]{1,0:T(8,128)} %bitcast.24, ...), custom_call_target="tpu_custom_call", output_to_operand_aliasing={{1}: (11, {}), {2}: (12, {})} | custom-call | flops 2560000000 | bytes 33554432 | tf_op jit(solution)/shard_map/attention/pallas_call | solution.py:201
  40.2 18.2 %attention.6 = (bf16[128,1024]{1,0:T(8,128)(2,1)}, bf16[512,4,64,128]{3,2,1,0:T(8,128)(2,1)}, bf16[512,4,64,128]{3,2,1,0:T(8,128)(2,1)}) custom-call(s32[512]{0:T(512)} %len_ref.7, bf16[512,1024]{1,0:T(8,128)(2,1)} %hid_ref.15, f32[32,512]{1,0:T(8,128)} %bitcast.21, f32[32,512]{1,0:T(8,128)} %bitcast.25, ...), custom_call_target="tpu_custom_call", output_to_operand_aliasing={{1}: (11, {}), {2}: (12, {})} | custom-call | flops 2560000000 | bytes 33554432 | tf_op jit(solution)/shard_map/attention/pallas_call | solution.py:201
  58.4 18.3 %attention.7 = (bf16[128,1024]{1,0:T(8,128)(2,1)}, bf16[512,4,64,128]{3,2,1,0:T(8,128)(2,1)}, bf16[512,4,64,128]{3,2,1,0:T(8,128)(2,1)}) custom-call(s32[512]{0:T(512)} %len_ref.7, bf16[512,1024]{1,0:T(8,128)(2,1)} %hid_ref.15, f32[32,512]{1,0:T(8,128)} %bitcast.22, f32[32,512]{1,0:T(8,128)} %bitcast.26, ...), custom_call_target="tpu_custom_call", output_to_operand_aliasing={{1}: (11, {}), {2}: (12, {})} | custom-call | flops 2560000000 | bytes 33554432 | tf_op jit(solution)/shard_map/attention/pallas_call | solution.py:201
  76.8 3.4 %collective-permute-start = (bf16[128,1024]{1,0:T(8,128)(2,1)}, bf16[128,1024]{1,0:T(8,128)(2,1)S(1)}, u32[]{:S(2)}, u32[]{:S(2)}) collective-permute-start(bf16[128,1024]{1,0:T(8,128)(2,1)} %get-tuple-element.45.one_ref), channel_id=1, source_target_pairs={{0,4},{4,0},{1,5},{5,1},{2,6},{6,2},{3,7},{7,3}} | collective-permute-start | bytes 786440 | tf_op jit(solution)/shard_map/ppermute | solution.py:346
  80.1 6.5 %collective-permute-done.two_ref = bf16[128,1024]{1,0:T(8,128)(2,1)S(1)} collective-permute-done((bf16[128,1024]{1,0:T(8,128)(2,1)}, bf16[128,1024]{1,0:T(8,128)(2,1)S(1)}, u32[]{:S(2)}, u32[]{:S(2)}) %collective-permute-start) | collective-permute-done | bytes 262176 | tf_op jit(solution)/shard_map/ppermute | solution.py:346
  87.3 2.5 %middle.4 = (bf16[128,1024]{1,0:T(8,128)(2,1)}, bf16[128,1152]{1,0:T(8,128)(2,1)}) custom-call(bf16[512,1024]{1,0:T(8,128)(2,1)} %hid_ref.15, bf16[128,1024]{1,0:T(8,128)(2,1)} %get-tuple-element.45.one_ref, bf16[128,1024]{1,0:T(8,128)(2,1)} %copy-done.12, bf16[1024]{0:T(1024)(128)(2,1)} %bo_ref.7, bf16[1024]{0:T(1024)(128)(2,1)} %s2_ref.7, ...), custom_call_target="tpu_custom_call" | custom-call | flops 51200000 | bytes 1310720 | tf_op jit(solution)/shard_map/middle/pallas_call | solution.py:243
  93.1 5.4 %collective-permute-done.8.two_ref = bf16[128,1024]{1,0:T(8,128)(2,1)S(1)} collective-permute-done((bf16[128,1024]{1,0:T(8,128)(2,1)S(1)}, bf16[128,1024]{1,0:T(8,128)(2,1)S(1)}, u32[]{:S(2)}, u32[]{:S(2)}) %collective-permute-start.8) | collective-permute-done | bytes 262176 | tf_op jit(solution)/shard_map/ppermute | solution.py:346
  99.2 2.5 %middle.5 = (bf16[128,1024]{1,0:T(8,128)(2,1)}, bf16[128,1152]{1,0:T(8,128)(2,1)}) custom-call(bf16[512,1024]{1,0:T(8,128)(2,1)} %hid_ref.15, bf16[128,1024]{1,0:T(8,128)(2,1)} %get-tuple-element.52.one_ref, bf16[128,1024]{1,0:T(8,128)(2,1)} %copy-done.11, bf16[1024]{0:T(1024)(128)(2,1)} %bo_ref.7, bf16[1024]{0:T(1024)(128)(2,1)} %s2_ref.7, ...), custom_call_target="tpu_custom_call" | custom-call | flops 51200000 | bytes 1310720 | tf_op jit(solution)/shard_map/middle/pallas_call | solution.py:243
  104.3 7.1 %collective-permute-done.16.two_ref = bf16[128,1024]{1,0:T(8,128)(2,1)S(1)} collective-permute-done((bf16[128,1024]{1,0:T(8,128)(2,1)S(1)}, bf16[128,1024]{1,0:T(8,128)(2,1)S(1)}, u32[]{:S(2)}, u32[]{:S(2)}) %collective-permute-start.16) | collective-permute-done | bytes 262176 | tf_op jit(solution)/shard_map/ppermute | solution.py:346
  112.2 2.5 %middle.6 = (bf16[128,1024]{1,0:T(8,128)(2,1)}, bf16[128,1152]{1,0:T(8,128)(2,1)}) custom-call(bf16[512,1024]{1,0:T(8,128)(2,1)} %hid_ref.15, bf16[128,1024]{1,0:T(8,128)(2,1)} %get-tuple-element.59.one_ref, bf16[128,1024]{1,0:T(8,128)(2,1)} %copy-done.10, bf16[1024]{0:T(1024)(128)(2,1)} %bo_ref.7, bf16[1024]{0:T(1024)(128)(2,1)} %s2_ref.7, ...), custom_call_target="tpu_custom_call" | custom-call | flops 51200000 | bytes 1310720 | tf_op jit(solution)/shard_map/middle/pallas_call | solution.py:243
  114.7 1.9 collective-permute-done.24.two_ref
  117.3 2.5 %middle.7 = (bf16[128,1024]{1,0:T(8,128)(2,1)}, bf16[128,1152]{1,0:T(8,128)(2,1)}) custom-call(bf16[512,1024]{1,0:T(8,128)(2,1)} %hid_ref.15, bf16[128,1024]{1,0:T(8,128)(2,1)} %get-tuple-element.66.one_ref, bf16[128,1024]{1,0:T(8,128)(2,1)} %copy-done.9, bf16[1024]{0:T(1024)(128)(2,1)} %bo_ref.7, bf16[1024]{0:T(1024)(128)(2,1)} %s2_ref.7, ...), custom_call_target="tpu_custom_call" | custom-call | flops 51200000 | bytes 1310720 | tf_op jit(solution)/shard_map/middle/pallas_call | solution.py:243
  122.6 12.5 %experts.4 = (bf16[128,1024]{1,0:T(8,128)(2,1)}, bf16[128,1024]{1,0:T(8,128)(2,1)}, bf16[128,1024]{1,0:T(8,128)(2,1)}, bf16[128,1024]{1,0:T(8,128)(2,1)}) custom-call(s32[1]{0:T(128)} %bitcast.6.first_ref, bf16[128,1152]{1,0:T(8,128)(2,1)} %get-tuple-element.47.x0, bf16[128,1152]{1,0:T(8,128)(2,1)} %copy-done.22, bf16[128,1152]{1,0:T(8,128)(2,1)} %copy-done.19, ...), custom_call_target="tpu_custom_call" | custom-call | flops 6553600000 | bytes 14000000 | tf_op jit(solution)/shard_map/experts/pallas_call | solution.py:288
  136.5 12.5 %experts.5 = (bf16[128,1024]{1,0:T(8,128)(2,1)}, bf16[128,1024]{1,0:T(8,128)(2,1)}, bf16[128,1024]{1,0:T(8,128)(2,1)}, bf16[128,1024]{1,0:T(8,128)(2,1)}) custom-call(s32[1]{0:T(128)} %bitcast.6.first_ref, bf16[128,1152]{1,0:T(8,128)(2,1)} %get-tuple-element.54.x0, bf16[128,1152]{1,0:T(8,128)(2,1)} %copy-done.23, bf16[128,1152]{1,0:T(8,128)(2,1)} %copy-done.18, ...), custom_call_target="tpu_custom_call" | custom-call | flops 6553600000 | bytes 14000000 | tf_op jit(solution)/shard_map/experts/pallas_call | solution.py:288
  151.1 12.5 %experts.6 = (bf16[128,1024]{1,0:T(8,128)(2,1)}, bf16[128,1024]{1,0:T(8,128)(2,1)}, bf16[128,1024]{1,0:T(8,128)(2,1)}, bf16[128,1024]{1,0:T(8,128)(2,1)}) custom-call(s32[1]{0:T(128)} %bitcast.6.first_ref, bf16[128,1152]{1,0:T(8,128)(2,1)} %get-tuple-element.61.x0, bf16[128,1152]{1,0:T(8,128)(2,1)} %copy-done.21, bf16[128,1152]{1,0:T(8,128)(2,1)} %copy-done.24, ...), custom_call_target="tpu_custom_call" | custom-call | flops 6553600000 | bytes 14000000 | tf_op jit(solution)/shard_map/experts/pallas_call | solution.py:288
  165.2 12.5 %experts.7 = (bf16[128,1024]{1,0:T(8,128)(2,1)}, bf16[128,1024]{1,0:T(8,128)(2,1)}, bf16[128,1024]{1,0:T(8,128)(2,1)}, bf16[128,1024]{1,0:T(8,128)(2,1)}) custom-call(s32[1]{0:T(128)} %bitcast.6.first_ref, bf16[128,1152]{1,0:T(8,128)(2,1)} %get-tuple-element.68.x0, bf16[128,1152]{1,0:T(8,128)(2,1)} %copy-done.25, bf16[128,1152]{1,0:T(8,128)(2,1)} %copy-done.20, ...), custom_call_target="tpu_custom_call" | custom-call | flops 6553600000 | bytes 14000000 | tf_op jit(solution)/shard_map/experts/pallas_call | solution.py:288
  180.9 6.3 %collective-permute-done.21 = bf16[128,1024]{1,0:T(8,128)(2,1)S(1)} collective-permute-done((bf16[128,1024]{1,0:T(8,128)(2,1)}, bf16[128,1024]{1,0:T(8,128)(2,1)S(1)}, u32[]{:S(2)}, u32[]{:S(2)}) %collective-permute-start.21) | collective-permute-done | bytes 262176 | tf_op jit(solution)/shard_map/ppermute | solution.py:343
  189.0 2.1 collective-permute-done.30
  192.6 5.8 %collective-permute-done.29 = bf16[128,1024]{1,0:T(8,128)(2,1)S(1)} collective-permute-done((bf16[128,1024]{1,0:T(8,128)(2,1)}, bf16[128,1024]{1,0:T(8,128)(2,1)S(1)}, u32[]{:S(2)}, u32[]{:S(2)}) %collective-permute-start.29) | collective-permute-done | bytes 262176 | tf_op jit(solution)/shard_map/ppermute | solution.py:343
  204.8 2.8 %collective-permute-done.23.refs_5_ = bf16[128,1024]{1,0:T(8,128)(2,1)S(1)} collective-permute-done((bf16[128,1024]{1,0:T(8,128)(2,1)S(1)}, bf16[128,1024]{1,0:T(8,128)(2,1)S(1)}, u32[]{:S(2)}, u32[]{:S(2)}) %collective-permute-start.23) | collective-permute-done | bytes 262176 | tf_op jit(solution)/shard_map/ppermute | solution.py:346
  207.6 5.6 %collective-permute-done.31.refs_8_ = bf16[128,1024]{1,0:T(8,128)(2,1)S(1)} collective-permute-done((bf16[128,1024]{1,0:T(8,128)(2,1)S(1)}, bf16[128,1024]{1,0:T(8,128)(2,1)S(1)}, u32[]{:S(2)}, u32[]{:S(2)}) %collective-permute-start.31) | collective-permute-done | bytes 262176 | tf_op jit(solution)/shard_map/ppermute | solution.py:346
  213.9 2.7 %finish.2.refs_3_ = bf16[512,1024]{1,0:T(8,128)(2,1)} custom-call(bf16[128,1024]{1,0:T(8,128)(2,1)} %get-tuple-element.53.refs_0_, bf16[128,1024]{1,0:T(8,128)(2,1)} %copy-done, bf16[128,1024]{1,0:T(8,128)(2,1)} %copy-done.14, bf16[128,1024]{1,0:T(8,128)(2,1)} %get-tuple-element.60.refs_3_, bf16[128,1024]{1,0:T(8,128)(2,1)} %copy-done.1, ...), custom_call_target="tpu_custom_call" | custom-call | flops 38400000 | bytes 3145728 | tf_op jit(solution)/shard_map/finish/pallas_call | solution.py:315
  217.8 1.9 finish.3
  (119 shorter events, 31.0 us)
Async XLA Ops:
  93.1 26.7 %collective-permute-start.1 = (bf16[128,1152]{1,0:T(8,128)(2,1)}, bf16[128,1152]{1,0:T(8,128)(2,1)S(1)}, u32[]{:S(2)}, u32[]{:S(2)}) collective-permute-start(bf16[128,1152]{1,0:T(8,128)(2,1)} %get-tuple-element.47.x0), channel_id=1, source_target_pairs={{0,1},{1,0},{2,3},{3,2},{4,5},{5,4},{6,7},{7,6}} | collective-permute-start | bytes 884744 | tf_op jit(solution)/shard_map/ppermute | solution.py:343
  101.7 19.6 %collective-permute-start.10 = (bf16[128,1152]{1,0:T(8,128)(2,1)}, bf16[128,1152]{1,0:T(8,128)(2,1)S(1)}, u32[]{:S(2)}, u32[]{:S(2)}) collective-permute-start(bf16[128,1152]{1,0:T(8,128)(2,1)} %get-tuple-element.54.x0), channel_id=1, source_target_pairs={{0,2},{1,3},{2,0},{3,1},{4,6},{5,7},{6,4},{7,5}} | collective-permute-start | bytes 884744 | tf_op jit(solution)/shard_map/ppermute | solution.py:343
  102.3 19.6 %collective-permute-start.3 = (bf16[128,1152]{1,0:T(8,128)(2,1)S(1)}, bf16[128,1152]{1,0:T(8,128)(2,1)S(1)}, u32[]{:S(2)}, u32[]{:S(2)}) collective-permute-start(bf16[128,1152]{1,0:T(8,128)(2,1)S(1)} %collective-permute-done.2.x2), channel_id=1, source_target_pairs={{0,1},{1,0},{2,3},{3,2},{4,5},{5,4},{6,7},{7,6}} | collective-permute-start | bytes 884744 | tf_op jit(solution)/shard_map/ppermute | solution.py:343
  103.8 12.8 %collective-permute-start.24 = (bf16[128,1024]{1,0:T(8,128)(2,1)S(1)}, bf16[128,1024]{1,0:T(8,128)(2,1)S(1)}, u32[]{:S(2)}, u32[]{:S(2)}) collective-permute-start(bf16[128,1024]{1,0:T(8,128)(2,1)S(1)} %copy-done.5), channel_id=1, source_target_pairs={{0,4},{4,0},{1,5},{5,1},{2,6},{6,2},{3,7},{7,3}} | collective-permute-start | bytes 786440 | tf_op jit(solution)/shard_map/ppermute | solution.py:346
  111.5 23.6 %collective-permute-start.9 = (bf16[128,1152]{1,0:T(8,128)(2,1)}, bf16[128,1152]{1,0:T(8,128)(2,1)S(1)}, u32[]{:S(2)}, u32[]{:S(2)}) collective-permute-start(bf16[128,1152]{1,0:T(8,128)(2,1)} %get-tuple-element.54.x0), channel_id=1, source_target_pairs={{0,1},{1,0},{2,3},{3,2},{4,5},{5,4},{6,7},{7,6}} | collective-permute-start | bytes 884744 | tf_op jit(solution)/shard_map/ppermute | solution.py:343
  116.6 32.4 %collective-permute-start.17 = (bf16[128,1152]{1,0:T(8,128)(2,1)}, bf16[128,1152]{1,0:T(8,128)(2,1)S(1)}, u32[]{:S(2)}, u32[]{:S(2)}) collective-permute-start(bf16[128,1152]{1,0:T(8,128)(2,1)} %get-tuple-element.61.x0), channel_id=1, source_target_pairs={{0,1},{1,0},{2,3},{3,2},{4,5},{5,4},{6,7},{7,6}} | collective-permute-start | bytes 884744 | tf_op jit(solution)/shard_map/ppermute | solution.py:343
  119.8 15.3 %collective-permute-start.18 = (bf16[128,1152]{1,0:T(8,128)(2,1)}, bf16[128,1152]{1,0:T(8,128)(2,1)S(1)}, u32[]{:S(2)}, u32[]{:S(2)}) collective-permute-start(bf16[128,1152]{1,0:T(8,128)(2,1)} %get-tuple-element.61.x0), channel_id=1, source_target_pairs={{0,2},{1,3},{2,0},{3,1},{4,6},{5,7},{6,4},{7,5}} | collective-permute-start | bytes 884744 | tf_op jit(solution)/shard_map/ppermute | solution.py:343
  121.3 14.4 %collective-permute-start.26 = (bf16[128,1152]{1,0:T(8,128)(2,1)}, bf16[128,1152]{1,0:T(8,128)(2,1)S(1)}, u32[]{:S(2)}, u32[]{:S(2)}) collective-permute-start(bf16[128,1152]{1,0:T(8,128)(2,1)} %get-tuple-element.68.x0), channel_id=1, source_target_pairs={{0,2},{1,3},{2,0},{3,1},{4,6},{5,7},{6,4},{7,5}} | collective-permute-start | bytes 884744 | tf_op jit(solution)/shard_map/ppermute | solution.py:343
  121.9 13.8 %collective-permute-start.11 = (bf16[128,1152]{1,0:T(8,128)(2,1)S(1)}, bf16[128,1152]{1,0:T(8,128)(2,1)S(1)}, u32[]{:S(2)}, u32[]{:S(2)}) collective-permute-start(bf16[128,1152]{1,0:T(8,128)(2,1)S(1)} %collective-permute-done.10.x2), channel_id=1, source_target_pairs={{0,1},{1,0},{2,3},{3,2},{4,5},{5,4},{6,7},{7,6}} | collective-permute-start | bytes 884744 | tf_op jit(solution)/shard_map/ppermute | solution.py:343
  135.1 28.5 %collective-permute-start.25 = (bf16[128,1152]{1,0:T(8,128)(2,1)}, bf16[128,1152]{1,0:T(8,128)(2,1)S(1)}, u32[]{:S(2)}, u32[]{:S(2)}) collective-permute-start(bf16[128,1152]{1,0:T(8,128)(2,1)} %get-tuple-element.68.x0), channel_id=1, source_target_pairs={{0,1},{1,0},{2,3},{3,2},{4,5},{5,4},{6,7},{7,6}} | collective-permute-start | bytes 884744 | tf_op jit(solution)/shard_map/ppermute | solution.py:343
  135.2 15.3 %collective-permute-start.19 = (bf16[128,1152]{1,0:T(8,128)(2,1)S(1)}, bf16[128,1152]{1,0:T(8,128)(2,1)}, u32[]{:S(2)}, u32[]{:S(2)}) collective-permute-start(bf16[128,1152]{1,0:T(8,128)(2,1)S(1)} %collective-permute-done.18.x2), channel_id=1, source_target_pairs={{0,1},{1,0},{2,3},{3,2},{4,5},{5,4},{6,7},{7,6}} | collective-permute-start | bytes 884744 | tf_op jit(solution)/shard_map/ppermute | solution.py:343
  135.7 28.0 %collective-permute-start.27 = (bf16[128,1152]{1,0:T(8,128)(2,1)S(1)}, bf16[128,1152]{1,0:T(8,128)(2,1)S(1)}, u32[]{:S(2)}, u32[]{:S(2)}) collective-permute-start(bf16[128,1152]{1,0:T(8,128)(2,1)S(1)} %collective-permute-done.26.x2), channel_id=1, source_target_pairs={{0,1},{1,0},{2,3},{3,2},{4,5},{5,4},{6,7},{7,6}} | collective-permute-start | bytes 884744 | tf_op jit(solution)/shard_map/ppermute | solution.py:343
  135.7 44.4 %collective-permute-start.5 = (bf16[128,1024]{1,0:T(8,128)(2,1)}, bf16[128,1024]{1,0:T(8,128)(2,1)S(1)}, u32[]{:S(2)}, u32[]{:S(2)}) collective-permute-start(bf16[128,1024]{1,0:T(8,128)(2,1)} %get-tuple-element.51), channel_id=1, source_target_pairs={{0,1},{1,0},{2,3},{3,2},{4,5},{5,4},{6,7},{7,6}} | collective-permute-start | bytes 786440 | tf_op jit(solution)/shard_map/ppermute | solution.py:343
  149.0 28.7 %collective-permute-start.14 = (bf16[128,1024]{1,0:T(8,128)(2,1)}, bf16[128,1024]{1,0:T(8,128)(2,1)S(1)}, u32[]{:S(2)}, u32[]{:S(2)}) collective-permute-start(bf16[128,1024]{1,0:T(8,128)(2,1)} %get-tuple-element.58), channel_id=1, source_target_pairs={{0,3},{1,2},{2,1},{3,0},{4,7},{5,6},{6,5},{7,4}} | collective-permute-start | bytes 786440 | tf_op jit(solution)/shard_map/ppermute | solution.py:343
  150.5 27.9 %collective-permute-start.13 = (bf16[128,1024]{1,0:T(8,128)(2,1)}, bf16[128,1024]{1,0:T(8,128)(2,1)S(1)}, u32[]{:S(2)}, u32[]{:S(2)}) collective-permute-start(bf16[128,1024]{1,0:T(8,128)(2,1)} %get-tuple-element.57), channel_id=1, source_target_pairs={{0,2},{1,3},{2,0},{3,1},{4,6},{5,7},{6,4},{7,5}} | collective-permute-start | bytes 786440 | tf_op jit(solution)/shard_map/ppermute | solution.py:343
  163.6 14.9 %collective-permute-start.12 = (bf16[128,1024]{1,0:T(8,128)(2,1)}, bf16[128,1024]{1,0:T(8,128)(2,1)S(1)}, u32[]{:S(2)}, u32[]{:S(2)}) collective-permute-start(bf16[128,1024]{1,0:T(8,128)(2,1)} %get-tuple-element.56), channel_id=1, source_target_pairs={{0,1},{1,0},{2,3},{3,2},{4,5},{5,4},{6,7},{7,6}} | collective-permute-start | bytes 786440 | tf_op jit(solution)/shard_map/ppermute | solution.py:343
  163.7 17.1 %collective-permute-start.22 = (bf16[128,1024]{1,0:T(8,128)(2,1)}, bf16[128,1024]{1,0:T(8,128)(2,1)S(1)}, u32[]{:S(2)}, u32[]{:S(2)}) collective-permute-start(bf16[128,1024]{1,0:T(8,128)(2,1)} %get-tuple-element.65), channel_id=1, source_target_pairs={{0,3},{1,2},{2,1},{3,0},{4,7},{5,6},{6,5},{7,4}} | collective-permute-start | bytes 786440 | tf_op jit(solution)/shard_map/ppermute | solution.py:343
  178.6 12.5 %collective-permute-start.30 = (bf16[128,1024]{1,0:T(8,128)(2,1)}, bf16[128,1024]{1,0:T(8,128)(2,1)S(1)}, u32[]{:S(2)}, u32[]{:S(2)}) collective-permute-start(bf16[128,1024]{1,0:T(8,128)(2,1)} %get-tuple-element.72), channel_id=1, source_target_pairs={{0,3},{1,2},{2,1},{3,0},{4,7},{5,6},{6,5},{7,4}} | collective-permute-start | bytes 786440 | tf_op jit(solution)/shard_map/ppermute | solution.py:343
  180.1 18.3 %collective-permute-start.29 = (bf16[128,1024]{1,0:T(8,128)(2,1)}, bf16[128,1024]{1,0:T(8,128)(2,1)S(1)}, u32[]{:S(2)}, u32[]{:S(2)}) collective-permute-start(bf16[128,1024]{1,0:T(8,128)(2,1)} %get-tuple-element.71), channel_id=1, source_target_pairs={{0,2},{1,3},{2,0},{3,1},{4,6},{5,7},{6,4},{7,5}} | collective-permute-start | bytes 786440 | tf_op jit(solution)/shard_map/ppermute | solution.py:343
  180.8 19.1 %collective-permute-start.28 = (bf16[128,1024]{1,0:T(8,128)(2,1)}, bf16[128,1024]{1,0:T(8,128)(2,1)S(1)}, u32[]{:S(2)}, u32[]{:S(2)}) collective-permute-start(bf16[128,1024]{1,0:T(8,128)(2,1)} %get-tuple-element.70), channel_id=1, source_target_pairs={{0,1},{1,0},{2,3},{3,2},{4,5},{5,4},{6,7},{7,6}} | collective-permute-start | bytes 786440 | tf_op jit(solution)/shard_map/ppermute | solution.py:343
  187.1 14.4 %collective-permute-start.4 = (bf16[128,1024]{1,0:T(8,128)(2,1)S(1)}, bf16[128,1024]{1,0:T(8,128)(2,1)S(1)}, u32[]{:S(2)}, u32[]{:S(2)}) collective-permute-start(bf16[128,1024]{1,0:T(8,128)(2,1)S(1)} %copy-done.29), channel_id=1, source_target_pairs={{0,1},{1,0},{2,3},{3,2},{4,5},{5,4},{6,7},{7,6}} | collective-permute-start | bytes 786440 | tf_op jit(solution)/shard_map/ppermute | solution.py:343
  187.2 15.9 %collective-permute-start.6 = (bf16[128,1024]{1,0:T(8,128)(2,1)S(1)}, bf16[128,1024]{1,0:T(8,128)(2,1)S(1)}, u32[]{:S(2)}, u32[]{:S(2)}) collective-permute-start(bf16[128,1024]{1,0:T(8,128)(2,1)S(1)} %add_convert_fusion.4), channel_id=1, source_target_pairs={{0,2},{1,3},{2,0},{3,1},{4,6},{5,7},{6,4},{7,5}} | collective-permute-start | bytes 786440 | tf_op jit(solution)/shard_map/ppermute | solution.py:343
  191.0 13.7 %collective-permute-start.15 = (bf16[128,1024]{1,0:T(8,128)(2,1)S(1)}, bf16[128,1024]{1,0:T(8,128)(2,1)S(1)}, u32[]{:S(2)}, u32[]{:S(2)}) collective-permute-start(bf16[128,1024]{1,0:T(8,128)(2,1)S(1)} %add_convert_fusion.2.refs_1_), channel_id=1, source_target_pairs={{0,4},{4,0},{1,5},{5,1},{2,6},{6,2},{3,7},{7,3}} | collective-permute-start | bytes 786440 | tf_op jit(solution)/shard_map/ppermute | solution.py:346
  203.2 13.9 %collective-permute-start.7 = (bf16[128,1024]{1,0:T(8,128)(2,1)S(1)}, bf16[128,1024]{1,0:T(8,128)(2,1)S(1)}, u32[]{:S(2)}, u32[]{:S(2)}) collective-permute-start(bf16[128,1024]{1,0:T(8,128)(2,1)S(1)} %add_convert_fusion.3.refs_1_), channel_id=1, source_target_pairs={{0,4},{4,0},{1,5},{5,1},{2,6},{6,2},{3,7},{7,3}} | collective-permute-start | bytes 786440 | tf_op jit(solution)/shard_map/ppermute | solution.py:346
  (38 other events, 586.6 us)

commit v4 on v2

v4 whole, which is shorter than its diff:
```python
import functools

import jax
import jax.numpy as jnp
from jax import lax
from jax.experimental import pallas as pl
from jax.experimental.pallas import tpu as pltpu
from jax.sharding import PartitionSpec as P

EPS = 1e-5
BF = jnp.bfloat16
F32 = jnp.float32
CHUNKS = 4
SUB = 128
BB = 16
WIDE = 1024 + 128
SLOTS = 8
AHEAD = 5
VMEM_LIMIT = 60 * 1024 * 1024


def norm_rows(x, scale, bias):
    mean = jnp.mean(x, axis=-1, keepdims=True)
    cen = x - mean
    var = jnp.mean(cen * cen, axis=-1, keepdims=True)
    return (cen * lax.rsqrt(var + EPS) * scale + bias).astype(BF)


def wide(ref):
    return ref[...].astype(F32).reshape(1, -1)


def attention_kernel(base_row, has_prev, len_ref, hid_ref, cos_ref, sin_ref, s1_ref, b1_ref, bqkv_ref, wqkv_hbm, wout_hbm, k_hbm, v_hbm, *rest):
    part_ref, ko_hbm, vo_hbm = rest[2 * has_prev:2 * has_prev + 3]
    wqkv_ref, wout_ref, kb_ref, vb_ref, qs_ref, kt_ref, vt_ref, sc_ref, pr_ref, cx_ref, ctx_ref, in_sem, out_sem, w_sem = rest[2 * has_prev + 3:]
    step = pl.program_id(0)
    n_step = pl.num_programs(0)
    per_sub = SUB // BB
    j = lax.rem(step, per_sub)
    lane = lax.broadcasted_iota(jnp.int32, (SUB, 128), 1)
    low = lane < 64

    def moves(s, out):
        slot = lax.rem(s, SLOTS)
        src = pl.ds(base_row + s * BB, BB)
        pairs = ((k_hbm, kb_ref, ko_hbm, 0), (v_hbm, vb_ref, vo_hbm, 1))
        if out:
            return [(pltpu.make_async_copy(buf.at[slot], dst.at[src], out_sem.at[t, slot]), t) for _, buf, dst, t in pairs]
        return [(pltpu.make_async_copy(hbm.at[src], buf.at[slot], in_sem.at[t, slot]), t) for hbm, buf, _, t in pairs]

    def begin(s, out):
        for copy, t in moves(s, out):
            copy.start(priority=t)

    def finish(s, out):
        for copy, _ in moves(s, out):
            copy.wait()

    load_qkv = pltpu.make_async_copy(wqkv_hbm, wqkv_ref, w_sem.at[0])
    load_out = pltpu.make_async_copy(wout_hbm, wout_ref, w_sem.at[1])

    @pl.when(step == 0)
    def _():
        load_qkv.start()
        for s in range(AHEAD):
            begin(s, False)
        load_out.start()
        load_qkv.wait()

    @pl.when(j == 0)
    def _():
        normed = norm_rows(hid_ref[...].astype(F32), wide(s1_ref), wide(b1_ref))
        qkv = jnp.dot(normed, wqkv_ref[...], preferred_element_type=F32) + wide(bqkv_ref)
        qkv = qkv.astype(BF).astype(F32)
        col = [qkv[:, m * 128:(m + 1) * 128] for m in range(8)]
        rol = [pltpu.roll(c, 64, 1) for c in col]

        def first(a, b):
            return jnp.where(low, col[a], rol[b])

        def second(a, b):
            return jnp.where(low, rol[a], col[b])

        cos_t, sin_t = cos_ref[...], sin_ref[...]
        cos = jnp.transpose(jnp.concatenate([cos_t] * 4, axis=0))
        sin = jnp.transpose(jnp.concatenate([-sin_t, sin_t] * 2, axis=0))

        def rope(x):
            other = jnp.where(lane % 64 < 32, pltpu.roll(x, 96, 1), pltpu.roll(x, 32, 1))
            return (x * cos + other * sin).astype(BF).astype(F32)

        for h in range(2):
            q0 = rope(first(4 * h, 4 * h + 2))
            q1 = rope(second(4 * h, 4 * h + 2))
            kk = rope(first(4 * h + 1, 4 * h + 3))
            vv = second(4 * h + 1, 4 * h + 3)
            kt_ref[h * 128:(h + 1) * 128, :] = jnp.transpose(kk)
            vt_ref[h * 128:(h + 1) * 128, :] = jnp.transpose(vv)
            for r in range(8):
                src = q0 if r % 2 == 0 else q1
                if r // 4 == h:
                    src = jnp.where(low if (r // 2) % 2 == 0 else ~low, src, 0.0)
                else:
                    src = jnp.zeros_like(src)
                qs_ref[pl.ds(h * SUB * 8 + r, SUB, stride=8), :] = src

    slot = lax.rem(step, SLOTS)
    finish(step, False)
    shift = lax.rem(SUB - j * BB, SUB)
    kt = pltpu.roll(kt_ref[...], shift, 1)
    vt = pltpu.roll(vt_ref[...], shift, 1)
    lane8 = lax.broadcasted_iota(jnp.int32, (8, 128), 1)
    lane256 = lax.broadcasted_iota(jnp.int32, (256, 128), 1)
    row0 = pl.multiple_of(j * BB * 8, BB * 8)
    base = base_row + step * BB

    def placed(buf, cols, b):
        pos = len_ref[base + b]
        old = buf[slot, b].reshape(256, 128).astype(F32)
        new = jnp.where(lane256 == pos, cols[:, b:b + 1], old).astype(BF)
        buf[slot, b] = new.reshape(4, 64, 128)
        return pos, new

    for b in range(BB):
        pos, k_new = placed(kb_ref, kt, b)
        q_one = jnp.concatenate([qs_ref[pl.ds(row0 + h * SUB * 8 + b * 8, 8), :] for h in range(2)], axis=1).astype(BF)
        s_one = jnp.dot(q_one, k_new, preferred_element_type=F32) * 0.125
        sc_ref[b * 8:(b + 1) * 8, :] = jnp.where(lane8 <= pos, s_one, -jnp.inf)
    s_all = sc_ref[...]
    e_all = jnp.exp(s_all - jnp.max(s_all, axis=-1, keepdims=True))
    pr_ref[...] = e_all / jnp.sum(e_all, axis=-1, keepdims=True)
    for b in range(BB):
        _, v_new = placed(vb_ref, vt, b)
        p_one = pr_ref[b * 8:(b + 1) * 8, :].astype(BF)
        c_one = lax.dot_general(p_one, v_new, (((1,), (1,)), ((), ())), preferred_element_type=F32)
        cx_ref[b * 8:(b + 1) * 8, :] = c_one[:, :128]
        cx_ref[BB * 8 + b * 8:BB * 8 + (b + 1) * 8, :] = c_one[:, 128:]
    low_b = lax.broadcasted_iota(jnp.int32, (BB, 128), 1) < 64
    for h in range(2):
        for g in range(2):
            r = 4 * h + 2 * g
            one = cx_ref[pl.ds(h * BB * 8 + r, BB, stride=8), :]
            two = cx_ref[pl.ds(h * BB * 8 + r + 1, BB, stride=8), :]
            if g == 0:
                both = jnp.where(low_b, one, pltpu.roll(two, 64, 1))
            else:
                both = jnp.where(low_b, pltpu.roll(one, 64, 1), two)
            ctx_ref[pl.ds(pl.multiple_of(j * BB, BB), BB), (2 * h + g) * 128:(2 * h + g + 1) * 128] = both.astype(BF)

    begin(step, True)

    @pl.when(step + AHEAD < n_step)
    def _():
        @pl.when(step + AHEAD >= SLOTS)
        def _():
            finish(step + AHEAD - SLOTS, True)
        begin(step + AHEAD, False)

    @pl.when(step == per_sub - 1)
    def _():
        load_out.wait()

    @pl.when(j == per_sub - 1)
    def _():
        part_ref[...] = jnp.dot(ctx_ref[...], wout_ref[...], preferred_element_type=F32).astype(BF)

    @pl.when(step == n_step - 1)
    def _():
        for back in range(SLOTS - 1, -1, -1):
            @pl.when(step >= back)
            def _():
                finish(step - back, True)


def attention(chunk, rows, lens, hidden, cos_t, sin_t, s1, b1, wqkv, bqkv, wout, kt, vt, prev):
    per_sub = SUB // BB
    n_step = rows // BB
    first = chunk * rows // SUB
    vec = pl.BlockSpec((1024,), lambda i, s: (0,))
    hbm = pl.BlockSpec(memory_space=pl.ANY)
    in_specs = [
        pl.BlockSpec((SUB, 1024), lambda i, s: (first + i // per_sub, 0)),
        pl.BlockSpec((32, SUB), lambda i, s: (0, first + i // per_sub)),
        pl.BlockSpec((32, SUB), lambda i, s: (0, first + i // per_sub)),
        vec, vec, vec, hbm, hbm, hbm, hbm,
    ]
    args = [lens, hidden, cos_t, sin_t, s1, b1, bqkv, wqkv, wout, kt, vt]
    aliases = {}
    if prev is not None:
        in_specs += [hbm, hbm]
        aliases = {len(args): 1, len(args) + 1: 2}
        args += list(prev)
    return pl.pallas_call(
        functools.partial(attention_kernel, chunk * rows, int(prev is not None)),
        grid_spec=pltpu.PrefetchScalarGridSpec(
            num_scalar_prefetch=1, grid=(n_step,), in_specs=in_specs,
            out_specs=[pl.BlockSpec((SUB, 1024), lambda i, s: (i // per_sub, 0)), hbm, hbm],
            scratch_shapes=[
                pltpu.VMEM(wqkv.shape, BF), pltpu.VMEM(wout.shape, BF),
                pltpu.VMEM((SLOTS, BB, 4, 64, 128), BF), pltpu.VMEM((SLOTS, BB, 4, 64, 128), BF),
                pltpu.VMEM((2 * SUB * 8, 128), F32), pltpu.VMEM((256, SUB), F32), pltpu.VMEM((256, SUB), F32),
                pltpu.VMEM((BB * 8, 128), F32), pltpu.VMEM((BB * 8, 128), F32),
                pltpu.VMEM((2 * BB * 8, 128), F32), pltpu.VMEM((SUB, 512), BF),
                pltpu.SemaphoreType.DMA((2, SLOTS)), pltpu.SemaphoreType.DMA((2, SLOTS)), pltpu.SemaphoreType.DMA((2,))]),
        out_shape=[jax.ShapeDtypeStruct((rows, 1024), BF), jax.ShapeDtypeStruct(kt.shape, BF), jax.ShapeDtypeStruct(vt.shape, BF)],
        input_output_aliases=aliases,
        compiler_params=pltpu.CompilerParams(dimension_semantics=("arbitrary",), vmem_limit_bytes=VMEM_LIMIT),
        cost_estimate=pl.CostEstimate(flops=rows * 20_000_000, bytes_accessed=rows * 262144, transcendentals=0),
        name="attention",
    )(*args)


PART, NEAR, FAR, PASS, BACK1, BACK3, BACKX, BACKY = range(8)


def moe_kernel(part_ref, hid_ref, bo_ref, s2_ref, b2_ref, wr_ref, ids_ref, wg_hbm, wu_hbm, wd_hbm, out_ref,
               other, x1, xb, wg, wu, wd, acc, ob, rb, fb, rf, tb, ry, w_sem, send, recv):
    me_ep, me_tp = lax.axis_index("ep"), lax.axis_index("tp")
    near = me_ep + 1 - 2 * lax.rem(me_ep, 2)
    far = lax.rem(me_ep + 2, 4)
    peer = 1 - me_tp
    barrier = pltpu.get_barrier_semaphore()
    for dev in ({"ep": near}, {"ep": far}, {"tp": peer}):
        pl.semaphore_signal(barrier, inc=1, device_id=dev, device_id_type=pl.DeviceIdType.MESH)
    loads = [pltpu.make_async_copy(h, v, w_sem.at[m]) for m, (h, v) in enumerate(((wg_hbm, wg), (wu_hbm, wu), (wd_hbm, wd)))]
    for one in loads:
        one.start()
    pl.semaphore_wait(barrier, 3)
    n_c = xb.shape[1]
    rows = xb.shape[2]
    n_e = wg.shape[0]

    def move(kind, c):
        span = pl.ds(c * rows, rows)
        src, dst, dev = {
            PART: (part_ref.at[span], other.at[span], {"tp": peer}),
            NEAR: (xb.at[0, c], xb.at[1, c], {"ep": near}),
            FAR: (xb.at[0, c], xb.at[2, c], {"ep": far}),
            PASS: (xb.at[2, c], xb.at[3, c], {"ep": near}),
            BACK1: (ob.at[1, c], rb.at[0, c], {"ep": near}),
            BACK3: (ob.at[3, c], rb.at[1, c], {"ep": near}),
            BACKX: (fb.at[c], rf.at[c], {"ep": far}),
            BACKY: (tb.at[c], ry.at[c], {"tp": peer}),
        }[kind]
        return pltpu.make_async_remote_copy(src_ref=src, dst_ref=dst, send_sem=send.at[kind, c], recv_sem=recv.at[kind, c], device_id=dev, device_id_type=pl.DeviceIdType.MESH)

    def go(kind, c):
        move(kind, c).start()

    def arrive(kind, c):
        move(kind, c).wait_recv()

    def mid(c):
        arrive(PART, c)
        span = slice(c * rows, (c + 1) * rows)
        attn = part_ref[span, :].astype(F32) + other[span, :].astype(F32)
        row = (hid_ref[span, :].astype(F32) + attn + wide(bo_ref)).astype(BF)
        x1[span, :] = row
        h2 = norm_rows(row.astype(F32), wide(s2_ref), wide(b2_ref))
        xb[0, c, :, :1024] = h2
        logit = lax.dot_general(wr_ref[...], h2, (((1,), (1,)), ((), ())), preferred_element_type=F32)
        eid = lax.broadcasted_iota(jnp.int32, (32, rows), 0)
        picked = eid == ids_ref[0:1, span]
        for m in range(1, 8):
            picked = picked | (eid == ids_ref[m:m + 1, span])
        logit = jnp.where(picked, logit, -jnp.inf)
        ex = jnp.exp(logit - jnp.max(logit, axis=0, keepdims=True))
        prob = ex / jnp.sum(ex, axis=0, keepdims=True)
        full = jnp.concatenate([prob, jnp.zeros((96, rows), F32)], axis=0)
        xb[0, c, :, 1024:] = jnp.transpose(full).astype(BF)
        go(FAR, c)
        go(NEAR, c)

    def hand_on(c):
        arrive(FAR, c)
        go(PASS, c)

    def ready(c):
        arrive(NEAR, c)
        arrive(PASS, c)

    def give_back(c):
        go(BACK3, c)
        go(BACK1, c)

    def far_sum(c):
        arrive(BACK3, c)
        fb[c] = (ob[2, c].astype(F32) + rb[1, c].astype(F32)).astype(BF)
        go(BACKX, c)

    def all_sum(c):
        arrive(BACK1, c)
        arrive(BACKX, c)
        tb[c] = (ob[0, c].astype(F32) + rb[0, c].astype(F32) + rf[c].astype(F32)).astype(BF)
        go(BACKY, c)

    def last_sum(c):
        arrive(BACKY, c)
        span = slice(c * rows, (c + 1) * rows)
        moe = tb[c].astype(F32) + ry[c].astype(F32)
        out_ref[span, :] = (x1[span, :].astype(F32) + moe).astype(BF)

    for c in range(n_c):
        go(PART, c)
    mid(0)
    mid(1)
    hand_on(0)
    for one in loads:
        one.wait()
    table = {
        0: [(ready, 0)], 1: [(mid, 2)], 3: [(hand_on, 1)],
        4: [(give_back, 0), (ready, 1)], 5: [(mid, 3)], 6: [(far_sum, 0)], 7: [(hand_on, 2)],
        8: [(give_back, 1), (ready, 2)], 10: [(far_sum, 1)], 11: [(hand_on, 3)],
        12: [(give_back, 2), (ready, 3)], 13: [(all_sum, 0)], 14: [(far_sum, 2)],
    }
    parts = 4
    lane = lax.broadcasted_iota(jnp.int32, (4 * rows, 128), 1)

    def step(s, carry):
        for k, acts in table.items():
            @pl.when(s == k)
            def _():
                for act, c in acts:
                    act(c)
        c, q = s // parts, lax.rem(s, parts)

        @pl.when(q == 0)
        def _():
            acc[...] = jnp.zeros_like(acc)

        x = jnp.concatenate([xb[n, c, :, :1024] for n in range(4)], axis=0)
        gates = jnp.concatenate([xb[n, c, :, 1024:] for n in range(4)], axis=0).astype(F32)
        total = None
        for m in range(n_e // parts):
            e = q * (n_e // parts) + m
            gate = jnp.dot(x, wg[e], preferred_element_type=F32)
            up = jnp.dot(x, wu[e], preferred_element_type=F32)
            act = (gate * jax.nn.sigmoid(gate) * up).astype(BF)
            y = jnp.dot(act, wd[e], preferred_element_type=F32)
            g_one = jnp.sum(jnp.where(lane == me_ep * n_e + e, gates, 0.0), axis=-1, keepdims=True)
            acc[...] += g_one * y

        @pl.when(q == parts - 1)
        def _():
            for n in range(4):
                ob[n, c] = acc[n * rows:(n + 1) * rows, :].astype(BF)
        return carry

    lax.fori_loop(0, n_c * parts, step, 0)
    give_back(3)
    all_sum(1)
    far_sum(3)
    all_sum(2)
    last_sum(0)
    last_sum(1)
    all_sum(3)
    last_sum(2)
    last_sum(3)
    for kind in range(8):
        for c in range(n_c):
            move(kind, c).wait_send()


def moe_layer(hidden, part, b_out, s2, b2, wr_t, ids, wg, wu, wd):
    n_batch = hidden.shape[0]
    rows = n_batch // CHUNKS
    vmem = pl.BlockSpec(memory_space=pltpu.VMEM)
    hbm = pl.BlockSpec(memory_space=pl.ANY)
    blocks = lambda *lead: pltpu.VMEM(lead + (CHUNKS, rows, 1024), BF)
    return pl.pallas_call(
        moe_kernel,
        in_specs=[vmem] * 7 + [hbm] * 3, out_specs=vmem,
        out_shape=jax.ShapeDtypeStruct((n_batch, 1024), BF),
        scratch_shapes=[
            pltpu.VMEM((n_batch, 1024), BF), pltpu.VMEM((n_batch, 1024), BF), pltpu.VMEM((4, CHUNKS, rows, WIDE), BF),
            pltpu.VMEM(wg.shape, BF), pltpu.VMEM(wu.shape, BF), pltpu.VMEM(wd.shape, BF),
            pltpu.VMEM((4 * rows, 1024), F32), blocks(4), blocks(2), blocks(), blocks(), blocks(), blocks(),
            pltpu.SemaphoreType.DMA((3,)), pltpu.SemaphoreType.DMA((8, CHUNKS)), pltpu.SemaphoreType.DMA((8, CHUNKS))],
        compiler_params=pltpu.CompilerParams(collective_id=0, has_side_effects=True, vmem_limit_bytes=VMEM_LIMIT),
        cost_estimate=pl.CostEstimate(flops=26_000_000_000, bytes_accessed=14_000_000, transcendentals=0),
        name="moe",
    )(part, hidden, b_out, s2, b2, wr_t, ids, wg, wu, wd)


def solution(mesh):
    token_rows = P(('dp', 'ep'), None)
    token_vec = P(('dp', 'ep'))
    cache_spec = P(('dp', 'ep'), None, 'tp', None)
    expert_in = P('ep', None, 'tp')
    expert_down = P('ep', 'tp', None)

    def device_step(hidden, seq_lens, rope_cos, rope_sin, ln1_scale, ln1_bias, w_qkv, b_qkv, w_out, b_out, k_cache, v_cache, ln2_scale, ln2_bias, w_router, expert_ids, w_gate, w_up, w_down):
        n_batch = hidden.shape[0]
        kt, vt = (jnp.transpose(c, (0, 2, 3, 1)) for c in (k_cache, v_cache))
        part, *caches = attention(0, n_batch, seq_lens, hidden, rope_cos.T, rope_sin.T, ln1_scale, ln1_bias, w_qkv, b_qkv, w_out, kt, vt, None)
        out = moe_layer(hidden, part, b_out, ln2_scale, ln2_bias, w_router.T, expert_ids.T, w_gate, w_up, w_down)
        return out, *(jnp.transpose(c, (0, 3, 1, 2)) for c in caches)

    in_specs = (token_rows, token_vec, token_rows, token_rows, P(), P(), P(None, 'tp'), P('tp'), P('tp', None), P(), cache_spec, cache_spec, P(), P(), P(), token_rows, expert_in, expert_in, expert_down)
    step = jax.shard_map(device_step, mesh=mesh, in_specs=in_specs, out_specs=(token_rows, cache_spec, cache_spec), check_vma=False)
    return step
```

time: 219 us -> 138 us (0.63)
  starting transfers between devices: 27 us -> 0 us
  waiting for transfers between devices: 24.8 us -> 0 us
  local copies, waits for them, and re-layouts: 17.4 us -> 2.26 us
  Pallas kernels: 144 us -> 135 us
  other arithmetic: 4.55 us -> 0 us
    ppermute x35 -> x0, starting transfers between devices: 27 us -> none  [the longest x27 14.5 us: swap_ep(): return lax.ppermute(x, 'ep', [(d, d ^ bit) for d in range(n_ep)])]
    ppermute x35 -> x0, waiting for transfers between devices: 24.8 us -> none  [the longest x27 13 us: swap_ep(): return lax.ppermute(x, 'ep', [(d, d ^ bit) for d in range(n_ep)])]
    unnamed x84 -> x1, local copies, waits for them, and re-layouts: 15 us -> 2.26 us
    pallas_call x4 -> x1, Pallas kernels: 64.5 us -> 59.5 us  [attention(): pl.pallas_call(functools.partial(attention_kernel, chunk * rows, int(prev...]
    convert_element_type x8 -> x0, other arithmetic: 4.55 us -> none  [add_rows(): return (one.astype(F32) + two.astype(F32)).astype(BF)]
    pallas_call x12 -> x1, Pallas kernels: 79.4 us -> 75.7 us  [moe_layer(): pl.pallas_call(moe_kernel, in_specs=[vmem] * 7 + [hbm] * 3, out_specs=vme...]
    slice x4 -> x0, local copies, waits for them, and re-layouts: 2.43 us -> none  [device_step(): a[:, c * rows:(c + 1) * rows]]
  transfers between devices with their start and end apart: 35 -> 0, of which waited for: 7 -> 0; matrix products, arithmetic and copies ran while one was open for 3% -> 0% of each run, Pallas kernels for 35% -> 0%
where the time goes in v4:
time: 138 us
  Pallas kernels  135 us (98%)
  local copies, waits for them, and re-layouts  2.26 us (2%)
    pallas_call x1, Pallas kernels, moe_layer(): pl.pallas_call(moe_kernel, in_specs=[vmem] * 7 + [hbm] * 3, out_specs=vme...  75.7 us
    pallas_call x1, Pallas kernels, attention(): pl.pallas_call(functools.partial(attention_kernel, chunk * rows, int(prev...  59.5 us

profile of v4, /device:TPU:0, one launch (start us, length us, event | category | flops | bytes accessed | tf_op | source)
XLA Modules:
  0.0 138.2 jit_solution(5879069123141834313)
XLA Ops:
  0.6 59.5 %attention.1 = (bf16[512,1024]{1,0:T(8,128)(2,1)}, bf16[512,4,64,128]{3,2,1,0:T(8,128)(2,1)}, bf16[512,4,64,128]{3,2,1,0:T(8,128)(2,1)}) custom-call(s32[512]{0:T(512)} %len_ref.1, bf16[512,1024]{1,0:T(8,128)(2,1)} %hid_ref.3, f32[32,512]{1,0:T(8,128)} %bitcast.10, f32[32,512]{1,0:T(8,128)} %bitcast.11, bf16[1024]{0:T(1024)(128)(2,1)} %s1_ref.1, ...), custom_call_target="tpu_custom_call" | custom-call | flops 10240000000 | bytes 134217728 | tf_op jit(solution)/shard_map/attention/pallas_call | solution.py:193
  60.2 75.7 %moe.1 = bf16[512,1024]{1,0:T(8,128)(2,1)} custom-call(bf16[512,1024]{1,0:T(8,128)(2,1)} %get-tuple-element.6.part_ref, bf16[512,1024]{1,0:T(8,128)(2,1)} %hid_ref.3, bf16[1024]{0:T(1024)(128)(2,1)} %bo_ref.1, bf16[1024]{0:T(1024)(128)(2,1)} %s2_ref.1, bf16[1024]{0:T(1024)(128)(2,1)} %b2_ref.1, bf16[32,1024]{1,0:T(8,128)(2,1)} %bitcast.14, ...), custom_call_target="tpu_custom_call" | custom-call | flops 25999998976 | bytes 14000000 | tf_op jit(solution)/shard_map/moe/pallas_call | solution.py:370
  135.9 2.3 %copy.23 = bf16[512,1024]{1,0:T(8,128)(2,1)} copy(bf16[512,1024]{1,0:T(8,128)(2,1)} %moe.1) | data formatting | bytes 2097152

commit v5 on v4

--- a/solution.py
+++ b/solution.py
@@ -13,6 +13,7 @@
 CHUNKS = 4
 SUB = 128
 BB = 16
+GROUP = 4
 WIDE = 1024 + 128
 SLOTS = 8
 AHEAD = 5
@@ -32,7 +33,7 @@
 
 def attention_kernel(base_row, has_prev, len_ref, hid_ref, cos_ref, sin_ref, s1_ref, b1_ref, bqkv_ref, wqkv_hbm, wout_hbm, k_hbm, v_hbm, *rest):
     part_ref, ko_hbm, vo_hbm = rest[2 * has_prev:2 * has_prev + 3]
-    wqkv_ref, wout_ref, kb_ref, vb_ref, qs_ref, kt_ref, vt_ref, sc_ref, pr_ref, cx_ref, ctx_ref, in_sem, out_sem, w_sem = rest[2 * has_prev + 3:]
+    wqkv_ref, wout_ref, kb_ref, vb_ref, qs_ref, kt_ref, vt_ref, sc_ref, pr_ref, cx_ref, ctx_ref, kc_ref, vc_ref, in_sem, out_sem, w_sem = rest[2 * has_prev + 3:]
     step = pl.program_id(0)
     n_step = pl.num_programs(0)
     per_sub = SUB // BB
@@ -106,31 +107,52 @@
 
     slot = lax.rem(step, SLOTS)
     finish(step, False)
-    shift = lax.rem(SUB - j * BB, SUB)
-    kt = pltpu.roll(kt_ref[...], shift, 1)
-    vt = pltpu.roll(vt_ref[...], shift, 1)
     lane8 = lax.broadcasted_iota(jnp.int32, (8, 128), 1)
     lane256 = lax.broadcasted_iota(jnp.int32, (256, 128), 1)
     row0 = pl.multiple_of(j * BB * 8, BB * 8)
     base = base_row + step * BB
+    pos = [len_ref[base + b] for b in range(BB)]
+    slow = []
+
+    def fetch(source, b):
+        for new, ref in ((kc_ref, kt_ref), (vc_ref, vt_ref)):
+            for r in range(0, 256, 8):
+                new[b, r:r + 8, :] = jnp.take_along_axis(ref[r:r + 8, :], source, axis=1, mode="promise_in_bounds")
+
+    for t in range(0, BB, GROUP):
+        source = jnp.zeros((8, 128), jnp.int32)
+        same = None
+        for m in range(t, t + GROUP):
+            source = jnp.where(lane8 == pos[m], j * BB + m, source)
+            for n in range(t, m):
+                hit = pos[m] == pos[n]
+                same = hit if same is None else same | hit
+        fetch(source, t)
+        slow.append(same)
+
+        @pl.when(same)
+        def _():
+            for m in range(t, t + GROUP):
+                fetch(jnp.full((8, 128), j * BB + m, jnp.int32), m)
 
     def placed(buf, cols, b):
-        pos = len_ref[base + b]
+        t = b // GROUP * GROUP
+        mine = t if b == t else jnp.where(slow[b // GROUP], b, t)
         old = buf[slot, b].reshape(256, 128).astype(F32)
-        new = jnp.where(lane256 == pos, cols[:, b:b + 1], old).astype(BF)
+        new = jnp.where(lane256 == pos[b], cols[mine], old).astype(BF)
         buf[slot, b] = new.reshape(4, 64, 128)
-        return pos, new
+        return new
 
     for b in range(BB):
-        pos, k_new = placed(kb_ref, kt, b)
+        k_new = placed(kb_ref, kc_ref, b)
         q_one = jnp.concatenate([qs_ref[pl.ds(row0 + h * SUB * 8 + b * 8, 8), :] for h in range(2)], axis=1).astype(BF)
         s_one = jnp.dot(q_one, k_new, preferred_element_type=F32) * 0.125
-        sc_ref[b * 8:(b + 1) * 8, :] = jnp.where(lane8 <= pos, s_one, -jnp.inf)
+        sc_ref[b * 8:(b + 1) * 8, :] = jnp.where(lane8 <= pos[b], s_one, -jnp.inf)
     s_all = sc_ref[...]
     e_all = jnp.exp(s_all - jnp.max(s_all, axis=-1, keepdims=True))
     pr_ref[...] = e_all / jnp.sum(e_all, axis=-1, keepdims=True)
     for b in range(BB):
-        _, v_new = placed(vb_ref, vt, b)
+        v_new = placed(vb_ref, vc_ref, b)
         p_one = pr_ref[b * 8:(b + 1) * 8, :].astype(BF)
         c_one = lax.dot_general(p_one, v_new, (((1,), (1,)), ((), ())), preferred_element_type=F32)
         cx_ref[b * 8:(b + 1) * 8, :] = c_one[:, :128]
@@ -201,6 +223,7 @@
                 pltpu.VMEM((2 * SUB * 8, 128), F32), pltpu.VMEM((256, SUB), F32), pltpu.VMEM((256, SUB), F32),
                 pltpu.VMEM((BB * 8, 128), F32), pltpu.VMEM((BB * 8, 128), F32),
                 pltpu.VMEM((2 * BB * 8, 128), F32), pltpu.VMEM((SUB, 512), BF),
+                pltpu.VMEM((BB, 256, 128), F32), pltpu.VMEM((BB, 256, 128), F32),
                 pltpu.SemaphoreType.DMA((2, SLOTS)), pltpu.SemaphoreType.DMA((2, SLOTS)), pltpu.SemaphoreType.DMA((2,))]),
         out_shape=[jax.ShapeDtypeStruct((rows, 1024), BF), jax.ShapeDtypeStruct(kt.shape, BF), jax.ShapeDtypeStruct(vt.shape, BF)],
         input_output_aliases=aliases,

time: 138 us -> 140 us (1.014)
  Pallas kernels: 135 us -> 137 us
where the time goes in v5:
time: 140 us
  Pallas kernels  137 us (98%)
  local copies, waits for them, and re-layouts  2.26 us (2%)
    pallas_call x1, Pallas kernels, moe_layer(): pl.pallas_call(moe_kernel, in_specs=[vmem] * 7 + [hbm] * 3, out_specs=vme...  76 us
    pallas_call x1, Pallas kernels, attention(): pl.pallas_call(functools.partial(attention_kernel, chunk * rows, int(prev...  60.8 us

profile of v5, /device:TPU:0, one launch (start us, length us, event | category | flops | bytes accessed | tf_op | source)
XLA Modules:
  0.0 139.7 jit_solution(12119497492080569963)
XLA Ops:
  0.6 60.8 %attention.1 = (bf16[512,1024]{1,0:T(8,128)(2,1)}, bf16[512,4,64,128]{3,2,1,0:T(8,128)(2,1)}, bf16[512,4,64,128]{3,2,1,0:T(8,128)(2,1)}) custom-call(s32[512]{0:T(512)} %len_ref.1, bf16[512,1024]{1,0:T(8,128)(2,1)} %hid_ref.3, f32[32,512]{1,0:T(8,128)} %bitcast.10, f32[32,512]{1,0:T(8,128)} %bitcast.11, bf16[1024]{0:T(1024)(128)(2,1)} %s1_ref.1, ...), custom_call_target="tpu_custom_call" | custom-call | flops 10240000000 | bytes 134217728 | tf_op jit(solution)/shard_map/attention/pallas_call | solution.py:215
  61.4 76.0 %moe.1 = bf16[512,1024]{1,0:T(8,128)(2,1)} custom-call(bf16[512,1024]{1,0:T(8,128)(2,1)} %get-tuple-element.6.part_ref, bf16[512,1024]{1,0:T(8,128)(2,1)} %hid_ref.3, bf16[1024]{0:T(1024)(128)(2,1)} %bo_ref.1, bf16[1024]{0:T(1024)(128)(2,1)} %s2_ref.1, bf16[1024]{0:T(1024)(128)(2,1)} %b2_ref.1, bf16[32,1024]{1,0:T(8,128)(2,1)} %bitcast.14, ...), custom_call_target="tpu_custom_call" | custom-call | flops 25999998976 | bytes 14000000 | tf_op jit(solution)/shard_map/moe/pallas_call | solution.py:393
  137.4 2.3 %copy.23 = bf16[512,1024]{1,0:T(8,128)(2,1)} copy(bf16[512,1024]{1,0:T(8,128)(2,1)} %moe.1) | data formatting | bytes 2097152

commit v6 on v4

--- a/solution.py
+++ b/solution.py
@@ -11,6 +11,8 @@
 BF = jnp.bfloat16
 F32 = jnp.float32
 CHUNKS = 4
+HEAD = 2
+TAIL = 4
 SUB = 128
 BB = 16
 WIDE = 1024 + 128
@@ -108,7 +110,9 @@
     finish(step, False)
     shift = lax.rem(SUB - j * BB, SUB)
     kt = pltpu.roll(kt_ref[...], shift, 1)
-    vt = pltpu.roll(vt_ref[...], shift, 1)
+    vt = pltpu.roll(vt_ref[...], shift, 1)[:, :BB].astype(BF)
+    unit_row = lax.broadcasted_iota(jnp.int32, (BB, 256), 0)
+    unit_col = lax.broadcasted_iota(jnp.int32, (BB, 256), 1) // 128
     lane8 = lax.broadcasted_iota(jnp.int32, (8, 128), 1)
     lane256 = lax.broadcasted_iota(jnp.int32, (256, 128), 1)
     row0 = pl.multiple_of(j * BB * 8, BB * 8)
@@ -117,12 +121,12 @@
     def placed(buf, cols, b):
         pos = len_ref[base + b]
         old = buf[slot, b].reshape(256, 128).astype(F32)
-        new = jnp.where(lane256 == pos, cols[:, b:b + 1], old).astype(BF)
+        new = jnp.where(lane256 == pos, cols, old).astype(BF)
         buf[slot, b] = new.reshape(4, 64, 128)
         return pos, new
 
     for b in range(BB):
-        pos, k_new = placed(kb_ref, kt, b)
+        pos, k_new = placed(kb_ref, kt[:, b:b + 1], b)
         q_one = jnp.concatenate([qs_ref[pl.ds(row0 + h * SUB * 8 + b * 8, 8), :] for h in range(2)], axis=1).astype(BF)
         s_one = jnp.dot(q_one, k_new, preferred_element_type=F32) * 0.125
         sc_ref[b * 8:(b + 1) * 8, :] = jnp.where(lane8 <= pos, s_one, -jnp.inf)
@@ -130,7 +134,10 @@
     e_all = jnp.exp(s_all - jnp.max(s_all, axis=-1, keepdims=True))
     pr_ref[...] = e_all / jnp.sum(e_all, axis=-1, keepdims=True)
     for b in range(BB):
-        _, v_new = placed(vb_ref, vt, b)
+        if b % 2 == 0:
+            unit = (unit_row == unit_col + b).astype(F32).astype(BF)
+            two = jnp.dot(vt, unit, preferred_element_type=F32)
+        _, v_new = placed(vb_ref, two[:, (b % 2) * 128:(b % 2 + 1) * 128], b)
         p_one = pr_ref[b * 8:(b + 1) * 8, :].astype(BF)
         c_one = lax.dot_general(p_one, v_new, (((1,), (1,)), ((), ())), preferred_element_type=F32)
         cx_ref[b * 8:(b + 1) * 8, :] = c_one[:, :128]
@@ -230,78 +237,104 @@
     rows = xb.shape[2]
     n_e = wg.shape[0]
 
-    def move(kind, c):
-        span = pl.ds(c * rows, rows)
+    split = {0: HEAD, n_c - 1: TAIL}
+
+    def pieces(kind, c):
+        early = kind in (PART, NEAR, FAR, PASS)
+        count = split.get(c, 1) if (c == 0) == early else 1
+        return [(c, p, count) for p in range(count)]
+
+    def move(kind, c, p, count):
+        size = rows // count
+        sub = pl.ds(p * size, size)
+        span = pl.ds(c * rows + p * size, size)
         src, dst, dev = {
             PART: (part_ref.at[span], other.at[span], {"tp": peer}),
-            NEAR: (xb.at[0, c], xb.at[1, c], {"ep": near}),
-            FAR: (xb.at[0, c], xb.at[2, c], {"ep": far}),
-            PASS: (xb.at[2, c], xb.at[3, c], {"ep": near}),
-            BACK1: (ob.at[1, c], rb.at[0, c], {"ep": near}),
-            BACK3: (ob.at[3, c], rb.at[1, c], {"ep": near}),
-            BACKX: (fb.at[c], rf.at[c], {"ep": far}),
-            BACKY: (tb.at[c], ry.at[c], {"tp": peer}),
+            NEAR: (xb.at[0, c, sub], xb.at[1, c, sub], {"ep": near}),
+            FAR: (xb.at[0, c, sub], xb.at[2, c, sub], {"ep": far}),
+            PASS: (xb.at[2, c, sub], xb.at[3, c, sub], {"ep": near}),
+            BACK1: (ob.at[1, c, sub], rb.at[0, c, sub], {"ep": near}),
+            BACK3: (ob.at[3, c, sub], rb.at[1, c, sub], {"ep": near}),
+            BACKX: (fb.at[c, sub], rf.at[c, sub], {"ep": far}),
+            BACKY: (tb.at[c, sub], ry.at[c, sub], {"tp": peer}),
         }[kind]
-        return pltpu.make_async_remote_copy(src_ref=src, dst_ref=dst, send_sem=send.at[kind, c], recv_sem=recv.at[kind, c], device_id=dev, device_id_type=pl.DeviceIdType.MESH)
-
-    def go(kind, c):
-        move(kind, c).start()
-
-    def arrive(kind, c):
-        move(kind, c).wait_recv()
+        lane = p * n_c + c
+        return pltpu.make_async_remote_copy(src_ref=src, dst_ref=dst, send_sem=send.at[kind, lane], recv_sem=recv.at[kind, lane], device_id=dev, device_id_type=pl.DeviceIdType.MESH)
+
+    def go(kind, *at):
+        move(kind, *at).start()
+
+    def arrive(kind, *at):
+        move(kind, *at).wait_recv()
+
+    def rows_of(c, p, count):
+        size = rows // count
+        return slice(p * size, (p + 1) * size), slice(c * rows + p * size, c * rows + (p + 1) * size)
 
     def mid(c):
-        arrive(PART, c)
-        span = slice(c * rows, (c + 1) * rows)
-        attn = part_ref[span, :].astype(F32) + other[span, :].astype(F32)
-        row = (hid_ref[span, :].astype(F32) + attn + wide(bo_ref)).astype(BF)
-        x1[span, :] = row
-        h2 = norm_rows(row.astype(F32), wide(s2_ref), wide(b2_ref))
-        xb[0, c, :, :1024] = h2
-        logit = lax.dot_general(wr_ref[...], h2, (((1,), (1,)), ((), ())), preferred_element_type=F32)
-        eid = lax.broadcasted_iota(jnp.int32, (32, rows), 0)
-        picked = eid == ids_ref[0:1, span]
-        for m in range(1, 8):
-            picked = picked | (eid == ids_ref[m:m + 1, span])
-        logit = jnp.where(picked, logit, -jnp.inf)
-        ex = jnp.exp(logit - jnp.max(logit, axis=0, keepdims=True))
-        prob = ex / jnp.sum(ex, axis=0, keepdims=True)
-        full = jnp.concatenate([prob, jnp.zeros((96, rows), F32)], axis=0)
-        xb[0, c, :, 1024:] = jnp.transpose(full).astype(BF)
-        go(FAR, c)
-        go(NEAR, c)
+        for at in pieces(FAR, c):
+            arrive(PART, *at)
+            sub, span = rows_of(*at)
+            attn = part_ref[span, :].astype(F32) + other[span, :].astype(F32)
+            row = (hid_ref[span, :].astype(F32) + attn + wide(bo_ref)).astype(BF)
+            x1[span, :] = row
+            h2 = norm_rows(row.astype(F32), wide(s2_ref), wide(b2_ref))
+            xb[0, c, sub, :1024] = h2
+            size = h2.shape[0]
+            logit = lax.dot_general(wr_ref[...], h2, (((1,), (1,)), ((), ())), preferred_element_type=F32)
+            eid = lax.broadcasted_iota(jnp.int32, (32, size), 0)
+            picked = eid == ids_ref[0:1, span]
+            for m in range(1, 8):
+                picked = picked | (eid == ids_ref[m:m + 1, span])
+            logit = jnp.where(picked, logit, -jnp.inf)
+            ex = jnp.exp(logit - jnp.max(logit, axis=0, keepdims=True))
+            prob = ex / jnp.sum(ex, axis=0, keepdims=True)
+            full = jnp.concatenate([prob, jnp.zeros((96, size), F32)], axis=0)
+            xb[0, c, sub, 1024:] = jnp.transpose(full).astype(BF)
+            go(FAR, *at)
+            go(NEAR, *at)
 
     def hand_on(c):
-        arrive(FAR, c)
-        go(PASS, c)
+        for at in pieces(PASS, c):
+            arrive(FAR, *at)
+            go(PASS, *at)
 
     def ready(c):
-        arrive(NEAR, c)
-        arrive(PASS, c)
+        for at in pieces(NEAR, c):
+            arrive(NEAR, *at)
+            arrive(PASS, *at)
 
     def give_back(c):
-        go(BACK3, c)
-        go(BACK1, c)
+        for at in pieces(BACK3, c):
+            go(BACK3, *at)
+        for at in pieces(BACK1, c):
+            go(BACK1, *at)
 
     def far_sum(c):
-        arrive(BACK3, c)
-        fb[c] = (ob[2, c].astype(F32) + rb[1, c].astype(F32)).astype(BF)
-        go(BACKX, c)
+        for at in pieces(BACKX, c):
+            arrive(BACK3, *at)
+            sub, _ = rows_of(*at)
+            fb[c, sub, :] = (ob[2, c, sub, :].astype(F32) + rb[1, c, sub, :].astype(F32)).astype(BF)
+            go(BACKX, *at)
 
     def all_sum(c):
-        arrive(BACK1, c)
-        arrive(BACKX, c)
-        tb[c] = (ob[0, c].astype(F32) + rb[0, c].astype(F32) + rf[c].astype(F32)).astype(BF)
-        go(BACKY, c)
+        for at in pieces(BACKY, c):
+            arrive(BACK1, *at)
+            arrive(BACKX, *at)
+            sub, _ = rows_of(*at)
+            tb[c, sub, :] = (ob[0, c, sub, :].astype(F32) + rb[0, c, sub, :].astype(F32) + rf[c, sub, :].astype(F32)).astype(BF)
+            go(BACKY, *at)
 
     def last_sum(c):
-        arrive(BACKY, c)
-        span = slice(c * rows, (c + 1) * rows)
-        moe = tb[c].astype(F32) + ry[c].astype(F32)
-        out_ref[span, :] = (x1[span, :].astype(F32) + moe).astype(BF)
+        for at in pieces(BACKY, c):
+            arrive(BACKY, *at)
+            sub, span = rows_of(*at)
+            moe = tb[c, sub, :].astype(F32) + ry[c, sub, :].astype(F32)
+            out_ref[span, :] = (x1[span, :].astype(F32) + moe).astype(BF)
 
     for c in range(n_c):
-        go(PART, c)
+        for at in pieces(PART, c):
+            go(PART, *at)
     mid(0)
     mid(1)
     hand_on(0)
@@ -358,7 +391,8 @@
     last_sum(3)
     for kind in range(8):
         for c in range(n_c):
-            move(kind, c).wait_send()
+            for at in pieces(kind, c):
+                move(kind, *at).wait_send()
 
 
 def moe_layer(hidden, part, b_out, s2, b2, wr_t, ids, wg, wu, wd):
@@ -375,7 +409,7 @@
             pltpu.VMEM((n_batch, 1024), BF), pltpu.VMEM((n_batch, 1024), BF), pltpu.VMEM((4, CHUNKS, rows, WIDE), BF),
             pltpu.VMEM(wg.shape, BF), pltpu.VMEM(wu.shape, BF), pltpu.VMEM(wd.shape, BF),
             pltpu.VMEM((4 * rows, 1024), F32), blocks(4), blocks(2), blocks(), blocks(), blocks(), blocks(),
-            pltpu.SemaphoreType.DMA((3,)), pltpu.SemaphoreType.DMA((8, CHUNKS)), pltpu.SemaphoreType.DMA((8, CHUNKS))],
+            pltpu.SemaphoreType.DMA((3,)), pltpu.SemaphoreType.DMA((8, 4 * CHUNKS)), pltpu.SemaphoreType.DMA((8, 4 * CHUNKS))],
         compiler_params=pltpu.CompilerParams(collective_id=0, has_side_effects=True, vmem_limit_bytes=VMEM_LIMIT),
         cost_estimate=pl.CostEstimate(flops=26_000_000_000, bytes_accessed=14_000_000, transcendentals=0),
         name="moe",

time: 138 us -> 134 us (0.971)
  Pallas kernels: 135 us -> 131 us
    pallas_call x1, Pallas kernels: 59.5 us -> 53.9 us  [attention(): pl.pallas_call(functools.partial(attention_kernel, chunk * rows, int(prev...]
where the time goes in v6:
time: 134 us
  Pallas kernels  131 us (98%)
  local copies, waits for them, and re-layouts  2.26 us (2%)
    pallas_call x1, Pallas kernels, moe_layer(): pl.pallas_call(moe_kernel, in_specs=[vmem] * 7 + [hbm] * 3, out_specs=vme...  76.8 us
    pallas_call x1, Pallas kernels, attention(): pl.pallas_call(functools.partial(attention_kernel, chunk * rows, int(prev...  53.9 us

profile of v6, /device:TPU:0, one launch (start us, length us, event | category | flops | bytes accessed | tf_op | source)
XLA Modules:
  0.0 133.6 jit_solution(11391161420526908393)
XLA Ops:
  0.6 53.9 %attention.1 = (bf16[512,1024]{1,0:T(8,128)(2,1)}, bf16[512,4,64,128]{3,2,1,0:T(8,128)(2,1)}, bf16[512,4,64,128]{3,2,1,0:T(8,128)(2,1)}) custom-call(s32[512]{0:T(512)} %len_ref.1, bf16[512,1024]{1,0:T(8,128)(2,1)} %hid_ref.3, f32[32,512]{1,0:T(8,128)} %bitcast.10, f32[32,512]{1,0:T(8,128)} %bitcast.11, bf16[1024]{0:T(1024)(128)(2,1)} %s1_ref.1, ...), custom_call_target="tpu_custom_call" | custom-call | flops 10240000000 | bytes 134217728 | tf_op jit(solution)/shard_map/attention/pallas_call | solution.py:200
  54.5 76.8 %moe.1 = bf16[512,1024]{1,0:T(8,128)(2,1)} custom-call(bf16[512,1024]{1,0:T(8,128)(2,1)} %get-tuple-element.6.part_ref, bf16[512,1024]{1,0:T(8,128)(2,1)} %hid_ref.3, bf16[1024]{0:T(1024)(128)(2,1)} %bo_ref.1, bf16[1024]{0:T(1024)(128)(2,1)} %s2_ref.1, bf16[1024]{0:T(1024)(128)(2,1)} %b2_ref.1, bf16[32,1024]{1,0:T(8,128)(2,1)} %bitcast.14, ...), custom_call_target="tpu_custom_call" | custom-call | flops 25999998976 | bytes 14000000 | tf_op jit(solution)/shard_map/moe/pallas_call | solution.py:404
  131.3 2.3 %copy.23 = bf16[512,1024]{1,0:T(8,128)(2,1)} copy(bf16[512,1024]{1,0:T(8,128)(2,1)} %moe.1) | data formatting | bytes 2097152

commit v7 on v6

--- a/solution.py
+++ b/solution.py
@@ -347,7 +347,8 @@
         12: [(give_back, 2), (ready, 3)], 13: [(all_sum, 0)], 14: [(far_sum, 2)],
     }
     parts = 4
-    lane = lax.broadcasted_iota(jnp.int32, (4 * rows, 128), 1)
+    unit_row = lax.broadcasted_iota(jnp.int32, (128, 128 * n_e // parts), 0)
+    unit_col = lax.broadcasted_iota(jnp.int32, (128, 128 * n_e // parts), 1) // 128
 
     def step(s, carry):
         for k, acts in table.items():
@@ -362,16 +363,16 @@
             acc[...] = jnp.zeros_like(acc)
 
         x = jnp.concatenate([xb[n, c, :, :1024] for n in range(4)], axis=0)
-        gates = jnp.concatenate([xb[n, c, :, 1024:] for n in range(4)], axis=0).astype(F32)
-        total = None
+        gates = jnp.concatenate([xb[n, c, :, 1024:] for n in range(4)], axis=0)
+        unit = (unit_row == me_ep * n_e + q * (n_e // parts) + unit_col).astype(F32).astype(BF)
+        wide_gates = jnp.dot(gates, unit, preferred_element_type=F32)
         for m in range(n_e // parts):
             e = q * (n_e // parts) + m
             gate = jnp.dot(x, wg[e], preferred_element_type=F32)
             up = jnp.dot(x, wu[e], preferred_element_type=F32)
             act = (gate * jax.nn.sigmoid(gate) * up).astype(BF)
             y = jnp.dot(act, wd[e], preferred_element_type=F32)
-            g_one = jnp.sum(jnp.where(lane == me_ep * n_e + e, gates, 0.0), axis=-1, keepdims=True)
-            acc[...] += g_one * y
+            acc[...] += jnp.concatenate([wide_gates[:, m * 128:(m + 1) * 128]] * 8, axis=1) * y
 
         @pl.when(q == parts - 1)
         def _():

time: 134 us -> 134 us (level)
  no operation moved by 1% of the time
where the time goes in v7:
time: 134 us
  Pallas kernels  131 us (98%)
  local copies, waits for them, and re-layouts  2.26 us (2%)
    pallas_call x1, Pallas kernels, moe_layer(): pl.pallas_call(moe_kernel, in_specs=[vmem] * 7 + [hbm] * 3, out_specs=vme...  77.4 us
    pallas_call x1, Pallas kernels, attention(): pl.pallas_call(functools.partial(attention_kernel, chunk * rows, int(prev...  53.9 us

profile of v7, /device:TPU:0, one launch (start us, length us, event | category | flops | bytes accessed | tf_op | source)
XLA Modules:
  0.0 134.2 jit_solution(8420533580434756381)
XLA Ops:
  0.6 53.9 %attention.1 = (bf16[512,1024]{1,0:T(8,128)(2,1)}, bf16[512,4,64,128]{3,2,1,0:T(8,128)(2,1)}, bf16[512,4,64,128]{3,2,1,0:T(8,128)(2,1)}) custom-call(s32[512]{0:T(512)} %len_ref.1, bf16[512,1024]{1,0:T(8,128)(2,1)} %hid_ref.3, f32[32,512]{1,0:T(8,128)} %bitcast.10, f32[32,512]{1,0:T(8,128)} %bitcast.11, bf16[1024]{0:T(1024)(128)(2,1)} %s1_ref.1, ...), custom_call_target="tpu_custom_call" | custom-call | flops 10240000000 | bytes 134217728 | tf_op jit(solution)/shard_map/attention/pallas_call | solution.py:200
  54.5 77.4 %moe.1 = bf16[512,1024]{1,0:T(8,128)(2,1)} custom-call(bf16[512,1024]{1,0:T(8,128)(2,1)} %get-tuple-element.6.part_ref, bf16[512,1024]{1,0:T(8,128)(2,1)} %hid_ref.3, bf16[1024]{0:T(1024)(128)(2,1)} %bo_ref.1, bf16[1024]{0:T(1024)(128)(2,1)} %s2_ref.1, bf16[1024]{0:T(1024)(128)(2,1)} %b2_ref.1, bf16[32,1024]{1,0:T(8,128)(2,1)} %bitcast.14, ...), custom_call_target="tpu_custom_call" | custom-call | flops 25999998976 | bytes 14000000 | tf_op jit(solution)/shard_map/moe/pallas_call | solution.py:405
  131.9 2.3 %copy.23 = bf16[512,1024]{1,0:T(8,128)(2,1)} copy(bf16[512,1024]{1,0:T(8,128)(2,1)} %moe.1) | data formatting | bytes 2097152

commit v8 on v7

--- a/solution.py
+++ b/solution.py
@@ -161,6 +161,7 @@
         @pl.when(step + AHEAD >= SLOTS)
         def _():
             finish(step + AHEAD - SLOTS, True)
+
         begin(step + AHEAD, False)
 
     @pl.when(step == per_sub - 1)
@@ -220,7 +221,7 @@
 PART, NEAR, FAR, PASS, BACK1, BACK3, BACKX, BACKY = range(8)
 
 
-def moe_kernel(part_ref, hid_ref, bo_ref, s2_ref, b2_ref, wr_ref, ids_ref, wg_hbm, wu_hbm, wd_hbm, out_ref,
+def moe_kernel(early_ref, early_other, part_ref, hid_ref, bo_ref, s2_ref, b2_ref, wr_ref, ids_ref, wg_hbm, wu_hbm, wd_hbm, out_ref,
                other, x1, xb, wg, wu, wd, acc, ob, rb, fb, rf, tb, ry, w_sem, send, recv):
     me_ep, me_tp = lax.axis_index("ep"), lax.axis_index("tp")
     near = me_ep + 1 - 2 * lax.rem(me_ep, 2)
@@ -239,7 +240,11 @@
 
     split = {0: HEAD, n_c - 1: TAIL}
 
+    first_late = n_c - part_ref.shape[0] // rows
+
     def pieces(kind, c):
+        if kind == PART and c < first_late:
+            return []
         early = kind in (PART, NEAR, FAR, PASS)
         count = split.get(c, 1) if (c == 0) == early else 1
         return [(c, p, count) for p in range(count)]
@@ -247,9 +252,9 @@
     def move(kind, c, p, count):
         size = rows // count
         sub = pl.ds(p * size, size)
-        span = pl.ds(c * rows + p * size, size)
+        late = pl.ds(max(c - first_late, 0) * rows + p * size, size)
         src, dst, dev = {
-            PART: (part_ref.at[span], other.at[span], {"tp": peer}),
+            PART: (part_ref.at[late], other.at[late], {"tp": peer}),
             NEAR: (xb.at[0, c, sub], xb.at[1, c, sub], {"ep": near}),
             FAR: (xb.at[0, c, sub], xb.at[2, c, sub], {"ep": far}),
             PASS: (xb.at[2, c, sub], xb.at[3, c, sub], {"ep": near}),
@@ -273,9 +278,13 @@
 
     def mid(c):
         for at in pieces(FAR, c):
-            arrive(PART, *at)
             sub, span = rows_of(*at)
-            attn = part_ref[span, :].astype(F32) + other[span, :].astype(F32)
+            if c < first_late:
+                attn = early_ref[span, :].astype(F32) + early_other[span, :].astype(F32)
+            else:
+                arrive(PART, *at)
+                _, late = rows_of(c - first_late, *at[1:])
+                attn = part_ref[late, :].astype(F32) + other[late, :].astype(F32)
             row = (hid_ref[span, :].astype(F32) + attn + wide(bo_ref)).astype(BF)
             x1[span, :] = row
             h2 = norm_rows(row.astype(F32), wide(s2_ref), wide(b2_ref))
@@ -337,14 +346,15 @@
             go(PART, *at)
     mid(0)
     mid(1)
+    mid(2)
     hand_on(0)
     for one in loads:
         one.wait()
     table = {
-        0: [(ready, 0)], 1: [(mid, 2)], 3: [(hand_on, 1)],
-        4: [(give_back, 0), (ready, 1)], 5: [(mid, 3)], 6: [(far_sum, 0)], 7: [(hand_on, 2)],
-        8: [(give_back, 1), (ready, 2)], 10: [(far_sum, 1)], 11: [(hand_on, 3)],
-        12: [(give_back, 2), (ready, 3)], 13: [(all_sum, 0)], 14: [(far_sum, 2)],
+        0: [(ready, 0)], 2: [(mid, 3)], 3: [(hand_on, 1)],
+        4: [(give_back, 0), (ready, 1)], 5: [(far_sum, 0)], 6: [(hand_on, 2)],
+        8: [(give_back, 1), (ready, 2)], 9: [(hand_on, 3), (far_sum, 1)], 11: [(all_sum, 0)],
+        12: [(give_back, 2), (ready, 3)], 13: [(far_sum, 2)], 15: [(all_sum, 1)],
     }
     parts = 4
     unit_row = lax.broadcasted_iota(jnp.int32, (128, 128 * n_e // parts), 0)
@@ -378,11 +388,11 @@
         def _():
             for n in range(4):
                 ob[n, c] = acc[n * rows:(n + 1) * rows, :].astype(BF)
+
         return carry
 
     lax.fori_loop(0, n_c * parts, step, 0)
     give_back(3)
-    all_sum(1)
     far_sum(3)
     all_sum(2)
     last_sum(0)
@@ -396,7 +406,7 @@
                 move(kind, *at).wait_send()
 
 
-def moe_layer(hidden, part, b_out, s2, b2, wr_t, ids, wg, wu, wd):
+def moe_layer(hidden, early, early_other, part, b_out, s2, b2, wr_t, ids, wg, wu, wd):
     n_batch = hidden.shape[0]
     rows = n_batch // CHUNKS
     vmem = pl.BlockSpec(memory_space=pltpu.VMEM)
@@ -404,17 +414,17 @@
     blocks = lambda *lead: pltpu.VMEM(lead + (CHUNKS, rows, 1024), BF)
     return pl.pallas_call(
         moe_kernel,
-        in_specs=[vmem] * 7 + [hbm] * 3, out_specs=vmem,
+        in_specs=[vmem] * 9 + [hbm] * 3, out_specs=vmem,
         out_shape=jax.ShapeDtypeStruct((n_batch, 1024), BF),
         scratch_shapes=[
-            pltpu.VMEM((n_batch, 1024), BF), pltpu.VMEM((n_batch, 1024), BF), pltpu.VMEM((4, CHUNKS, rows, WIDE), BF),
+            pltpu.VMEM(part.shape, BF), pltpu.VMEM((n_batch, 1024), BF), pltpu.VMEM((4, CHUNKS, rows, WIDE), BF),
             pltpu.VMEM(wg.shape, BF), pltpu.VMEM(wu.shape, BF), pltpu.VMEM(wd.shape, BF),
             pltpu.VMEM((4 * rows, 1024), F32), blocks(4), blocks(2), blocks(), blocks(), blocks(), blocks(),
             pltpu.SemaphoreType.DMA((3,)), pltpu.SemaphoreType.DMA((8, 4 * CHUNKS)), pltpu.SemaphoreType.DMA((8, 4 * CHUNKS))],
         compiler_params=pltpu.CompilerParams(collective_id=0, has_side_effects=True, vmem_limit_bytes=VMEM_LIMIT),
         cost_estimate=pl.CostEstimate(flops=26_000_000_000, bytes_accessed=14_000_000, transcendentals=0),
         name="moe",
-    )(part, hidden, b_out, s2, b2, wr_t, ids, wg, wu, wd)
+    )(early, early_other, part, hidden, b_out, s2, b2, wr_t, ids, wg, wu, wd)
 
 
 def solution(mesh):
@@ -427,10 +437,15 @@
     def device_step(hidden, seq_lens, rope_cos, rope_sin, ln1_scale, ln1_bias, w_qkv, b_qkv, w_out, b_out, k_cache, v_cache, ln2_scale, ln2_bias, w_router, expert_ids, w_gate, w_up, w_down):
         n_batch = hidden.shape[0]
         kt, vt = (jnp.transpose(c, (0, 2, 3, 1)) for c in (k_cache, v_cache))
-        part, *caches = attention(0, n_batch, seq_lens, hidden, rope_cos.T, rope_sin.T, ln1_scale, ln1_bias, w_qkv, b_qkv, w_out, kt, vt, None)
-        out = moe_layer(hidden, part, b_out, ln2_scale, ln2_bias, w_router.T, expert_ids.T, w_gate, w_up, w_down)
+        half = n_batch // 2
+        caches, parts = None, []
+        for c in range(2):
+            part, *caches = attention(c, half, seq_lens, hidden, rope_cos.T, rope_sin.T, ln1_scale, ln1_bias, w_qkv, b_qkv, w_out, kt, vt, caches)
+            parts.append(part)
+            if c == 0:
+                other = lax.ppermute(part, 'tp', [(0, 1), (1, 0)])
+        out = moe_layer(hidden, parts[0], other, parts[1], b_out, ln2_scale, ln2_bias, w_router.T, expert_ids.T, w_gate, w_up, w_down)
         return out, *(jnp.transpose(c, (0, 3, 1, 2)) for c in caches)
 
     in_specs = (token_rows, token_vec, token_rows, token_rows, P(), P(), P(None, 'tp'), P('tp'), P('tp', None), P(), cache_spec, cache_spec, P(), P(), P(), token_rows, expert_in, expert_in, expert_down)
-    step = jax.shard_map(device_step, mesh=mesh, in_specs=in_specs, out_specs=(token_rows, cache_spec, cache_spec), check_vma=False)
-    return step
+    return jax.shard_map(device_step, mesh=mesh, in_specs=in_specs, out_specs=(token_rows, cache_spec, cache_spec), check_vma=False)

time: 134 us -> 135 us (level)
  starting transfers between devices: 0 us -> 3.36 us
  Pallas kernels: 131 us -> 128 us
    pallas_call x1, Pallas kernels: 77.4 us -> 66.9 us  [moe_layer(): pl.pallas_call(moe_kernel, in_specs=[vmem] * 9 + [hbm] * 3, out_specs=vme...]
    pallas_call x1 -> x2, Pallas kernels: 53.9 us -> 60.7 us  [attention(): pl.pallas_call(functools.partial(attention_kernel, chunk * rows, int(prev...]
    ppermute x0 -> x1, starting transfers between devices: none -> 3.36 us  [device_step(): other = lax.ppermute(part, 'tp', [(0, 1), (1, 0)])]
    unnamed x1 -> x3, local copies, waits for them, and re-layouts: 2.26 us -> 3.06 us
  transfers between devices with their start and end apart: 0 -> 1, of which waited for: 0 -> 0; matrix products, arithmetic and copies ran while one was open for 0% -> 0% of each run, Pallas kernels for 0% -> 23%
where the time goes in v8:
time: 135 us
  Pallas kernels  128 us (95%)
  starting transfers between devices  3.36 us (2%)
  local copies, waits for them, and re-layouts  3.06 us (2%)
    pallas_call x1, Pallas kernels, moe_layer(): pl.pallas_call(moe_kernel, in_specs=[vmem] * 9 + [hbm] * 3, out_specs=vme...  66.9 us
    pallas_call x2, Pallas kernels, attention(): pl.pallas_call(functools.partial(attention_kernel, chunk * rows, int(prev...  60.7 us
    ppermute x1, starting transfers between devices, device_step(): other = lax.ppermute(part, 'tp', [(0, 1), (1, 0)])  3.36 us
    unnamed x3, local copies, waits for them, and re-layouts  3.06 us
  transfers between devices with their start and end apart: 1, of which 0 were waited for; matrix products, arithmetic and copies ran while one was open for 0% of the time, Pallas kernels for 23%

profile of v8, /device:TPU:0, one launch (start us, length us, event | category | flops | bytes accessed | tf_op | source)
XLA Modules:
  0.0 134.7 jit_solution(15249135709978511824)
XLA Ops:
  0.6 30.0 %attention.2 = (bf16[256,1024]{1,0:T(8,128)(2,1)}, bf16[512,4,64,128]{3,2,1,0:T(8,128)(2,1)}, bf16[512,4,64,128]{3,2,1,0:T(8,128)(2,1)}) custom-call(s32[512]{0:T(512)} %len_ref.3, bf16[512,1024]{1,0:T(8,128)(2,1)} %hid_ref.5, f32[32,512]{1,0:T(8,128)} %bitcast.14, f32[32,512]{1,0:T(8,128)} %bitcast.16, bf16[1024]{0:T(1024)(128)(2,1)} %s1_ref.3, ...), custom_call_target="tpu_custom_call" | custom-call | flops 5120000000 | bytes 67108864 | tf_op jit(solution)/shard_map/attention/pallas_call | solution.py:201
  30.7 3.4 %collective-permute-start = (bf16[256,1024]{1,0:T(8,128)(2,1)}, bf16[256,1024]{1,0:T(8,128)(2,1)S(1)}, u32[]{:S(2)}, u32[]{:S(2)}) collective-permute-start(bf16[256,1024]{1,0:T(8,128)(2,1)} %get-tuple-element.9.early_ref), channel_id=1, source_target_pairs={{0,4},{4,0},{1,5},{5,1},{2,6},{6,2},{3,7},{7,3}} | collective-permute-start | bytes 1572872 | tf_op jit(solution)/shard_map/ppermute | solution.py:446
  34.0 30.6 %attention.3 = (bf16[256,1024]{1,0:T(8,128)(2,1)}, bf16[512,4,64,128]{3,2,1,0:T(8,128)(2,1)}, bf16[512,4,64,128]{3,2,1,0:T(8,128)(2,1)}) custom-call(s32[512]{0:T(512)} %len_ref.3, bf16[512,1024]{1,0:T(8,128)(2,1)} %hid_ref.5, f32[32,512]{1,0:T(8,128)} %bitcast.15, f32[32,512]{1,0:T(8,128)} %bitcast.17, ...), custom_call_target="tpu_custom_call", output_to_operand_aliasing={{1}: (11, {}), {2}: (12, {})} | custom-call | flops 5120000000 | bytes 67108864 | tf_op jit(solution)/shard_map/attention/pallas_call | solution.py:201
  64.7 0.0 collective-permute-done.early_other
  64.7 0.0 copy-start
  64.7 0.8 copy-done
  65.5 66.9 %moe.1 = bf16[512,1024]{1,0:T(8,128)(2,1)} custom-call(bf16[256,1024]{1,0:T(8,128)(2,1)} %get-tuple-element.9.early_ref, bf16[256,1024]{1,0:T(8,128)(2,1)} %copy-done, bf16[256,1024]{1,0:T(8,128)(2,1)} %get-tuple-element.12.part_ref, bf16[512,1024]{1,0:T(8,128)(2,1)} %hid_ref.5, bf16[1024]{0:T(1024)(128)(2,1)} %bo_ref.1, bf16[1024]{0:T(1024)(128)(2,1)} %s2_ref.1, ...), custom_call_target="tpu_custom_call" | custom-call | flops 25999998976 | bytes 14000000 | tf_op jit(solution)/shard_map/moe/pallas_call | solution.py:415
  132.4 2.3 %copy.27 = bf16[512,1024]{1,0:T(8,128)(2,1)} copy(bf16[512,1024]{1,0:T(8,128)(2,1)} %moe.1) | data formatting | bytes 2097152
Async XLA Ops:
  30.7 34.0 %collective-permute-start = (bf16[256,1024]{1,0:T(8,128)(2,1)}, bf16[256,1024]{1,0:T(8,128)(2,1)S(1)}, u32[]{:S(2)}, u32[]{:S(2)}) collective-permute-start(bf16[256,1024]{1,0:T(8,128)(2,1)} %get-tuple-element.9.early_ref), channel_id=1, source_target_pairs={{0,4},{4,0},{1,5},{5,1},{2,6},{6,2},{3,7},{7,3}} | collective-permute-start | bytes 1572872 | tf_op jit(solution)/shard_map/ppermute | solution.py:446
  64.7 0.8 copy-start

commit v9 on v7

--- a/solution.py
+++ b/solution.py
@@ -14,10 +14,10 @@
 HEAD = 2
 TAIL = 4
 SUB = 128
-BB = 16
+BB = 32
 WIDE = 1024 + 128
-SLOTS = 8
-AHEAD = 5
+SLOTS = 5
+AHEAD = 3
 VMEM_LIMIT = 60 * 1024 * 1024
 
 

time: 134 us -> 136 us (1.015)
  Pallas kernels: 131 us -> 133 us
where the time goes in v9:
time: 136 us
  Pallas kernels  133 us (98%)
  local copies, waits for them, and re-layouts  2.26 us (2%)
    pallas_call x1, Pallas kernels, moe_layer(): pl.pallas_call(moe_kernel, in_specs=[vmem] * 7 + [hbm] * 3, out_specs=vme...  77.4 us
    pallas_call x1, Pallas kernels, attention(): pl.pallas_call(functools.partial(attention_kernel, chunk * rows, int(prev...  55.2 us

profile of v9, /device:TPU:0, one launch (start us, length us, event | category | flops | bytes accessed | tf_op | source)
XLA Modules:
  0.0 135.5 jit_solution(9021366486224829176)
XLA Ops:
  0.6 55.2 %attention.1 = (bf16[512,1024]{1,0:T(8,128)(2,1)}, bf16[512,4,64,128]{3,2,1,0:T(8,128)(2,1)}, bf16[512,4,64,128]{3,2,1,0:T(8,128)(2,1)}) custom-call(s32[512]{0:T(512)} %len_ref.1, bf16[512,1024]{1,0:T(8,128)(2,1)} %hid_ref.3, f32[32,512]{1,0:T(8,128)} %bitcast.10, f32[32,512]{1,0:T(8,128)} %bitcast.11, bf16[1024]{0:T(1024)(128)(2,1)} %s1_ref.1, ...), custom_call_target="tpu_custom_call" | custom-call | flops 10240000000 | bytes 134217728 | tf_op jit(solution)/shard_map/attention/pallas_call | solution.py:200
  55.9 77.4 %moe.1 = bf16[512,1024]{1,0:T(8,128)(2,1)} custom-call(bf16[512,1024]{1,0:T(8,128)(2,1)} %get-tuple-element.6.part_ref, bf16[512,1024]{1,0:T(8,128)(2,1)} %hid_ref.3, bf16[1024]{0:T(1024)(128)(2,1)} %bo_ref.1, bf16[1024]{0:T(1024)(128)(2,1)} %s2_ref.1, bf16[1024]{0:T(1024)(128)(2,1)} %b2_ref.1, bf16[32,1024]{1,0:T(8,128)(2,1)} %bitcast.14, ...), custom_call_target="tpu_custom_call" | custom-call | flops 25999998976 | bytes 14000000 | tf_op jit(solution)/shard_map/moe/pallas_call | solution.py:405
  133.2 2.3 %copy.23 = bf16[512,1024]{1,0:T(8,128)(2,1)} copy(bf16[512,1024]{1,0:T(8,128)(2,1)} %moe.1) | data formatting | bytes 2097152
